TPU v7x, 32 devices: a whole 2x2x4 slice. The times are simulated.
32 devices in a mesh: group: 16 (over z, y, core), shard: 2 (over x).
Axes of the slice: x: 2, y: 2, z: 4, core: 2. Of those that a mesh axis runs over, the one named last changes fastest.
Arguments:
- tokens: float32 [16384, 1024], P(('group', 'shard')), may hold values from -6 to 6
- cotangent: float32 [16384, 1024], P(('group', 'shard')), may hold values from -6 to 6
- lengths: int32 [16], replicated, may hold values from 512 to 1024, as said below
- qkv_weight: float32 [1024, 3072], P('shard'), may hold values from -0.1875 to 0.1875
- qkv_momentum: float32 [1024, 3072], P('shard')
- qkv_average: float32 [1024, 3072], P('shard'), may hold values from -0.1875 to 0.1875
- out_weight: float32 [1024, 1024], P('shard'), may hold values from -0.5 to 0.5
- out_momentum: float32 [1024, 1024], P('shard')
- out_average: float32 [1024, 1024], P('shard'), may hold values from -0.5 to 0.5
- up_weight: float32 [1024, 4096], P(None, 'shard'), may hold values from -0.1875 to 0.1875
- up_momentum: float32 [1024, 4096], P(None, 'shard')
- up_average: float32 [1024, 4096], P(None, 'shard'), may hold values from -0.1875 to 0.1875
- down_weight: float32 [4096, 1024], P('shard'), may hold values from -0.09375 to 0.09375
- down_momentum: float32 [4096, 1024], P('shard')
- down_average: float32 [4096, 1024], P('shard'), may hold values from -0.09375 to 0.09375
- small_params: float32 [12, 1024], P(None, 'shard')
- small_momentum: float32 [12, 1024], P(None, 'shard')
- small_average: float32 [12, 1024], P(None, 'shard')
Outputs:
- block_out: float32 [16384, 1024], P(('group', 'shard'))
- input_grad: float32 [16384, 1024], P(('group', 'shard'))
- qkv_weight_new: float32 [1024, 3072], P('shard')
- qkv_momentum_new: float32 [1024, 3072], P('shard')
- qkv_average_new: float32 [1024, 3072], P('shard')
- out_weight_new: float32 [1024, 1024], P('shard')
- out_momentum_new: float32 [1024, 1024], P('shard')
- out_average_new: float32 [1024, 1024], P('shard')
- up_weight_new: float32 [1024, 4096], P(None, 'shard')
- up_momentum_new: float32 [1024, 4096], P(None, 'shard')
- up_average_new: float32 [1024, 4096], P(None, 'shard')
- down_weight_new: float32 [4096, 1024], P('shard')
- down_momentum_new: float32 [4096, 1024], P('shard')
- down_average_new: float32 [4096, 1024], P('shard')
- small_params_new: float32 [12, 1024], P(None, 'shard')
- small_momentum_new: float32 [12, 1024], P(None, 'shard')
- small_average_new: float32 [12, 1024], P(None, 'shard')
Inputs may be any that keep to these rules, and one draw needn't show every extreme that they name: `lengths`: the first 512 positions of every sequence are live; in every draw some sequence is live in all 1024 positions and some in exactly 512.
All inputs are finite; a program needn't handle non-finite values.
Results may differ from a plain program's by a relative error of at most 0.012.
Values may be sent and summed in bfloat16 or wider, within the bound.
A program may use at most 384 MiB of HBM per device.

v0:
```python
import math

import jax
import jax.numpy as jnp
from jax import lax
from jax.sharding import PartitionSpec as P

HEADS = 16
FF = 4096


EPS = 1e-05
MOMENTUM = 0.9
AVERAGING = 0.9
NEG_FILL = -1e30


def passed_along(value, axis, steps):
    count = lax.axis_size(axis)
    leading, last = (max(0, -steps), min(count, count - steps))
    return lax.ppermute(value, axis, [(source, source + steps) for source in range(leading, last)])


def norm_stats(field_in):
    centred = field_in - jnp.mean(field_in, axis=-1, keepdims=True)
    inverse = lax.rsqrt(jnp.mean(centred * centred, axis=-1, keepdims=True) + EPS)
    return (centred * inverse, inverse)


def norm_back(grad_hat, normed, inverse):
    first_mean = jnp.mean(grad_hat, axis=-1, keepdims=True)
    second_mean = jnp.mean(grad_hat * normed, axis=-1, keepdims=True)
    return inverse * (grad_hat - first_mean - normed * second_mean)


def contract_rows(left_side, right_side):
    return lax.dot_general(
        left_side, right_side, (((0,), (0,)), ((), ())), preferred_element_type=jnp.float32
    )


def contract_cols(left_side, right_side):
    return lax.dot_general(
        left_side, right_side, (((1,), (1,)), ((), ())), preferred_element_type=jnp.float32
    )


def split_heads(field_in):
    return field_in.reshape(field_in.shape[0], HEADS, -1).transpose(1, 0, 2)


def merge_heads(field_in):
    return field_in.transpose(1, 0, 2).reshape(field_in.shape[1], -1)


def gelu_tanh(field_in):
    return jax.nn.gelu(field_in, approximate=True)


def gelu_back(pre_act, grad_act):
    unused, pull_back = jax.vjp(gelu_tanh, pre_act)
    return pull_back(grad_act)[0]


def head_scores(queries, key_block, slope, allowed, distance, score_scale):
    raw = contract_cols(queries, key_block) * score_scale - slope * distance
    return jnp.where(allowed, raw, NEG_FILL)


def nesterov(grad_total, weight_old, moment_old, average_old, rate):
    moment_new = MOMENTUM * moment_old + grad_total
    weight_new = weight_old - rate * (grad_total + MOMENTUM * moment_new)
    average_new = AVERAGING * average_old + (1.0 - AVERAGING) * weight_new
    return (weight_new, moment_new, average_new)


def body(
    tokens,
    cotangent,
    lengths,
    qkv_weight,
    qkv_momentum,
    qkv_average,
    out_weight,
    out_momentum,
    out_average,
    up_weight,
    up_momentum,
    up_average,
    down_weight,
    down_momentum,
    down_average,
    small_params,
    small_momentum,
    small_average,
):
    tok_rows = tokens.shape[0]
    model_width = tokens.shape[1]
    shard_count = lax.axis_size("shard")
    group_count = lax.axis_size("group")
    shard_place = lax.axis_index("shard")
    group_place = lax.axis_index("group")
    upper_half = shard_place % 2
    seq_place = group_place * (shard_count // 2) + shard_place // 2
    seq_length = lax.dynamic_index_in_dim(lengths, seq_place, 0, keepdims=False)
    local_pos = jnp.arange(tok_rows, dtype=jnp.int32)
    query_pos = upper_half * tok_rows + local_pos
    key_pos = jnp.concatenate([local_pos, query_pos])
    prev_live = jnp.full((tok_rows,), upper_half == 1)
    key_live = jnp.concatenate([prev_live, jnp.ones((tok_rows,), bool)]) & (key_pos < seq_length)
    allowed = key_live[None, :] & (key_pos[None, :] <= query_pos[:, None])
    distance = (query_pos[:, None] - key_pos[None, :]).astype(jnp.float32)
    row_live = (query_pos < seq_length).astype(jnp.float32)[:, None]
    head_size = model_width // HEADS
    score_scale = head_size ** (-0.5)
    slopes = 2.0 ** (-8.0 * (jnp.arange(HEADS, dtype=jnp.float32) + 1.0) / HEADS)
    qkv_low = qkv_weight.astype(jnp.bfloat16)
    out_low = out_weight.astype(jnp.bfloat16)
    up_low = up_weight.astype(jnp.bfloat16)
    down_low = down_weight.astype(jnp.bfloat16)
    small_low = small_params.astype(jnp.bfloat16)
    qkv_full, out_full, small_full, up_full, down_full = (
        lax.all_gather(qkv_low, "shard", axis=0, tiled=True),
        lax.all_gather(out_low, "shard", axis=0, tiled=True),
        lax.all_gather(small_low, "shard", axis=1, tiled=True),
        lax.all_gather(up_low, "shard", axis=1, tiled=True),
        lax.all_gather(down_low, "shard", axis=0, tiled=True),
    )
    table = small_full.astype(jnp.float32)
    up_bias = table[8:12].reshape(FF)
    normed_one, inverse_one = norm_stats(tokens)
    entry_low = (normed_one * table[0] + table[1]).astype(jnp.bfloat16)
    mapped = jnp.dot(entry_low, qkv_full, preferred_element_type=jnp.float32)
    queries = (mapped[:, :model_width] + table[2]).astype(jnp.bfloat16)
    key_own = mapped[:, model_width : 2 * model_width].astype(jnp.bfloat16)
    value_own = (mapped[:, 2 * model_width :] + table[3]).astype(jnp.bfloat16)
    received = passed_along(jnp.concatenate([key_own, value_own], 1), "shard", 1)
    key_all = jnp.concatenate([received[:, :model_width], key_own], 0)
    value_all = jnp.concatenate([received[:, model_width:], value_own], 0)
    query_heads = split_heads(queries)
    key_heads = split_heads(key_all)
    value_heads = split_heads(value_all)

    def head_forward(head_item):
        head_query, head_keys, head_values, slope = head_item
        scores = head_scores(head_query, head_keys, slope, allowed, distance, score_scale)
        row_top = jnp.max(scores, axis=-1, keepdims=True)
        weights = jnp.exp(scores - row_top)
        row_total = jnp.sum(weights, axis=-1, keepdims=True)
        probs_low = (weights / row_total).astype(jnp.bfloat16)
        mixture = jnp.dot(probs_low, head_values, preferred_element_type=jnp.float32)
        return (mixture, (row_top + jnp.log(row_total))[:, 0])

    mixture_heads, log_total = lax.map(head_forward, (query_heads, key_heads, value_heads, slopes))
    attended_low = merge_heads(mixture_heads).astype(jnp.bfloat16)
    resid_one = (
        tokens + jnp.dot(attended_low, out_full, preferred_element_type=jnp.float32) + table[4]
    )
    normed_two, inverse_two = norm_stats(resid_one)
    inner_low = (normed_two * table[5] + table[6]).astype(jnp.bfloat16)
    grad_out = cotangent * row_live
    down_bias_grad = jnp.sum(grad_out, axis=0)
    grad_low = grad_out.astype(jnp.bfloat16)
    pre_act = jnp.dot(inner_low, up_full, preferred_element_type=jnp.float32) + up_bias
    act_low = gelu_tanh(pre_act).astype(jnp.bfloat16)
    branch_out = jnp.dot(act_low, down_full, preferred_element_type=jnp.float32)
    block_out = resid_one + branch_out + table[7]
    grad_act = contract_cols(grad_low, down_full)
    down_grad = contract_rows(act_low, grad_low)
    grad_pre = gelu_back(pre_act, grad_act)
    up_bias_grad = jnp.sum(grad_pre, axis=0)
    pre_low = grad_pre.astype(jnp.bfloat16)
    up_grad = contract_rows(inner_low, pre_low)
    grad_inner = contract_cols(pre_low, up_full)
    gain_two_grad = jnp.sum(grad_inner * normed_two, axis=0)
    shift_two_grad = jnp.sum(grad_inner, axis=0)
    grad_resid = grad_out + norm_back(grad_inner * table[5], normed_two, inverse_two)
    out_bias_grad = jnp.sum(grad_resid, axis=0)
    resid_low = grad_resid.astype(jnp.bfloat16)
    out_grad = contract_rows(attended_low, resid_low)
    grad_mixture = contract_cols(resid_low, out_full).astype(jnp.bfloat16)
    grad_heads = split_heads(grad_mixture)

    def head_backward(head_item):
        head_query, head_keys, head_values, head_grad, head_lse, slope = head_item
        scores = head_scores(head_query, head_keys, slope, allowed, distance, score_scale)
        probs = jnp.exp(scores - head_lse[:, None])
        probs_low = probs.astype(jnp.bfloat16)
        grad_values = contract_rows(probs_low, head_grad)
        grad_probs = contract_cols(head_grad, head_values)
        row_delta = jnp.sum(probs * grad_probs, axis=-1, keepdims=True)
        grad_scores = (probs * (grad_probs - row_delta)).astype(jnp.bfloat16)
        grad_query = (
            jnp.dot(grad_scores, head_keys, preferred_element_type=jnp.float32) * score_scale
        )
        grad_keys = contract_rows(grad_scores, head_query) * score_scale
        return (grad_query, grad_keys, grad_values)

    query_grads, key_grads, value_grads = lax.map(
        head_backward, (query_heads, key_heads, value_heads, grad_heads, log_total, slopes)
    )
    grad_query = merge_heads(query_grads)
    grad_keys = merge_heads(key_grads)
    grad_values = merge_heads(value_grads)
    returned = passed_along(
        jnp.concatenate([grad_keys[:tok_rows], grad_values[:tok_rows]], 1).astype(jnp.bfloat16),
        "shard",
        -1,
    ).astype(jnp.float32)
    grad_key_own = grad_keys[tok_rows:] + returned[:, :model_width]
    grad_value_own = grad_values[tok_rows:] + returned[:, model_width:]
    query_bias_grad = jnp.sum(grad_query, axis=0)
    value_bias_grad = jnp.sum(grad_value_own, axis=0)
    mapped_low = jnp.concatenate([grad_query, grad_key_own, grad_value_own], 1).astype(jnp.bfloat16)
    qkv_grad = contract_rows(entry_low, mapped_low)
    grad_entry = contract_cols(mapped_low, qkv_full)
    gain_one_grad = jnp.sum(grad_entry * normed_one, axis=0)
    shift_one_grad = jnp.sum(grad_entry, axis=0)
    input_grad = grad_resid + norm_back(grad_entry * table[0], normed_one, inverse_one)
    head_rows = jnp.stack(
        [
            gain_one_grad,
            shift_one_grad,
            query_bias_grad,
            value_bias_grad,
            out_bias_grad,
            gain_two_grad,
            shift_two_grad,
            down_bias_grad,
        ]
    )
    small_grad = jnp.concatenate([head_rows, up_bias_grad.reshape(4, model_width)], 0)
    qkv_piece, out_piece, up_piece, down_piece, small_piece = (
        lax.psum_scatter(
            qkv_grad.astype(jnp.bfloat16), "shard", scatter_dimension=0, tiled=True
        ).astype(jnp.float32),
        lax.psum_scatter(
            out_grad.astype(jnp.bfloat16), "shard", scatter_dimension=0, tiled=True
        ).astype(jnp.float32),
        lax.psum_scatter(
            up_grad.astype(jnp.bfloat16), "shard", scatter_dimension=1, tiled=True
        ).astype(jnp.float32),
        lax.psum_scatter(
            down_grad.astype(jnp.bfloat16), "shard", scatter_dimension=0, tiled=True
        ).astype(jnp.float32),
        lax.psum_scatter(
            small_grad.astype(jnp.bfloat16), "shard", scatter_dimension=1, tiled=True
        ).astype(jnp.float32),
    )
    qkv_total, out_total, up_total, down_total, small_total = lax.psum(
        (qkv_piece, out_piece, up_piece, down_piece, small_piece), "group"
    )
    rate = 2.0 / math.sqrt(model_width * tok_rows * shard_count * group_count)
    qkv_new = nesterov(qkv_total, qkv_weight, qkv_momentum, qkv_average, rate)
    out_new = nesterov(out_total, out_weight, out_momentum, out_average, rate)
    up_new = nesterov(up_total, up_weight, up_momentum, up_average, rate)
    down_new = nesterov(down_total, down_weight, down_momentum, down_average, rate)
    small_new = nesterov(small_total, small_params, small_momentum, small_average, rate)
    return (
        block_out,
        input_grad,
        qkv_new[0],
        qkv_new[1],
        qkv_new[2],
        out_new[0],
        out_new[1],
        out_new[2],
        up_new[0],
        up_new[1],
        up_new[2],
        down_new[0],
        down_new[1],
        down_new[2],
        small_new[0],
        small_new[1],
        small_new[2],
    )


def solution(mesh):
    in_specs = (
        P(("group", "shard"), None),
        P(("group", "shard"), None),
        P(),
        P("shard", None),
        P("shard", None),
        P("shard", None),
        P("shard", None),
        P("shard", None),
        P("shard", None),
        P(None, "shard"),
        P(None, "shard"),
        P(None, "shard"),
        P("shard", None),
        P("shard", None),
        P("shard", None),
        P(None, "shard"),
        P(None, "shard"),
        P(None, "shard"),
    )
    out_specs = (
        P(("group", "shard"), None),
        P(("group", "shard"), None),
        P("shard", None),
        P("shard", None),
        P("shard", None),
        P("shard", None),
        P("shard", None),
        P("shard", None),
        P(None, "shard"),
        P(None, "shard"),
        P(None, "shard"),
        P("shard", None),
        P("shard", None),
        P("shard", None),
        P(None, "shard"),
        P(None, "shard"),
        P(None, "shard"),
    )
    return jax.shard_map(body, mesh=mesh, in_specs=in_specs, out_specs=out_specs, check_vma=False)
```

profile of v0, /device:TPU:9, one launch (start us, length us, event | category | flops | bytes accessed | tf_op | source)
XLA Modules:
  0.0 1561.7 jit_solution(5818911206095260283)
XLA Ops:
  15.0 6.1 convert_element_type.119
  27.5 66.7 %all-gather.5.cloned.1.call-done = bf16[1024,3072]{1,0:T(8,128)(2,1)} async-done(((bf16[512,3072]{1,0:T(8,128)(2,1)}), bf16[1024,3072]{1,0:T(8,128)(2,1)}) %all-gather.5.cloned.1.call-update) | async-done | bytes 6291472 | tf_op jit(solution)/shard_map/all_gather | solution.py:123
  94.2 5.8 fusion.71
  106.7 6.1 convert_element_type.121
  121.4 57.3 %collective-permute-done = bf16[512,2048]{1,0:T(8,128)(2,1)} collective-permute-done((bf16[512,2048]{1,0:T(8,128)(2,1)}, bf16[512,2048]{1,0:T(8,128)(2,1)}, u32[]{:S(2)}, u32[]{:S(2)}) %collective-permute-start) | collective-permute-done | bytes 2097184 | tf_op jit(solution)/shard_map/ppermute | solution.py:21
  200.4 87.1 %while.32 = (s32[]{:T(128)}, bf16[16,512,64]{1,2,0:T(8,128)(2,1)S(1)}, f32[16,512]{1,0:T(8,128)S(1)}, bf16[16,512,64]{2,1,0:T(8,128)(2,1)}, bf16[16,1024,64]{2,1...) while((s32[]{:T(128)}, ...), condition=%wide.region_5.6_spmd.clone.clone.clone, body=%wide.region_2.5_spmd.clone.clone.sunk.clone | while | flops 141557248 | bytes 7108221 | solution.py:154
  292.5 12.0 fusion.72
  304.6 65.5 %all-gather.11.cloned.1.call-done = bf16[4096,1024]{1,0:T(8,128)(2,1)} async-done(((bf16[2048,1024]{1,0:T(8,128)(2,1)}), bf16[4096,1024]{1,0:T(8,128)(2,1)}) %all-gather.11.cloned.1.call-update) | async-done | bytes 8388624 | tf_op jit(solution)/shard_map/all_gather | solution.py:127
  370.1 15.6 fusion.78
  385.7 7.2 multiply_reduce_fusion.1
  399.1 164.0 %while.33 = (s32[]{:T(128)}, f32[16,512,64]{1,2,0:T(8,128)}, f32[16,1024,64]{1,2,0:T(8,128)}, f32[16,1024,64]{1,2,0:T(8,128)}, bf16[16,512,64]{2,1,0:T(8,128)(2,...) while((s32[]{:T(128)}, f32[16,512,64]{1,2,0:T(8,128)}, ...), condition=%wide.region_12.13_spmd.clone.clone.clone, body=%wide.region_10.12_spmd.clone.clone.sunk.clone | while | flops 343506432 | bytes 17586836 | solution.py:199
  575.8 41.1 %collective-permute-done.1 = bf16[512,2048]{0,1:T(8,128)(2,1)} collective-permute-done((bf16[512,2048]{0,1:T(8,128)(2,1)}, bf16[512,2048]{0,1:T(8,128)(2,1)}, u32[]{:S(2)}, u32[]{:S(2)}) %collective-permute-start.1) | collective-permute-done | bytes 2097184 | tf_op jit(solution)/shard_map/ppermute | solution.py:21
  620.9 5.2 multiply_reduce_fusion.2
  632.1 8.1 convolution_convert_fusion.2
  640.2 11.0 convolution_convert_fusion.1
  651.4 14.1 convolution_convert_fusion
  666.2 13.4 add_add_fusion
  681.6 71.5 %reduce-scatter.6.cloned.1.call-done = bf16[512,3072]{1,0:T(8,128)(2,1)} async-done(((bf16[1024,3072]{1,0:T(8,128)(2,1)}), bf16[512,3072]{1,0:T(8,128)(2,1)}) %reduce-scatter.6.cloned.1.call-update) | async-done | bytes 3145744 | tf_op jit(solution)/shard_map/reduce_scatter | solution.py:234
  753.1 102.2 %reduce-scatter.10.cloned.1.call-done = bf16[1024,2048]{1,0:T(8,128)(2,1)} async-done(((bf16[1024,4096]{1,0:T(8,128)(2,1)}), bf16[1024,2048]{1,0:T(8,128)(2,1)}) %reduce-scatter.10.cloned.1.call-update) | async-done | bytes 4194320 | tf_op jit(solution)/shard_map/reduce_scatter | solution.py:240
  855.3 102.2 %reduce-scatter.12.cloned.1.call-done = bf16[2048,1024]{1,0:T(8,128)(2,1)} async-done(((bf16[4096,1024]{1,0:T(8,128)(2,1)}), bf16[2048,1024]{1,0:T(8,128)(2,1)}) %reduce-scatter.12.cloned.1.call-update) | async-done | bytes 4194320 | tf_op jit(solution)/shard_map/reduce_scatter | solution.py:243
  957.6 531.3 %all-reduce.3 = (f32[512,3072]{1,0:T(8,128)}, f32[512,1024]{1,0:T(8,128)}, f32[1024,2048]{1,0:T(8,128)}, f32[2048,1024]{1,0:T(8,128)}, f32[12,512]{1,0:T(8,128)S(1)}) all-reduce(bf16[512,3072]{1,0:T(8,128)(2,1)} %reduce-scatter.6.cloned.1.call-done, ...), channel_id=1, replica_groups=mesh['group'=16,'shard'=2] {'group'}, use_global_device_ids=true, to_apply=%region_16.17 | all-reduce | flops 6297600 | bytes 37785600 | tf_op jit(solution)/shard_map/psum | solution.py:250
  1488.9 16.2 %multiply_add_fusion.4 = (f32[512,3072]{1,0:T(8,128)}, f32[512,3072]{1,0:T(8,128)}, f32[512,3072]{1,0:T(8,128)}) fusion(f32[512,3072]{1,0:T(8,128)} %param.27, f32[512,3072]{1,0:T(8,128)} %param.25, f32[512,3072]{1,0:T(8,128)} %get-tuple-element.341, f32[512,3072]{1,0:T(8,128)} %param.26), kind=kLoop, calls=%fused_computation.76 | loop fusion | flops 14155776 | bytes 44040192 | tf_op jit(solution)/shard_map/add | solution.py:73
  1509.1 22.3 %multiply_add_fusion.2 = (f32[1024,2048]{1,0:T(8,128)}, f32[1024,2048]{1,0:T(8,128)}, f32[1024,2048]{1,0:T(8,128)}) fusion(f32[1024,2048]{1,0:T(8,128)} %param.33, f32[1024,2048]{1,0:T(8,128)} %param.31, f32[1024,2048]{1,0:T(8,128)} %get-tuple-element.343, f32[1024,2048]{1,0:T(8,128)} %param.32), kind=kLoop, calls=%fused_computation.70 | loop fusion | flops 18874368 | bytes 58720256 | tf_op jit(solution)/shard_map/add | solution.py:73
  1531.4 22.6 %multiply_add_fusion = (f32[2048,1024]{1,0:T(8,128)}, f32[2048,1024]{1,0:T(8,128)}, f32[2048,1024]{1,0:T(8,128)}) fusion(f32[2048,1024]{1,0:T(8,128)} %param.36, f32[2048,1024]{1,0:T(8,128)} %param.34, f32[2048,1024]{1,0:T(8,128)} %get-tuple-element.344, f32[2048,1024]{1,0:T(8,128)} %param.35), kind=kLoop, calls=%fused_computation.67 | loop fusion | flops 18874368 | bytes 58720256 | tf_op jit(solution)/shard_map/add | solution.py:73
  (385 shorter events, 342.5 us)
Async XLA Ops:
  7.2 87.0 %all-gather.5.cloned.1.call-start = ((), (), s32[]{:S(2)}) async-start(), calls=%async_computation.5 | async-start | bytes 9437184 | tf_op jit(solution)/shard_map/all_gather | solution.py:123
  12.2 275.3 %all-gather.7.cloned.1.call-start = ((), (), s32[]{:S(2)}) async-start(), calls=%async_computation.6 | async-start | bytes 3145728 | tf_op jit(solution)/shard_map/all_gather | solution.py:124
  14.9 277.6 %all-gather.9.cloned.1.call-start = ((), (), s32[]{:S(2)}) async-start(), calls=%async_computation.7 | async-start | bytes 12582912 | tf_op jit(solution)/shard_map/all_gather | solution.py:126
  21.1 349.0 %all-gather.11.cloned.1.call-start = ((), (), s32[]{:S(2)}) async-start(), calls=%async_computation.8 | async-start | bytes 12582912 | tf_op jit(solution)/shard_map/all_gather | solution.py:127
  103.3 75.4 %collective-permute-start = (bf16[512,2048]{1,0:T(8,128)(2,1)}, bf16[512,2048]{1,0:T(8,128)(2,1)}, u32[]{:S(2)}, u32[]{:S(2)}) collective-permute-start(bf16[512,2048]{1,0:T(8,128)(2,1)} %pad_maximum_fusion.1), channel_id=1, source_target_pairs={{0,1},{2,3},{4,5},{6,7},{8,9},{10,11},{12,13},{14,15},{16,17},{18,... | collective-permute-start | bytes 6291464 | tf_op jit(solution)/shard_map/ppermute | solution.py:21
  112.8 568.8 %reduce-scatter.14.cloned.1.call-start = ((), (), s32[]{:S(2)}) async-start(), calls=%async_computation.13 | async-start | bytes 49152 | tf_op jit(solution)/shard_map/reduce_scatter | solution.py:246
  121.4 59.1 %copy-start.2 = (bf16[512,1024]{1,0:T(8,128)(2,1)S(1)}, bf16[512,1024]{1,0:T(8,128)(2,1)}, u32[]{:S(2)}) copy-start(bf16[512,1024]{1,0:T(8,128)(2,1)} %copy-done.1) | copy-start | bytes 3145732
  370.1 15.6 copy-start.8
  370.1 15.6 copy-start.28
  568.0 48.8 %collective-permute-start.1 = (bf16[512,2048]{0,1:T(8,128)(2,1)}, bf16[512,2048]{0,1:T(8,128)(2,1)}, u32[]{:S(2)}, u32[]{:S(2)}) collective-permute-start(bf16[512,2048]{0,1:T(8,128)(2,1)} %pad_maximum_fusion.4), channel_id=1, source_target_pairs={{1,0},{3,2},{5,4},{7,6},{9,8},{11,10},{13,12},{15,14},{17,16},{19,... | collective-permute-start | bytes 6291464 | tf_op jit(solution)/shard_map/ppermute | solution.py:21
  575.7 43.4 %copy-start.10 = (f32[512,16,64]{0,2,1:T(8,128)S(1)}, f32[512,16,64]{0,2,1:T(8,128)}, u32[]{:S(2)}) copy-start(f32[512,16,64]{0,2,1:T(8,128)} %slice.119) | copy-start | bytes 6291460
  575.8 43.4 %copy-start.11 = (f32[512,16,64]{0,2,1:T(8,128)S(1)}, f32[512,16,64]{0,2,1:T(8,128)}, u32[]{:S(2)}) copy-start(f32[512,16,64]{0,2,1:T(8,128)} %slice.115) | copy-start | bytes 6291460
  627.4 54.2 %reduce-scatter.8.cloned.1.call-start = ((), (), s32[]{:S(2)}) async-start(), calls=%async_computation.10 | async-start | bytes 3145728 | tf_op jit(solution)/shard_map/reduce_scatter | solution.py:237
  632.0 121.1 %reduce-scatter.6.cloned.1.call-start = ((), (), s32[]{:S(2)}) async-start(), calls=%async_computation.9 | async-start | bytes 9437184 | tf_op jit(solution)/shard_map/reduce_scatter | solution.py:234
  640.1 215.2 %reduce-scatter.10.cloned.1.call-start = ((), (), s32[]{:S(2)}) async-start(), calls=%async_computation.11 | async-start | bytes 12582912 | tf_op jit(solution)/shard_map/reduce_scatter | solution.py:240
  651.2 306.4 %reduce-scatter.12.cloned.1.call-start = ((), (), s32[]{:S(2)}) async-start(), calls=%async_computation.12 | async-start | bytes 12582912 | tf_op jit(solution)/shard_map/reduce_scatter | solution.py:243
  666.2 13.4 copy-start.17
  1488.9 16.2 %copy-start.6 = (f32[512,1024]{1,0:T(8,128)S(1)}, f32[512,1024]{1,0:T(8,128)}, u32[]{:S(2)}) copy-start(f32[512,1024]{1,0:T(8,128)} %param.28) | copy-start | bytes 6291460
  1488.9 16.2 %copy-start.15 = (f32[512,1024]{1,0:T(8,128)S(1)}, f32[512,1024]{1,0:T(8,128)}, u32[]{:S(2)}) copy-start(f32[512,1024]{1,0:T(8,128)} %param.30) | copy-start | bytes 6291460
  1488.9 16.2 %copy-start.16 = (f32[512,1024]{1,0:T(8,128)S(1)}, f32[512,1024]{1,0:T(8,128)}, u32[]{:S(2)}) copy-start(f32[512,1024]{1,0:T(8,128)} %param.29) | copy-start | bytes 6291460
  1488.9 16.2 %copy-start.18 = (f32[512,1024]{1,0:T(8,128)S(1)}, f32[512,1024]{1,0:T(8,128)}, u32[]{:S(2)}) copy-start(f32[512,1024]{1,0:T(8,128)} %get-tuple-element.342) | copy-start | bytes 6291460
  1531.4 22.6 %copy-start.24 = (f32[12,512]{1,0:T(8,128)S(1)}, f32[12,512]{1,0:T(8,128)}, u32[]{:S(2)}) copy-start(f32[12,512]{1,0:T(8,128)} %param.37) | copy-start | bytes 73732
  1531.4 22.6 %copy-start.25 = (f32[12,512]{1,0:T(8,128)S(1)}, f32[12,512]{1,0:T(8,128)}, u32[]{:S(2)}) copy-start(f32[12,512]{1,0:T(8,128)} %param.39) | copy-start | bytes 73732
  1531.4 22.6 %copy-start.26 = (f32[12,512]{1,0:T(8,128)S(1)}, f32[12,512]{1,0:T(8,128)}, u32[]{:S(2)}) copy-start(f32[12,512]{1,0:T(8,128)} %param.38) | copy-start | bytes 73732
  (20 other events, 67.1 us)
Sparse Core Ops, SparseCore 0:
  12.3 81.8 all-gather.4
  96.3 51.7 all-gather.6
  150.2 112.1 all-gather.8
  264.4 105.6 all-gather.10
  627.6 10.4 reduce-scatter.13
  640.7 32.2 reduce-scatter.7
  675.9 77.1 reduce-scatter.5
  755.9 99.3 reduce-scatter.9
  858.2 99.3 reduce-scatter.11
where the time goes:
time: 1570 us; the launch traced here: 1560 us
  blocking collectives  535 us (34%)
  waiting for transfers between devices  507 us (32%)
  matrix products  320 us (20%)
  other arithmetic  115 us (7%)
  local copies, waits for them, and re-layouts  63.7 us (4%)
    psum x1, blocking collectives, body(): lax.psum((qkv_piece, out_piece, up_piece, down_piece, small_piece), 'group')  531 us
    dot_general x52, matrix products, contract_cols(): lax.dot_general(left_side, right_side, (((1,), (1,)), ((), ())), preferre...  142 us
    reduce_scatter x1, waiting for transfers between devices, body(): lax.psum_scatter(down_grad.astype(jnp.bfloat16), 'shard', scatter_dimensi...  102 us
    reduce_scatter x1, waiting for transfers between devices, body(): lax.psum_scatter(up_grad.astype(jnp.bfloat16), 'shard', scatter_dimension...  102 us
    ppermute x2, waiting for transfers between devices, passed_along(): lax.ppermute(value, axis, [(source, source + steps) for source in range(l...  98.4 us
    dot_general x36, matrix products, contract_rows(): lax.dot_general(left_side, right_side, (((0,), (0,)), ((), ())), preferre...  84.9 us
    reduce_scatter x1, waiting for transfers between devices, body(): lax.psum_scatter(qkv_grad.astype(jnp.bfloat16), 'shard', scatter_dimensio...  71.5 us
    all_gather x1, waiting for transfers between devices, body(): lax.all_gather(qkv_low, 'shard', axis=0, tiled=True)  66.7 us
  transfers between devices with their start and end apart: 11, of which 7 were waited for; matrix products, arithmetic and copies ran while one was open for 14% of the time, Pallas kernels for 0%

commit v1 on v0

--- a/solution.py
+++ b/solution.py
@@ -19,6 +19,46 @@
     count = lax.axis_size(axis)
     leading, last = (max(0, -steps), min(count, count - steps))
     return lax.ppermute(value, axis, [(source, source + steps) for source in range(leading, last)])
+
+
+def gather_weight(weight_own, dim):
+    low_own = weight_own.astype(jnp.bfloat16)
+    cores = lax.axis_size("core")
+    quarter = low_own.shape[dim] // cores
+    mine = lax.dynamic_slice_in_dim(low_own, lax.axis_index("core") * quarter, quarter, axis=dim)
+    across = lax.all_gather(mine, "shard", axis=0, tiled=False)
+    both = lax.all_gather(across, "core", axis=0, tiled=False)
+    if dim == 0:
+        ordered = both.transpose(1, 0, 2, 3)
+        return ordered.reshape(-1, ordered.shape[-1])
+    ordered = both.transpose(2, 1, 0, 3)
+    return ordered.reshape(ordered.shape[0], -1)
+
+
+def reduce_grad(grad_full, dim):
+    low_full = grad_full.astype(jnp.bfloat16)
+    shard_count = lax.axis_size("shard")
+    cores = lax.axis_size("core")
+    outer = lax.axis_size("outer")
+    rows, cols = low_full.shape
+    if dim == 0:
+        split = low_full.reshape(shard_count, cores, rows // (shard_count * cores), cols)
+        split = split.transpose(1, 0, 2, 3)
+    else:
+        split = low_full.reshape(rows, shard_count, cores, cols // (shard_count * cores))
+        split = split.transpose(2, 1, 0, 3)
+    split = lax.psum_scatter(split, "core", scatter_dimension=0, tiled=True)
+    split = lax.psum_scatter(split, "shard", scatter_dimension=1, tiled=True)
+    piece = split.reshape(split.shape[2:])
+    spread_dim = 0 if piece.shape[0] % outer == 0 else 1
+    piece = lax.psum_scatter(piece, "outer", scatter_dimension=spread_dim, tiled=True)
+    piece = lax.all_gather(piece, "outer", axis=spread_dim, tiled=True)
+    piece = lax.all_gather(piece, "core", axis=0, tiled=False)
+    if dim == 0:
+        piece = piece.reshape(-1, piece.shape[-1])
+    else:
+        piece = piece.transpose(1, 0, 2).reshape(piece.shape[1], -1)
+    return piece.astype(jnp.float32)
 
 
 def norm_stats(field_in):
@@ -97,9 +137,9 @@
     tok_rows = tokens.shape[0]
     model_width = tokens.shape[1]
     shard_count = lax.axis_size("shard")
-    group_count = lax.axis_size("group")
+    group_count = lax.axis_size("outer") * lax.axis_size("core")
     shard_place = lax.axis_index("shard")
-    group_place = lax.axis_index("group")
+    group_place = lax.axis_index("outer") * lax.axis_size("core") + lax.axis_index("core")
     upper_half = shard_place % 2
     seq_place = group_place * (shard_count // 2) + shard_place // 2
     seq_length = lax.dynamic_index_in_dim(lengths, seq_place, 0, keepdims=False)
@@ -114,18 +154,11 @@
     head_size = model_width // HEADS
     score_scale = head_size ** (-0.5)
     slopes = 2.0 ** (-8.0 * (jnp.arange(HEADS, dtype=jnp.float32) + 1.0) / HEADS)
-    qkv_low = qkv_weight.astype(jnp.bfloat16)
-    out_low = out_weight.astype(jnp.bfloat16)
-    up_low = up_weight.astype(jnp.bfloat16)
-    down_low = down_weight.astype(jnp.bfloat16)
-    small_low = small_params.astype(jnp.bfloat16)
-    qkv_full, out_full, small_full, up_full, down_full = (
-        lax.all_gather(qkv_low, "shard", axis=0, tiled=True),
-        lax.all_gather(out_low, "shard", axis=0, tiled=True),
-        lax.all_gather(small_low, "shard", axis=1, tiled=True),
-        lax.all_gather(up_low, "shard", axis=1, tiled=True),
-        lax.all_gather(down_low, "shard", axis=0, tiled=True),
-    )
+    qkv_full = gather_weight(qkv_weight, 0)
+    out_full = gather_weight(out_weight, 0)
+    small_full = gather_weight(small_params, 1)
+    up_full = gather_weight(up_weight, 1)
+    down_full = gather_weight(down_weight, 0)
     table = small_full.astype(jnp.float32)
     up_bias = table[8:12].reshape(FF)
     normed_one, inverse_one = norm_stats(tokens)
@@ -230,26 +263,11 @@
         ]
     )
     small_grad = jnp.concatenate([head_rows, up_bias_grad.reshape(4, model_width)], 0)
-    qkv_piece, out_piece, up_piece, down_piece, small_piece = (
-        lax.psum_scatter(
-            qkv_grad.astype(jnp.bfloat16), "shard", scatter_dimension=0, tiled=True
-        ).astype(jnp.float32),
-        lax.psum_scatter(
-            out_grad.astype(jnp.bfloat16), "shard", scatter_dimension=0, tiled=True
-        ).astype(jnp.float32),
-        lax.psum_scatter(
-            up_grad.astype(jnp.bfloat16), "shard", scatter_dimension=1, tiled=True
-        ).astype(jnp.float32),
-        lax.psum_scatter(
-            down_grad.astype(jnp.bfloat16), "shard", scatter_dimension=0, tiled=True
-        ).astype(jnp.float32),
-        lax.psum_scatter(
-            small_grad.astype(jnp.bfloat16), "shard", scatter_dimension=1, tiled=True
-        ).astype(jnp.float32),
-    )
-    qkv_total, out_total, up_total, down_total, small_total = lax.psum(
-        (qkv_piece, out_piece, up_piece, down_piece, small_piece), "group"
-    )
+    qkv_total = reduce_grad(qkv_grad, 0)
+    out_total = reduce_grad(out_grad, 0)
+    up_total = reduce_grad(up_grad, 1)
+    down_total = reduce_grad(down_grad, 0)
+    small_total = reduce_grad(small_grad, 1)
     rate = 2.0 / math.sqrt(model_width * tok_rows * shard_count * group_count)
     qkv_new = nesterov(qkv_total, qkv_weight, qkv_momentum, qkv_average, rate)
     out_new = nesterov(out_total, out_weight, out_momentum, out_average, rate)
@@ -278,9 +296,13 @@
 
 
 def solution(mesh):
+    cores = 2
+    devices = mesh.devices.reshape(mesh.shape["group"] // cores, cores, mesh.shape["shard"])
+    inner_mesh = jax.sharding.Mesh(devices, ("outer", "core", "shard"))
+    rows = P(("outer", "core", "shard"), None)
     in_specs = (
-        P(("group", "shard"), None),
-        P(("group", "shard"), None),
+        rows,
+        rows,
         P(),
         P("shard", None),
         P("shard", None),
@@ -299,22 +321,22 @@
         P(None, "shard"),
     )
     out_specs = (
-        P(("group", "shard"), None),
-        P(("group", "shard"), None),
-        P("shard", None),
-        P("shard", None),
-        P("shard", None),
-        P("shard", None),
-        P("shard", None),
-        P("shard", None),
-        P(None, "shard"),
-        P(None, "shard"),
-        P(None, "shard"),
-        P("shard", None),
-        P("shard", None),
-        P("shard", None),
-        P(None, "shard"),
-        P(None, "shard"),
-        P(None, "shard"),
-    )
-    return jax.shard_map(body, mesh=mesh, in_specs=in_specs, out_specs=out_specs, check_vma=False)
+        rows,
+        rows,
+        P("shard", None),
+        P("shard", None),
+        P("shard", None),
+        P("shard", None),
+        P("shard", None),
+        P("shard", None),
+        P(None, "shard"),
+        P(None, "shard"),
+        P(None, "shard"),
+        P("shard", None),
+        P("shard", None),
+        P("shard", None),
+        P(None, "shard"),
+        P(None, "shard"),
+        P(None, "shard"),
+    )
+    return jax.shard_map(body, mesh=inner_mesh, in_specs=in_specs, out_specs=out_specs, check_vma=False)

time: 1570 us -> 1560 us (level)
  blocking collectives: 535 us -> 69 us
  waiting for transfers between devices: 507 us -> 889 us
  local copies, waits for them, and re-layouts: 63.7 us -> 143 us
  other arithmetic: 115 us -> 97.9 us
    psum x1 -> x0, blocking collectives: 531 us -> none  [body(): lax.psum((qkv_piece, out_piece, up_piece, down_piece, small_piece), 'group')]
    reduce_scatter x5 -> x13, waiting for transfers between devices: 276 us -> 473 us  [the longest x4 271 us: reduce_grad(): lax.psum_scatter(piece, 'outer', scatter_dimension=spread_dim, tiled=True)]
    all_gather x4 -> x15, waiting for transfers between devices: 132 us -> 321 us  [the longest x4 201 us: gather_weight(): across = lax.all_gather(mine, 'shard', axis=0, tiled=False)]
    all_gather x1 -> x5, blocking collectives: 3.32 us -> 64.9 us  [the longest x2 48.1 us: reduce_grad(): piece = lax.all_gather(piece, 'outer', axis=spread_dim, tiled=True)]
    ppermute x2, waiting for transfers between devices: 98.4 us -> 44.4 us  [passed_along(): lax.ppermute(value, axis, [(source, source + steps) for source in range(l...]
    unnamed x9 -> x30, waiting for transfers between devices: 0.15 us -> 49.9 us
    reshape x1 -> x5, local copies, waits for them, and re-layouts: 0.01 us -> 37 us  [the longest x2 24.3 us: reduce_grad(): low_full.reshape(rows, shard_count, cores, cols // (shard_count * cores))]
    transpose x0 -> x5, local copies, waits for them, and re-layouts: none -> 25.6 us  [the longest x3 14.2 us: gather_weight(): ordered = both.transpose(1, 0, 2, 3)]
  transfers between devices with their start and end apart: 11 -> 31, of which waited for: 7 -> 24; matrix products, arithmetic and copies ran while one was open for 14% -> 20% of each run, Pallas kernels for 0% -> 0%
where the time goes in v1:
time: 1560 us; the launch traced here: 1540 us
  waiting for transfers between devices  889 us (57%)
  matrix products  322 us (21%)
  local copies, waits for them, and re-layouts  143 us (9%)
  other arithmetic  97.9 us (6%)
  blocking collectives  69 us (4%)
    reduce_scatter x4, waiting for transfers between devices, reduce_grad(): lax.psum_scatter(piece, 'outer', scatter_dimension=spread_dim, tiled=True)  271 us
    all_gather x4, waiting for transfers between devices, gather_weight(): across = lax.all_gather(mine, 'shard', axis=0, tiled=False)  201 us
    reduce_scatter x5, waiting for transfers between devices, reduce_grad(): split = lax.psum_scatter(split, 'shard', scatter_dimension=1, tiled=True)  177 us
    dot_general x52, matrix products, contract_cols(): lax.dot_general(left_side, right_side, (((1,), (1,)), ((), ())), preferre...  148 us
    all_gather x3, waiting for transfers between devices, reduce_grad(): piece = lax.all_gather(piece, 'outer', axis=spread_dim, tiled=True)  89 us
    dot_general x36, matrix products, contract_rows(): lax.dot_general(left_side, right_side, (((0,), (0,)), ((), ())), preferre...  85 us
    add x5, other arithmetic, nesterov(): average_new = AVERAGING * average_old + (1.0 - AVERAGING) * weight_new  64.9 us
    unnamed x30, waiting for transfers between devices  49.9 us
  transfers between devices with their start and end apart: 31, of which 24 were waited for; matrix products, arithmetic and copies ran while one was open for 20% of the time, Pallas kernels for 0%

profile of v1, /device:TPU:9, one launch (start us, length us, event | category | flops | bytes accessed | tf_op | source)
XLA Modules:
  0.0 1544.8 jit_solution(16976272134874888948)
XLA Ops:
  16.7 39.9 %all-gather.40.cloned.1.call-done = bf16[512,3072]{1,0:T(8,128)(2,1)} async-done(((bf16[256,3072]{1,0:T(8,128)(2,1)}), bf16[512,3072]{1,0:T(8,128)(2,1)}) %all-gather.40.cloned.1.call-update) | async-done | bytes 3145744 | tf_op jit(solution)/shard_map/all_gather | solution.py:29
  56.6 23.4 %all-gather.44.cloned.1.call-done = bf16[512,1024]{1,0:T(8,128)(2,1)} async-done(((bf16[256,1024]{1,0:T(8,128)(2,1)}), bf16[512,1024]{1,0:T(8,128)(2,1)}) %all-gather.44.cloned.1.call-update) | async-done | bytes 1048592 | tf_op jit(solution)/shard_map/all_gather | solution.py:29
  84.0 54.9 %all-gather.48.cloned.1.call-done = bf16[2048,1024]{1,0:T(8,128)(2,1)} async-done(((bf16[1024,1024]{1,0:T(8,128)(2,1)}), bf16[2048,1024]{1,0:T(8,128)(2,1)}) %all-gather.48.cloned.1.call-update) | async-done | bytes 4194320 | tf_op jit(solution)/shard_map/all_gather | solution.py:29
  179.4 82.5 %all-gather.52.cloned.1.call-done = bf16[2048,1024]{1,0:T(8,128)(2,1)} async-done(((bf16[1024,1024]{1,0:T(8,128)(2,1)}), bf16[2048,1024]{1,0:T(8,128)(2,1)}) %all-gather.52.cloned.1.call-update) | async-done | bytes 4194320 | tf_op jit(solution)/shard_map/all_gather | solution.py:29
  292.1 87.0 %while.32 = (s32[]{:T(128)}, bf16[16,512,64]{1,2,0:T(8,128)(2,1)S(1)}, f32[16,512]{1,0:T(8,128)S(1)}, bf16[16,512,64]{2,1,0:T(8,128)(2,1)}, bf16[16,1024,64]{2,1...) while((s32[]{:T(128)}, ...), condition=%wide.region_5.6_spmd.clone.clone.clone, body=%wide.region_2.5_spmd.clone.clone.sunk.clone | while | flops 141557248 | bytes 7108221 | solution.py:187
  414.1 16.2 %fusion.88 = (bf16[4096]{0:T(1024)(128)(2,1)S(1)}, bf16[512,4096]{1,0:T(8,128)(2,1)}) fusion(f32[512,4096]{1,0:T(8,128)} %fusion.79, f32[4096]{0:T(1024)S(1)} %bitcast.324, bf16[4096,1024]{1,0:T(8,128)(2,1)S(1)} %bitcast.266, f32[512,1024]{1,0:T(8,128)S(1)} %copy-done.13, f32[512]{0:T(512)S(1)} %compare_convert_fusion), kind=kOutput, calls=%fused_computation.191 | convolution fusion | flops 4342149120 | bytes 23095296 | tf_op jit(solution)/shard_map/dot_general | solution.py:83
  445.2 163.7 %while.33 = (s32[]{:T(128)}, f32[16,512,64]{1,2,0:T(8,128)}, f32[16,1024,64]{1,2,0:T(8,128)}, f32[16,1024,64]{1,2,0:T(8,128)}, bf16[16,512,64]{2,1,0:T(8,128)(2,...) while((s32[]{:T(128)}, f32[16,512,64]{1,2,0:T(8,128)}, ...), condition=%wide.region_12.13_spmd.clone.clone.clone, body=%wide.region_10.12_spmd.clone.clone.sunk.clone | while | flops 343506432 | bytes 17586836 | solution.py:232
  617.7 44.4 %collective-permute-done.1 = bf16[512,2048]{0,1:T(8,128)(2,1)S(1)} collective-permute-done((bf16[512,2048]{0,1:T(8,128)(2,1)S(1)}, bf16[512,2048]{0,1:T(8,128)(2,1)S(1)}, u32[]{:S(2)}, u32[]{:S(2)}) %collective-permute-start.1) | collective-permute-done | bytes 2097184 | tf_op jit(solution)/shard_map/ppermute | solution.py:21
  765.1 46.0 %reduce-scatter.19.cloned.1.call-done = bf16[1,1,256,3072]{3,2,1,0:T(8,128)(2,1)} async-done(((bf16[1,2,256,3072]{3,2,1,0:T(8,128)(2,1)}), bf16[1,1,256,3072]{3,2,1,0:T(8,128)(2,1)}) %reduce-scatter.19.cloned.1.call-update) | async-done | bytes 1572880 | tf_op jit(solution)/shard_map/reduce_scatter | solution.py:51
  811.1 56.5 %reduce-scatter.31.cloned.1.call-done = bf16[1,1,1024,1024]{3,2,1,0:T(8,128)(2,1)} async-done(((bf16[1,2,1024,1024]{3,2,1,0:T(8,128)(2,1)}), bf16[1,1,1024,1024]{3,2,1,0:T(8,128)(2,1)}) %reduce-scatter.31.cloned.1.call-update) | async-done | bytes 2097168 | tf_op jit(solution)/shard_map/reduce_scatter | solution.py:51
  884.9 39.4 %reduce-scatter.37.cloned.1.call-done = bf16[1,1,1024,1024]{3,2,1,0:T(8,128)(2,1)} async-done(((bf16[1,2,1024,1024]{3,2,1,0:T(8,128)(2,1)}), bf16[1,1,1024,1024]{3,2,1,0:T(8,128)(2,1)}) %reduce-scatter.37.cloned.1.call-update) | async-done | bytes 2097168 | tf_op jit(solution)/shard_map/reduce_scatter | solution.py:51
  924.3 22.4 %reduce-scatter.25.cloned.1.call-done = bf16[1,1,256,1024]{3,2,1,0:T(8,128)(2,1)} async-done(((bf16[1,2,256,1024]{3,2,1,0:T(8,128)(2,1)}), bf16[1,1,256,1024]{3,2,1,0:T(8,128)(2,1)}) %reduce-scatter.25.cloned.1.call-update) | async-done | bytes 524304 | tf_op jit(solution)/shard_map/reduce_scatter | solution.py:51
  946.8 66.4 %reduce-scatter.21.cloned.1.call-done = bf16[32,3072]{1,0:T(8,128)(2,1)} async-done(((bf16[256,3072]{1,0:T(8,128)(2,1)}), bf16[32,3072]{1,0:T(8,128)(2,1)}) %reduce-scatter.21.cloned.1.call-update) | async-done | bytes 196624 | tf_op jit(solution)/shard_map/reduce_scatter | solution.py:54
  1013.2 71.0 %reduce-scatter.33.cloned.1.call-done = bf16[128,1024]{1,0:T(8,128)(2,1)} async-done(((bf16[1024,1024]{1,0:T(8,128)(2,1)}), bf16[128,1024]{1,0:T(8,128)(2,1)}) %reduce-scatter.33.cloned.1.call-update) | async-done | bytes 262160 | tf_op jit(solution)/shard_map/reduce_scatter | solution.py:54
  1098.8 68.9 %reduce-scatter.39.cloned.1.call-done = bf16[128,1024]{1,0:T(8,128)(2,1)} async-done(((bf16[1024,1024]{1,0:T(8,128)(2,1)}), bf16[128,1024]{1,0:T(8,128)(2,1)}) %reduce-scatter.39.cloned.1.call-update) | async-done | bytes 262160 | tf_op jit(solution)/shard_map/reduce_scatter | solution.py:54
  1167.8 64.8 %reduce-scatter.27.cloned.1.call-done = bf16[32,1024]{1,0:T(8,128)(2,1)} async-done(((bf16[256,1024]{1,0:T(8,128)(2,1)}), bf16[32,1024]{1,0:T(8,128)(2,1)}) %reduce-scatter.27.cloned.1.call-update) | async-done | bytes 65552 | tf_op jit(solution)/shard_map/reduce_scatter | solution.py:54
  1232.5 25.8 %all_gather.128 = bf16[256,1024]{1,0:T(8,128)(2,1)} all-gather(bf16[32,1024]{1,0:T(8,128)(2,1)} %reduce-scatter.27.cloned.1.call-done), channel_id=1, replica_groups=mesh['outer'=8,'core'=2,'shard'=2] {'outer'}, dimensions={0}, use_global_device_ids=true | all-gather | bytes 589824 | tf_op jit(solution)/shard_map/all_gather | solution.py:55
  1258.4 21.8 %all-gather.34.cloned.1.call-done = bf16[256,3072]{1,0:T(8,128)(2,1)} async-done(((bf16[32,3072]{1,0:T(8,128)(2,1)}), bf16[256,3072]{1,0:T(8,128)(2,1)}) %all-gather.34.cloned.1.call-update) | async-done | bytes 1572880 | tf_op jit(solution)/shard_map/all_gather | solution.py:55
  1280.3 49.7 %all-gather.36.cloned.1.call-done = bf16[1024,1024]{1,0:T(8,128)(2,1)} async-done(((bf16[128,1024]{1,0:T(8,128)(2,1)}), bf16[1024,1024]{1,0:T(8,128)(2,1)}) %all-gather.36.cloned.1.call-update) | async-done | bytes 2097168 | tf_op jit(solution)/shard_map/all_gather | solution.py:55
  1345.5 48.3 %reduce-scatter.43.cloned.1.call-done = bf16[32,12]{1,0:T(8,128)(2,1)} async-done(((bf16[256,12]{1,0:T(8,128)(2,1)}), bf16[32,12]{1,0:T(8,128)(2,1)}) %reduce-scatter.43.cloned.1.call-update) | async-done | bytes 784
  1394.6 22.3 %all-gather.16 = bf16[8,32,12]{1,2,0:T(8,128)(2,1)S(1)} all-gather(bf16[1,32,12]{1,2,0:T(8,128)(2,1)S(1)} %bitcast.323), channel_id=1, replica_groups=mesh['outer'=8,'core'=2,'shard'=2] {'outer'}, dimensions={0}, use_global_device_ids=true | all-gather | bytes 6912 | tf_op jit(solution)/shard_map/all_gather | solution.py:55
  1427.8 17.4 %all-gather.38.cloned.1.call-done = bf16[1024,1024]{1,0:T(8,128)(2,1)} async-done(((bf16[128,1024]{1,0:T(8,128)(2,1)}), bf16[1024,1024]{1,0:T(8,128)(2,1)}) %all-gather.38.cloned.1.call-update) | async-done | bytes 2097168 | tf_op jit(solution)/shard_map/all_gather | solution.py:55
  1494.6 24.5 %multiply_add_fusion.1 = (f32[1024,2048]{1,0:T(8,128)}, f32[1024,2048]{1,0:T(8,128)}, f32[1024,2048]{1,0:T(8,128)}) fusion(f32[1024,2048]{1,0:T(8,128)} %param.33, f32[1024,2048]{1,0:T(8,128)} %param.31, f32[1024,2048]{1,0:T(8,128)} %bitcast.259, f32[1024,2048]{1,0:T(8,128)} %param.32), kind=kLoop, calls=%fused_computation.75 | loop fusion | flops 18874368 | bytes 58720256 | tf_op jit(solution)/shard_map/add | solution.py:113
  1519.1 18.6 %multiply_add_fusion = (f32[2048,1024]{1,0:T(8,128)}, f32[2048,1024]{1,0:T(8,128)}, f32[2048,1024]{1,0:T(8,128)}) fusion(f32[2048,1024]{1,0:T(8,128)} %param.36, f32[2048,1024]{1,0:T(8,128)} %param.34, bf16[2048,1024]{1,0:T(8,128)(2,1)} %all-gather.62.cloned.1.call-done, f32[2048,1024]{1,0:T(8,128)} %param.35), kind=kLoop, calls=%fused_computation.74 | loop fusion | flops 20971520 | bytes 54525952 | tf_op jit(solution)/shard_map/add | solution.py:113
  (479 shorter events, 603.6 us)
Async XLA Ops:
  12.7 126.2 %all-gather.48.cloned.1.call-start = ((), (), s32[]{:S(2)}) async-start(), calls=%async_computation.34 | async-start | bytes 6291456 | tf_op jit(solution)/shard_map/all_gather | solution.py:29
  16.6 141.3 %all-gather.42.cloned.1.call-start = ((), (), s32[]{:S(2)}) async-start(), calls=%async_computation.31 | async-start | bytes 9437184 | tf_op jit(solution)/shard_map/all_gather | solution.py:30
  56.6 119.8 %all-gather.46.cloned.1.call-start = ((), (), s32[]{:S(2)}) async-start(), calls=%async_computation.33 | async-start | bytes 3145728 | tf_op jit(solution)/shard_map/all_gather | solution.py:30
  80.0 181.9 %all-gather.52.cloned.1.call-start = ((), (), s32[]{:S(2)}) async-start(), calls=%async_computation.36 | async-start | bytes 6291456 | tf_op jit(solution)/shard_map/all_gather | solution.py:29
  83.9 300.3 %all-gather.50.cloned.1.call-start = ((), (), s32[]{:S(2)}) async-start(), calls=%async_computation.35 | async-start | bytes 12582912 | tf_op jit(solution)/shard_map/all_gather | solution.py:30
  138.9 256.7 %all-gather.54.cloned.1.call-start = ((), (), s32[]{:S(2)}) async-start(), calls=%async_computation.37 | async-start | bytes 12582912 | tf_op jit(solution)/shard_map/all_gather | solution.py:30
  168.2 99.0 %collective-permute-start = (bf16[512,2048]{1,0:T(8,128)(2,1)}, bf16[512,2048]{1,0:T(8,128)(2,1)}, u32[]{:S(2)}, u32[]{:S(2)}) collective-permute-start(bf16[512,2048]{1,0:T(8,128)(2,1)} %pad_maximum_fusion.1), channel_id=1, source_target_pairs={{0,1},{2,3},{4,5},{6,7},{8,9},{10,11},{12,13},{14,15},{16,17},{18,... | collective-permute-start | bytes 6291464 | tf_op jit(solution)/shard_map/ppermute | solution.py:21
  261.9 476.7 %reduce-scatter.17.cloned.1.call-start = ((), (), s32[]{:S(2)}) async-start(), calls=%async_computation.14 | async-start | bytes 9437184 | tf_op jit(solution)/shard_map/reduce_scatter | solution.py:50
  739.3 128.3 %reduce-scatter.31.cloned.1.call-start = ((), (), s32[]{:S(2)}) async-start(), calls=%async_computation.22 | async-start | bytes 6291456 | tf_op jit(solution)/shard_map/reduce_scatter | solution.py:51
  739.9 184.3 %reduce-scatter.37.cloned.1.call-start = ((), (), s32[]{:S(2)}) async-start(), calls=%async_computation.26 | async-start | bytes 6291456 | tf_op jit(solution)/shard_map/reduce_scatter | solution.py:51
  751.2 195.5 %reduce-scatter.25.cloned.1.call-start = ((), (), s32[]{:S(2)}) async-start(), calls=%async_computation.19 | async-start | bytes 1572864 | tf_op jit(solution)/shard_map/reduce_scatter | solution.py:51
  765.0 248.2 %reduce-scatter.21.cloned.1.call-start = ((), (), s32[]{:S(2)}) async-start(), calls=%async_computation.16 | async-start | bytes 1769472 | tf_op jit(solution)/shard_map/reduce_scatter | solution.py:54
  811.1 273.1 %reduce-scatter.33.cloned.1.call-start = ((), (), s32[]{:S(2)}) async-start(), calls=%async_computation.23 | async-start | bytes 2359296 | tf_op jit(solution)/shard_map/reduce_scatter | solution.py:54
  867.7 229.6 %reduce-scatter.41.cloned.1.call-start = ((), (), s32[]{:S(2)}) async-start(), calls=%async_computation.29 | async-start | bytes 24576 | tf_op jit(solution)/shard_map/reduce_scatter | solution.py:51
  884.8 282.9 %reduce-scatter.39.cloned.1.call-start = ((), (), s32[]{:S(2)}) async-start(), calls=%async_computation.27 | async-start | bytes 2359296 | tf_op jit(solution)/shard_map/reduce_scatter | solution.py:54
  924.2 308.3 %reduce-scatter.27.cloned.1.call-start = ((), (), s32[]{:S(2)}) async-start(), calls=%async_computation.20 | async-start | bytes 589824 | tf_op jit(solution)/shard_map/reduce_scatter | solution.py:54
  946.7 333.5 %all-gather.34.cloned.1.call-start = ((), (), s32[]{:S(2)}) async-start(), calls=%async_computation.17 | async-start | bytes 1769472 | tf_op jit(solution)/shard_map/all_gather | solution.py:55
  1013.2 316.8 %all-gather.36.cloned.1.call-start = ((), (), s32[]{:S(2)}) async-start(), calls=%async_computation.24 | async-start | bytes 2359296 | tf_op jit(solution)/shard_map/all_gather | solution.py:55
  1084.2 309.5 %reduce-scatter.43.cloned.1.call-start = ((), (), s32[]{:S(2)}) async-start(), calls=%async_computation.42 | async-start | bytes 73728
  1098.7 346.5 %all-gather.38.cloned.1.call-start = ((), (), s32[]{:S(2)}) async-start(), calls=%async_computation.28 | async-start | bytes 2359296 | tf_op jit(solution)/shard_map/all_gather | solution.py:55
  1167.7 288.3 %all-gather.58.cloned.1.call-start = ((), (), s32[]{:S(2)}) async-start(), calls=%async_computation.39 | async-start | bytes 1572864 | tf_op jit(solution)/shard_map/all_gather | solution.py:56
  1258.3 212.4 %all-gather.56.cloned.1.call-start = ((), (), s32[]{:S(2)}) async-start(), calls=%async_computation.38 | async-start | bytes 4718592 | tf_op jit(solution)/shard_map/all_gather | solution.py:56
  1280.3 206.9 %all-gather.60.cloned.1.call-start = ((), (), s32[]{:S(2)}) async-start(), calls=%async_computation.40 | async-start | bytes 6291456 | tf_op jit(solution)/shard_map/all_gather | solution.py:56
  1330.1 189.1 %all-gather.62.cloned.1.call-start = ((), (), s32[]{:S(2)}) async-start(), calls=%async_computation.41 | async-start | bytes 6291456 | tf_op jit(solution)/shard_map/all_gather | solution.py:56
  (33 other events, 1028.3 us)
Sparse Core Ops, SparseCore 0:
  10.6 45.8 all-gather.39
  58.7 21.2 all-gather.43
  82.1 56.7 all-gather.47
  140.3 17.6 all-gather.41
  173.1 88.7 all-gather.51
  263.4 22.4 all-gather.49
  287.4 21.0 all-gather.53
  673.8 15.2 reduce-scatter.16
  710.0 17.6 reduce-scatter.28
  733.9 17.2 reduce-scatter.34
  767.2 43.8 reduce-scatter.18
  813.2 54.3 reduce-scatter.30
  869.8 54.3 reduce-scatter.36
  926.3 20.3 reduce-scatter.24
  950.0 63.1 reduce-scatter.20
  1016.6 67.6 reduce-scatter.32
  1100.6 67.0 reduce-scatter.38
  1171.0 61.4 reduce-scatter.26
  1234.7 45.4 all-gather.33
  1282.4 47.6 all-gather.35
  1333.9 59.8 reduce-scatter.42
  1395.9 49.3 all-gather.37
  1472.3 14.8 all-gather.59
  1488.7 14.8 all-gather.61
  (5 shorter events, 55.4 us)

commit v2 on v1

--- a/solution.py
+++ b/solution.py
@@ -4,6 +4,7 @@
 import jax.numpy as jnp
 from jax import lax
 from jax.sharding import PartitionSpec as P
+
 
 HEADS = 16
 FF = 4096
@@ -35,30 +36,67 @@
     return ordered.reshape(ordered.shape[0], -1)
 
 
-def reduce_grad(grad_full, dim):
-    low_full = grad_full.astype(jnp.bfloat16)
+LANE = 1024
+
+
+def pack_halves(grad_full, dim, blocks):
+    shard_count = lax.axis_size("shard")
+    rows, cols = grad_full.shape
+    if dim == 0:
+        halves = grad_full.reshape(shard_count, -1)
+    else:
+        halves = grad_full.reshape(rows, shard_count, cols // shard_count).transpose(1, 0, 2)
+        halves = halves.reshape(shard_count, -1)
+    half_size = halves.shape[1]
+    padded = -(-half_size // (blocks * LANE)) * blocks * LANE
+    if padded != half_size:
+        halves = jnp.pad(halves, ((0, 0), (0, padded - half_size)))
+    return halves.reshape(shard_count, blocks, -1, LANE), half_size
+
+
+def unpack_half(packed, half_size, half_shape):
+    return packed.reshape(-1)[:half_size].reshape(half_shape)
+
+
+def reduce_grads(grads):
     shard_count = lax.axis_size("shard")
     cores = lax.axis_size("core")
     outer = lax.axis_size("outer")
-    rows, cols = low_full.shape
-    if dim == 0:
-        split = low_full.reshape(shard_count, cores, rows // (shard_count * cores), cols)
-        split = split.transpose(1, 0, 2, 3)
-    else:
-        split = low_full.reshape(rows, shard_count, cores, cols // (shard_count * cores))
-        split = split.transpose(2, 1, 0, 3)
-    split = lax.psum_scatter(split, "core", scatter_dimension=0, tiled=True)
-    split = lax.psum_scatter(split, "shard", scatter_dimension=1, tiled=True)
-    piece = split.reshape(split.shape[2:])
-    spread_dim = 0 if piece.shape[0] % outer == 0 else 1
-    piece = lax.psum_scatter(piece, "outer", scatter_dimension=spread_dim, tiled=True)
-    piece = lax.all_gather(piece, "outer", axis=spread_dim, tiled=True)
-    piece = lax.all_gather(piece, "core", axis=0, tiled=False)
-    if dim == 0:
-        piece = piece.reshape(-1, piece.shape[-1])
-    else:
-        piece = piece.transpose(1, 0, 2).reshape(piece.shape[1], -1)
-    return piece.astype(jnp.float32)
+    blocks = cores * outer
+    packed, sizes, shapes = [], [], []
+    for grad_full, dim in grads:
+        piece, half_size = pack_halves(grad_full, dim, blocks)
+        packed.append(piece)
+        sizes.append(half_size)
+        rows, cols = grad_full.shape
+        shapes.append((rows // shard_count, cols) if dim == 0 else (rows, cols // shard_count))
+    widths = [piece.shape[2] for piece in packed]
+    return reduce_packed(packed, widths, sizes, shapes)
+
+
+def reduce_packed(packed, widths, sizes, shapes):
+    shard_count = lax.axis_size("shard")
+    cores = lax.axis_size("core")
+    outer = lax.axis_size("outer")
+    blocks = cores * outer
+    stacked = jnp.concatenate(packed, axis=2).astype(jnp.bfloat16)
+    stacked = stacked.reshape(shard_count, cores, outer, -1, LANE).transpose(1, 2, 0, 3, 4)
+    stacked = stacked.reshape(cores, -1, LANE)
+    stacked = lax.psum_scatter(stacked, "core", scatter_dimension=0, tiled=True)
+    stacked = stacked.reshape(outer, -1, LANE)
+    stacked = lax.psum_scatter(stacked, "outer", scatter_dimension=0, tiled=True)
+    stacked = stacked.reshape(shard_count, -1, LANE)
+    stacked = lax.psum_scatter(stacked, "shard", scatter_dimension=0, tiled=True)
+    stacked = stacked.reshape(stacked.shape[1:])
+    stacked = lax.all_gather(stacked, "outer", axis=0, tiled=True)
+    stacked = lax.all_gather(stacked, "core", axis=0, tiled=True)
+    stacked = stacked.reshape(blocks, -1, LANE).astype(jnp.float32)
+    totals = []
+    offset = 0
+    for width, half_size, half_shape in zip(widths, sizes, shapes):
+        totals.append(unpack_half(stacked[:, offset : offset + width], half_size, half_shape))
+        offset += width
+    return totals
 
 
 def norm_stats(field_in):
@@ -98,7 +136,7 @@
 
 
 def gelu_back(pre_act, grad_act):
-    unused, pull_back = jax.vjp(gelu_tanh, pre_act)
+    _, pull_back = jax.vjp(gelu_tanh, pre_act)
     return pull_back(grad_act)[0]
 
 
@@ -208,6 +246,8 @@
     gain_two_grad = jnp.sum(grad_inner * normed_two, axis=0)
     shift_two_grad = jnp.sum(grad_inner, axis=0)
     grad_resid = grad_out + norm_back(grad_inner * table[5], normed_two, inverse_two)
+    grad_resid, up_grad, down_grad = lax.optimization_barrier((grad_resid, up_grad, down_grad))
+    up_total, down_total = reduce_grads([(up_grad, 1), (down_grad, 0)])
     out_bias_grad = jnp.sum(grad_resid, axis=0)
     resid_low = grad_resid.astype(jnp.bfloat16)
     out_grad = contract_rows(attended_low, resid_low)
@@ -263,11 +303,7 @@
         ]
     )
     small_grad = jnp.concatenate([head_rows, up_bias_grad.reshape(4, model_width)], 0)
-    qkv_total = reduce_grad(qkv_grad, 0)
-    out_total = reduce_grad(out_grad, 0)
-    up_total = reduce_grad(up_grad, 1)
-    down_total = reduce_grad(down_grad, 0)
-    small_total = reduce_grad(small_grad, 1)
+    qkv_total, out_total, small_total = reduce_grads([(qkv_grad, 0), (out_grad, 0), (small_grad, 1)])
     rate = 2.0 / math.sqrt(model_width * tok_rows * shard_count * group_count)
     qkv_new = nesterov(qkv_total, qkv_weight, qkv_momentum, qkv_average, rate)
     out_new = nesterov(out_total, out_weight, out_momentum, out_average, rate)
@@ -339,4 +375,5 @@
         P(None, "shard"),
         P(None, "shard"),
     )
+
     return jax.shard_map(body, mesh=inner_mesh, in_specs=in_specs, out_specs=out_specs, check_vma=False)

time: 1560 us -> 1380 us (0.88)
  waiting for transfers between devices: 889 us -> 700 us
  local copies, waits for them, and re-layouts: 143 us -> 208 us
  blocking collectives: 69 us -> 6.66 us
  other arithmetic: 97.9 us -> 116 us
    reduce_scatter x13 -> x6, waiting for transfers between devices: 473 us -> 303 us  [the longest x2 242 us: reduce_packed(): lax.psum_scatter(stacked, 'outer', scatter_dimension=0, tiled=True)]
    all_gather x3 -> x0, blocking collectives: 58.2 us -> none  [the longest x2 48.1 us: reduce_grad(): piece = lax.all_gather(piece, 'outer', axis=spread_dim, tiled=True)]
    unnamed x30 -> x18, waiting for transfers between devices: 49.9 us -> 0.29 us
    all_gather x7 -> x4, waiting for transfers between devices: 110 us -> 147 us  [the longest x2 143 us: reduce_packed(): stacked = lax.all_gather(stacked, 'outer', axis=0, tiled=True)]
    concatenate x0 -> x3, local copies, waits for them, and re-layouts: none -> 24.2 us  [reduce_packed(): stacked = jnp.concatenate(packed, axis=2).astype(jnp.bfloat16)]
    slice x0 -> x5, local copies, waits for them, and re-layouts: none -> 20.4 us  [the longest x4 20.3 us: reduce_packed(): stacked[:, offset:offset + width]]
    another operation x0 -> x2, local copies, waits for them, and re-layouts: none -> 17.8 us  [unpack_half(): return packed.reshape(-1)[:half_size].reshape(half_shape)]
  transfers between devices with their start and end apart: 31 -> 20, of which waited for: 24 -> 14; matrix products, arithmetic and copies ran while one was open for 20% -> 20% of each run, Pallas kernels for 0% -> 0%
where the time goes in v2:
time: 1380 us; the launch traced here: 1370 us
  waiting for transfers between devices  700 us (51%)
  matrix products  312 us (23%)
  local copies, waits for them, and re-layouts  208 us (15%)
  other arithmetic  116 us (8%)
  between operations  15.2 us (1%)
    reduce_scatter x2, waiting for transfers between devices, reduce_packed(): lax.psum_scatter(stacked, 'outer', scatter_dimension=0, tiled=True)  242 us
    all_gather x4, waiting for transfers between devices, gather_weight(): across = lax.all_gather(mine, 'shard', axis=0, tiled=False)  201 us
    dot_general x52, matrix products, contract_cols(): lax.dot_general(left_side, right_side, (((1,), (1,)), ((), ())), preferre...  143 us
    all_gather x2, waiting for transfers between devices, reduce_packed(): stacked = lax.all_gather(stacked, 'outer', axis=0, tiled=True)  143 us
    dot_general x36, matrix products, contract_rows(): lax.dot_general(left_side, right_side, (((0,), (0,)), ((), ())), preferre...  80.5 us
    add x5, other arithmetic, nesterov(): average_new = AVERAGING * average_old + (1.0 - AVERAGING) * weight_new  64.6 us
    reduce_scatter x2, waiting for transfers between devices, reduce_packed(): lax.psum_scatter(stacked, 'shard', scatter_dimension=0, tiled=True)  38.4 us
    ppermute x2, waiting for transfers between devices, passed_along(): lax.ppermute(value, axis, [(source, source + steps) for source in range(l...  38.1 us
  transfers between devices with their start and end apart: 20, of which 14 were waited for; matrix products, arithmetic and copies ran while one was open for 20% of the time, Pallas kernels for 0%

profile of v2, /device:TPU:9, one launch (start us, length us, event | category | flops | bytes accessed | tf_op | source)
XLA Modules:
  0.0 1366.1 jit_solution(15592184018462649303)
XLA Ops:
  16.7 39.9 %all-gather.28.cloned.1.call-done = bf16[512,3072]{1,0:T(8,128)(2,1)} async-done(((bf16[256,3072]{1,0:T(8,128)(2,1)}), bf16[512,3072]{1,0:T(8,128)(2,1)}) %all-gather.28.cloned.1.call-update) | async-done | bytes 3145744 | tf_op jit(solution)/shard_map/all_gather | solution.py:30
  56.6 23.4 %all-gather.32.cloned.1.call-done = bf16[512,1024]{1,0:T(8,128)(2,1)} async-done(((bf16[256,1024]{1,0:T(8,128)(2,1)}), bf16[512,1024]{1,0:T(8,128)(2,1)}) %all-gather.32.cloned.1.call-update) | async-done | bytes 1048592 | tf_op jit(solution)/shard_map/all_gather | solution.py:30
  84.0 54.9 %all-gather.36.cloned.1.call-done = bf16[2048,1024]{1,0:T(8,128)(2,1)} async-done(((bf16[1024,1024]{1,0:T(8,128)(2,1)}), bf16[2048,1024]{1,0:T(8,128)(2,1)}) %all-gather.36.cloned.1.call-update) | async-done | bytes 4194320 | tf_op jit(solution)/shard_map/all_gather | solution.py:30
  147.0 10.9 all-gather.30.cloned.1.call-done
  180.3 82.5 %all-gather.40.cloned.1.call-done = bf16[2048,1024]{1,0:T(8,128)(2,1)} async-done(((bf16[1024,1024]{1,0:T(8,128)(2,1)}), bf16[2048,1024]{1,0:T(8,128)(2,1)}) %all-gather.40.cloned.1.call-update) | async-done | bytes 4194320 | tf_op jit(solution)/shard_map/all_gather | solution.py:30
  293.2 87.0 %while.32 = (s32[]{:T(128)}, bf16[16,512,64]{1,2,0:T(8,128)(2,1)S(1)}, f32[16,512]{1,0:T(8,128)S(1)}, bf16[16,512,64]{2,1,0:T(8,128)(2,1)}, bf16[16,1024,64]{2,1...) while((s32[]{:T(128)}, ...), condition=%wide.region_5.6_spmd.clone.clone.clone, body=%wide.region_2.5_spmd.clone.clone.sunk.clone | while | flops 141557248 | bytes 7108221 | solution.py:225
  385.3 11.4 copy.163
  415.3 14.2 %fusion.77 = bf16[4096,1024]{1,0:T(8,128)(2,1)} fusion(f32[512,1024]{1,0:T(8,128)} %param.23, f32[512]{0:T(512)S(1)} %compare_convert_fusion, f32[512,4096]{1,0:T(8,128)} %fusion.80, f32[4096]{0:T(1024)S(1)} %bitcast.331), kind=kOutput, calls=%fused_computation.179 | convolution fusion | flops 4316987392 | bytes 18892800 | tf_op jit(solution)/shard_map/dot_general | solution.py:115
  429.5 14.1 %fusion.89 = (bf16[4096]{0:T(1024)(128)(2,1)S(1)}, bf16[512,4096]{1,0:T(8,128)(2,1)}) fusion(f32[512,4096]{1,0:T(8,128)} %fusion.80, f32[4096]{0:T(1024)S(1)} %bitcast.332, bf16[4096,1024]{1,0:T(8,128)(2,1)S(1)} %bitcast.279, f32[512,1024]{1,0:T(8,128)} %param.23, f32[512]{0:T(512)S(1)} %compare_convert_fusion), kind=kOutput, calls=%fused_computation.189 | convolution fusion | flops 4342149120 | bytes 23095296 | tf_op jit(solution)/shard_map/dot_general | solution.py:121
  466.0 163.7 %while.33 = (s32[]{:T(128)}, f32[16,512,64]{1,2,0:T(8,128)}, f32[16,1024,64]{1,2,0:T(8,128)}, f32[16,1024,64]{1,2,0:T(8,128)}, bf16[16,512,64]{2,1,0:T(8,128)(2,...) while((s32[]{:T(128)}, f32[16,512,64]{1,2,0:T(8,128)}, ...), condition=%wide.region_12.13_spmd.clone.clone.clone, body=%wide.region_10.12_spmd.clone.clone.sunk.clone | while | flops 343506432 | bytes 17586836 | solution.py:272
  646.3 38.1 %collective-permute-done.1 = bf16[512,2048]{0,1:T(8,128)(2,1)} collective-permute-done((bf16[512,2048]{0,1:T(8,128)(2,1)}, bf16[512,2048]{0,1:T(8,128)(2,1)}, u32[]{:S(2)}, u32[]{:S(2)}) %collective-permute-start.1) | collective-permute-done | bytes 2097184 | tf_op jit(solution)/shard_map/ppermute | solution.py:22
  741.7 13.5 concatenate.84
  774.5 22.5 %reduce-scatter.13.cloned.1.call-done = bf16[1,4096,1024]{2,1,0:T(8,128)(2,1)} async-done(((bf16[2,4096,1024]{2,1,0:T(8,128)(2,1)}), bf16[1,4096,1024]{2,1,0:T(8,128)(2,1)}) %reduce-scatter.13.cloned.1.call-update) | async-done | bytes 8388624 | tf_op jit(solution)/shard_map/reduce_scatter | solution.py:85
  797.1 94.8 %reduce-scatter.9.cloned.1.call-done = bf16[1,258,1024]{2,1,0:T(8,128)(2,1)} async-done(((bf16[8,258,1024]{2,1,0:T(8,128)(2,1)}), bf16[1,258,1024]{2,1,0:T(8,128)(2,1)}) %reduce-scatter.9.cloned.1.call-update) | async-done | bytes 528400 | tf_op jit(solution)/shard_map/reduce_scatter | solution.py:87
  894.0 147.4 %reduce-scatter.15.cloned.1.call-done = bf16[1,512,1024]{2,1,0:T(8,128)(2,1)} async-done(((bf16[8,512,1024]{2,1,0:T(8,128)(2,1)}), bf16[1,512,1024]{2,1,0:T(8,128)(2,1)}) %reduce-scatter.15.cloned.1.call-update) | async-done | bytes 1048592 | tf_op jit(solution)/shard_map/reduce_scatter | solution.py:87
  1041.4 18.1 %reduce-scatter.11.cloned.1.call-done = bf16[1,129,1024]{2,1,0:T(8,128)(2,1)} async-done(((bf16[2,129,1024]{2,1,0:T(8,128)(2,1)}), bf16[1,129,1024]{2,1,0:T(8,128)(2,1)}) %reduce-scatter.11.cloned.1.call-update) | async-done | bytes 264208 | tf_op jit(solution)/shard_map/reduce_scatter | solution.py:89
  1061.8 20.3 %reduce-scatter.17.cloned.1.call-done = bf16[1,256,1024]{2,1,0:T(8,128)(2,1)} async-done(((bf16[2,256,1024]{2,1,0:T(8,128)(2,1)}), bf16[1,256,1024]{2,1,0:T(8,128)(2,1)}) %reduce-scatter.17.cloned.1.call-update) | async-done | bytes 524304 | tf_op jit(solution)/shard_map/reduce_scatter | solution.py:89
  1082.3 73.7 %all-gather.44.cloned.1.call-done = bf16[1,1032,1024]{2,0,1:T(2,128)(2,1)} async-done(((bf16[1,129,1024]{2,0,1:T(2,128)(2,1)}), bf16[1,1032,1024]{2,0,1:T(2,128)(2,1)}) %all-gather.44.cloned.1.call-update) | async-done | bytes 2113552 | tf_op jit(solution)/shard_map/all_gather | solution.py:91
  1160.4 68.9 %all-gather.48.cloned.1.call-done = bf16[1,2048,1024]{2,1,0:T(8,128)(2,1)} async-done(((bf16[1,256,1024]{2,1,0:T(8,128)(2,1)}), bf16[1,2048,1024]{2,1,0:T(8,128)(2,1)}) %all-gather.48.cloned.1.call-update) | async-done | bytes 4194320 | tf_op jit(solution)/shard_map/all_gather | solution.py:91
  1229.4 12.6 add_add_fusion
  1280.4 12.1 multiply_add_fusion.3
  1292.4 11.8 fusion.84
  1314.1 22.3 %multiply_add_fusion.1 = (f32[1024,2048]{1,0:T(8,128)}, f32[1024,2048]{1,0:T(8,128)}, f32[1024,2048]{1,0:T(8,128)}) fusion(f32[1024,2048]{1,0:T(8,128)} %param.33, f32[1024,2048]{1,0:T(8,128)} %param.31, f32[1024,2048]{1,0:T(8,128)} %reshape_reshape.18, f32[1024,2048]{1,0:T(8,128)} %param.32), kind=kLoop, calls=%fused_computation.75 | loop fusion | flops 18874368 | bytes 58720256 | tf_op jit(solution)/shard_map/add | solution.py:151
  1336.4 22.6 %multiply_add_fusion = (f32[2048,1024]{1,0:T(8,128)}, f32[2048,1024]{1,0:T(8,128)}, f32[2048,1024]{1,0:T(8,128)}) fusion(f32[2048,1024]{1,0:T(8,128)} %param.36, f32[2048,1024]{1,0:T(8,128)} %param.34, f32[16,128,1024]{2,1,0:T(8,128)} %get-tuple-element.458, f32[2048,1024]{1,0:T(8,128)} %param.35), kind=kLoop, calls=%fused_computation.74 | loop fusion | flops 18874368 | bytes 58720256 | tf_op jit(solution)/shard_map/add | solution.py:151
  (477 shorter events, 520.0 us)
Async XLA Ops:
  7.2 49.4 %all-gather.28.cloned.1.call-start = ((), (), s32[]{:S(2)}) async-start(), calls=%async_computation.12 | async-start | bytes 4718592 | tf_op jit(solution)/shard_map/all_gather | solution.py:30
  10.5 69.5 %all-gather.32.cloned.1.call-start = ((), (), s32[]{:S(2)}) async-start(), calls=%async_computation.14 | async-start | bytes 1572864 | tf_op jit(solution)/shard_map/all_gather | solution.py:30
  12.7 126.2 %all-gather.36.cloned.1.call-start = ((), (), s32[]{:S(2)}) async-start(), calls=%async_computation.16 | async-start | bytes 6291456 | tf_op jit(solution)/shard_map/all_gather | solution.py:30
  16.6 141.3 %all-gather.30.cloned.1.call-start = ((), (), s32[]{:S(2)}) async-start(), calls=%async_computation.13 | async-start | bytes 9437184 | tf_op jit(solution)/shard_map/all_gather | solution.py:31
  56.6 120.6 %all-gather.34.cloned.1.call-start = ((), (), s32[]{:S(2)}) async-start(), calls=%async_computation.15 | async-start | bytes 3145728 | tf_op jit(solution)/shard_map/all_gather | solution.py:31
  80.0 182.7 %all-gather.40.cloned.1.call-start = ((), (), s32[]{:S(2)}) async-start(), calls=%async_computation.18 | async-start | bytes 6291456 | tf_op jit(solution)/shard_map/all_gather | solution.py:30
  83.9 62.5 %copy-start.1 = (f32[512,1024]{1,0:T(8,128)S(1)}, f32[512,1024]{1,0:T(8,128)}, u32[]{:S(2)}) copy-start(f32[512,1024]{1,0:T(8,128)} %param.22) | copy-start | bytes 6291460
  83.9 301.4 %all-gather.38.cloned.1.call-start = ((), (), s32[]{:S(2)}) async-start(), calls=%async_computation.17 | async-start | bytes 12582912 | tf_op jit(solution)/shard_map/all_gather | solution.py:31
  138.9 257.8 %all-gather.42.cloned.1.call-start = ((), (), s32[]{:S(2)}) async-start(), calls=%async_computation.19 | async-start | bytes 12582912 | tf_op jit(solution)/shard_map/all_gather | solution.py:31
  169.0 99.2 %collective-permute-start = (bf16[512,2048]{1,0:T(8,128)(2,1)}, bf16[512,2048]{1,0:T(8,128)(2,1)}, u32[]{:S(2)}, u32[]{:S(2)}) collective-permute-start(bf16[512,2048]{1,0:T(8,128)(2,1)} %pad_maximum_fusion.1), channel_id=1, source_target_pairs={{0,1},{2,3},{4,5},{6,7},{8,9},{10,11},{12,13},{14,15},{16,17},{18,... | collective-permute-start | bytes 6291464 | tf_op jit(solution)/shard_map/ppermute | solution.py:22
  262.8 507.5 %reduce-scatter.7.cloned.1.call-start = ((), (), s32[]{:S(2)}) async-start(), calls=%async_computation.6 | async-start | bytes 12681216 | tf_op jit(solution)/shard_map/reduce_scatter | solution.py:85
  634.8 49.6 %collective-permute-start.1 = (bf16[512,2048]{0,1:T(8,128)(2,1)}, bf16[512,2048]{0,1:T(8,128)(2,1)}, u32[]{:S(2)}, u32[]{:S(2)}) collective-permute-start(bf16[512,2048]{0,1:T(8,128)(2,1)} %pad_maximum_fusion.4), channel_id=1, source_target_pairs={{1,0},{3,2},{5,4},{7,6},{9,8},{11,10},{13,12},{15,14},{17,16},{19,... | collective-permute-start | bytes 6291464 | tf_op jit(solution)/shard_map/ppermute | solution.py:22
  646.3 40.5 %copy-start.10 = (f32[512,16,64]{0,2,1:T(8,128)S(1)}, f32[512,16,64]{0,2,1:T(8,128)}, u32[]{:S(2)}) copy-start(f32[512,16,64]{0,2,1:T(8,128)} %slice.151) | copy-start | bytes 6291460
  733.1 63.9 %reduce-scatter.13.cloned.1.call-start = ((), (), s32[]{:S(2)}) async-start(), calls=%async_computation.9 | async-start | bytes 25165824 | tf_op jit(solution)/shard_map/reduce_scatter | solution.py:85
  770.2 121.8 %reduce-scatter.9.cloned.1.call-start = ((), (), s32[]{:S(2)}) async-start(), calls=%async_computation.7 | async-start | bytes 4866048 | tf_op jit(solution)/shard_map/reduce_scatter | solution.py:87
  774.5 266.9 %reduce-scatter.15.cloned.1.call-start = ((), (), s32[]{:S(2)}) async-start(), calls=%async_computation.10 | async-start | bytes 9437184 | tf_op jit(solution)/shard_map/reduce_scatter | solution.py:87
  797.1 262.4 %reduce-scatter.11.cloned.1.call-start = ((), (), s32[]{:S(2)}) async-start(), calls=%async_computation.8 | async-start | bytes 835584 | tf_op jit(solution)/shard_map/reduce_scatter | solution.py:89
  893.9 188.1 %reduce-scatter.17.cloned.1.call-start = ((), (), s32[]{:S(2)}) async-start(), calls=%async_computation.11 | async-start | bytes 1572864 | tf_op jit(solution)/shard_map/reduce_scatter | solution.py:89
  1041.4 114.6 %all-gather.44.cloned.1.call-start = ((), (), s32[]{:S(2)}) async-start(), calls=%async_computation.20 | async-start | bytes 4755456 | tf_op jit(solution)/shard_map/all_gather | solution.py:91
  1061.7 167.6 %all-gather.48.cloned.1.call-start = ((), (), s32[]{:S(2)}) async-start(), calls=%async_computation.22 | async-start | bytes 4718592 | tf_op jit(solution)/shard_map/all_gather | solution.py:91
  1082.1 164.2 %all-gather.46.cloned.1.call-start = ((), (), s32[]{:S(2)}) async-start(), calls=%async_computation.21 | async-start | bytes 6340608 | tf_op jit(solution)/shard_map/all_gather | solution.py:92
  1160.3 69.0 %copy-start.27 = (f32[2,2,2,128]{3,2,1,0:T(2,128)S(1)}, f32[2,2,2,128]{3,2,1,0:T(2,128)}, u32[]{:S(2)}) copy-start(f32[2,2,2,128]{3,2,1,0:T(2,128)} %get-tuple-element.485) | copy-start | bytes 12292
  1160.3 69.1 %copy-start.8 = (f32[512,1024]{1,0:T(8,128)S(1)}, f32[512,1024]{1,0:T(8,128)}, u32[]{:S(2)}) copy-start(f32[512,1024]{1,0:T(8,128)} %copy-done.6) | copy-start | bytes 6291460
  1160.3 132.1 %all-gather.50.cloned.1.call-start = ((), (), s32[]{:S(2)}) async-start(), calls=%async_computation.23 | async-start | bytes 12582912 | tf_op jit(solution)/shard_map/all_gather | solution.py:92
  (37 other events, 287.7 us)
Sparse Core Ops, SparseCore 0:
  10.6 45.8 all-gather.27
  58.7 21.2 all-gather.31
  82.1 56.7 all-gather.35
  140.3 17.6 all-gather.29
  159.4 11.7 all-gather.33
  173.1 89.5 all-gather.39
  264.3 22.4 all-gather.37
  288.3 21.0 all-gather.41
  733.3 17.6 reduce-scatter.6
  770.3 26.7 reduce-scatter.12
  801.2 90.6 reduce-scatter.8
  895.4 145.8 reduce-scatter.14
  1044.2 15.3 reduce-scatter.10
  1061.6 20.3 reduce-scatter.16
  1084.6 71.2 all-gather.43
  1157.9 71.3 all-gather.47
  1231.3 14.9 all-gather.45
  1247.7 21.0 all-gather.49

commit v3 on v2

--- a/solution.py
+++ b/solution.py
@@ -22,21 +22,42 @@
     return lax.ppermute(value, axis, [(source, source + steps) for source in range(leading, last)])
 
 
-def gather_weight(weight_own, dim):
-    low_own = weight_own.astype(jnp.bfloat16)
+LANE = 1024
+
+
+def to_blocks(half, blocks):
+    flat = half.reshape(-1)
+    size = flat.shape[0]
+    padded = -(-size // (blocks * LANE)) * blocks * LANE
+    if padded != size:
+        flat = jnp.pad(flat, (0, padded - size))
+    return flat.reshape(blocks, -1, LANE)
+
+
+def gather_weights(halves):
     cores = lax.axis_size("core")
-    quarter = low_own.shape[dim] // cores
-    mine = lax.dynamic_slice_in_dim(low_own, lax.axis_index("core") * quarter, quarter, axis=dim)
-    across = lax.all_gather(mine, "shard", axis=0, tiled=False)
-    both = lax.all_gather(across, "core", axis=0, tiled=False)
-    if dim == 0:
-        ordered = both.transpose(1, 0, 2, 3)
-        return ordered.reshape(-1, ordered.shape[-1])
-    ordered = both.transpose(2, 1, 0, 3)
-    return ordered.reshape(ordered.shape[0], -1)
-
-
-LANE = 1024
+    outer = lax.axis_size("outer")
+    blocks = cores * outer
+    lows = [half.astype(jnp.bfloat16) for half, unused in halves]
+    packed = [to_blocks(low, blocks) for low in lows]
+    widths = [piece.shape[1] for piece in packed]
+    own = jnp.concatenate(packed, axis=1)
+    place = lax.axis_index("core") * outer + lax.axis_index("outer")
+    mine = lax.dynamic_index_in_dim(own, place, 0, keepdims=False)
+    other = lax.ppermute(mine, "shard", [(0, 1), (1, 0)])
+    got = lax.all_gather(other, "outer", axis=0, tiled=False)
+    got = lax.all_gather(got, "core", axis=0, tiled=False)
+    got = got.reshape(blocks, -1, LANE)
+    upper = lax.axis_index("shard") == 1
+    fulls = []
+    offset = 0
+    for (half, dim), low, width in zip(halves, lows, widths):
+        other_half = got[:, offset : offset + width].reshape(-1)[: low.size].reshape(low.shape)
+        offset += width
+        in_order = jnp.concatenate([low, other_half], axis=dim)
+        swapped = jnp.concatenate([other_half, low], axis=dim)
+        fulls.append(jnp.where(upper, swapped, in_order))
+    return fulls
 
 
 def pack_halves(grad_full, dim, blocks):
@@ -192,11 +213,10 @@
     head_size = model_width // HEADS
     score_scale = head_size ** (-0.5)
     slopes = 2.0 ** (-8.0 * (jnp.arange(HEADS, dtype=jnp.float32) + 1.0) / HEADS)
-    qkv_full = gather_weight(qkv_weight, 0)
-    out_full = gather_weight(out_weight, 0)
-    small_full = gather_weight(small_params, 1)
-    up_full = gather_weight(up_weight, 1)
-    down_full = gather_weight(down_weight, 0)
+    qkv_full, small_full = gather_weights([(qkv_weight, 0), (small_params, 1)])
+    out_full, up_full, down_full = gather_weights(
+        [(out_weight, 0), (up_weight, 1), (down_weight, 0)]
+    )
     table = small_full.astype(jnp.float32)
     up_bias = table[8:12].reshape(FF)
     normed_one, inverse_one = norm_stats(tokens)
@@ -246,11 +266,13 @@
     gain_two_grad = jnp.sum(grad_inner * normed_two, axis=0)
     shift_two_grad = jnp.sum(grad_inner, axis=0)
     grad_resid = grad_out + norm_back(grad_inner * table[5], normed_two, inverse_two)
-    grad_resid, up_grad, down_grad = lax.optimization_barrier((grad_resid, up_grad, down_grad))
-    up_total, down_total = reduce_grads([(up_grad, 1), (down_grad, 0)])
-    out_bias_grad = jnp.sum(grad_resid, axis=0)
     resid_low = grad_resid.astype(jnp.bfloat16)
     out_grad = contract_rows(attended_low, resid_low)
+    grad_resid, resid_low, up_grad, down_grad, out_grad = lax.optimization_barrier(
+        (grad_resid, resid_low, up_grad, down_grad, out_grad)
+    )
+    up_total, down_total, out_total = reduce_grads([(up_grad, 1), (down_grad, 0), (out_grad, 0)])
+    out_bias_grad = jnp.sum(grad_resid, axis=0)
     grad_mixture = contract_cols(resid_low, out_full).astype(jnp.bfloat16)
     grad_heads = split_heads(grad_mixture)
 
@@ -269,8 +291,26 @@
         grad_keys = contract_rows(grad_scores, head_query) * score_scale
         return (grad_query, grad_keys, grad_values)
 
-    query_grads, key_grads, value_grads = lax.map(
-        head_backward, (query_heads, key_heads, value_heads, grad_heads, log_total, slopes)
+    groups = 4
+    per_group = HEADS // groups
+    parts = []
+    for group in range(groups):
+        chosen = slice(group * per_group, (group + 1) * per_group)
+        parts.append(
+            lax.map(
+                head_backward,
+                (
+                    query_heads[chosen],
+                    key_heads[chosen],
+                    value_heads[chosen],
+                    grad_heads[chosen],
+                    log_total[chosen],
+                    slopes[chosen],
+                ),
+            )
+        )
+    query_grads, key_grads, value_grads = (
+        jnp.concatenate([part[index] for part in parts], 0) for index in range(3)
     )
     grad_query = merge_heads(query_grads)
     grad_keys = merge_heads(key_grads)
@@ -303,7 +343,7 @@
         ]
     )
     small_grad = jnp.concatenate([head_rows, up_bias_grad.reshape(4, model_width)], 0)
-    qkv_total, out_total, small_total = reduce_grads([(qkv_grad, 0), (out_grad, 0), (small_grad, 1)])
+    qkv_total, small_total = reduce_grads([(qkv_grad, 0), (small_grad, 1)])
     rate = 2.0 / math.sqrt(model_width * tok_rows * shard_count * group_count)
     qkv_new = nesterov(qkv_total, qkv_weight, qkv_momentum, qkv_average, rate)
     out_new = nesterov(out_total, out_weight, out_momentum, out_average, rate)

time: 1380 us -> 1300 us (0.942)
  waiting for transfers between devices: 700 us -> 587 us
  other arithmetic: 116 us -> 143 us
    all_gather x8 -> x4, waiting for transfers between devices: 212 us -> 46.2 us  [the longest x2 46.2 us: gather_weights(): got = lax.all_gather(other, 'outer', axis=0, tiled=False)]
    ppermute x2, waiting for transfers between devices: 38.1 us -> 75.9 us  [passed_along(): lax.ppermute(value, axis, [(source, source + steps) for source in range(l...]
    another operation x0 -> x16, local copies, waits for them, and re-layouts: none -> 29.5 us  [the longest x2 13 us: gather_weights(): got[:, offset:offset + width].reshape(-1)[:low.size].reshape(low.shape)]
    transpose x4 -> x0, local copies, waits for them, and re-layouts: 25.6 us -> none  [the longest x3 14.2 us: gather_weight(): ordered = both.transpose(1, 0, 2, 3)]
    slice x2 -> x12, local copies, waits for them, and re-layouts: 0.01 us -> 22.5 us  [the longest x6 13.5 us: gather_weights(): got[:, offset:offset + width].reshape(-1)[:low.size].reshape(low.shape)]
    convert_element_type x0 -> x7, other arithmetic: none -> 17.7 us  [the longest x5 15.2 us: gather_weights(): lows = [half.astype(jnp.bfloat16) for half, unused in halves]]
    ppermute x0 -> x2, waiting for transfers between devices: none -> 16 us  [gather_weights(): other = lax.ppermute(mine, 'shard', [(0, 1), (1, 0)])]
    dynamic_slice x16 -> x32, local copies, waits for them, and re-layouts: 0.1 us -> 14.9 us  [body(): lax.map(head_backward, (query_heads[chosen], key_heads[chosen], value_hea...]
  transfers between devices with their start and end apart: 20 -> 18, of which waited for: 14 -> 13; matrix products, arithmetic and copies ran while one was open for 20% -> 20% of each run, Pallas kernels for 0% -> 0%
where the time goes in v3:
time: 1300 us; the launch traced here: 1280 us
  waiting for transfers between devices  587 us (45%)
  matrix products  304 us (23%)
  local copies, waits for them, and re-layouts  218 us (17%)
  other arithmetic  143 us (11%)
  between operations  15.1 us (1%)
    reduce_scatter x2, waiting for transfers between devices, reduce_packed(): lax.psum_scatter(stacked, 'outer', scatter_dimension=0, tiled=True)  242 us
    dot_general x52, matrix products, contract_cols(): lax.dot_general(left_side, right_side, (((1,), (1,)), ((), ())), preferre...  150 us
    all_gather x2, waiting for transfers between devices, reduce_packed(): stacked = lax.all_gather(stacked, 'outer', axis=0, tiled=True)  137 us
    ppermute x2, waiting for transfers between devices, passed_along(): lax.ppermute(value, axis, [(source, source + steps) for source in range(l...  75.9 us
    dot_general x36, matrix products, contract_rows(): lax.dot_general(left_side, right_side, (((0,), (0,)), ((), ())), preferre...  69.3 us
    add x5, other arithmetic, nesterov(): average_new = AVERAGING * average_old + (1.0 - AVERAGING) * weight_new  68.1 us
    all_gather x2, waiting for transfers between devices, gather_weights(): got = lax.all_gather(other, 'outer', axis=0, tiled=False)  46.2 us
    reduce_scatter x2, waiting for transfers between devices, reduce_packed(): lax.psum_scatter(stacked, 'shard', scatter_dimension=0, tiled=True)  38.6 us
  transfers between devices with their start and end apart: 18, of which 13 were waited for; matrix products, arithmetic and copies ran while one was open for 20% of the time, Pallas kernels for 0%

profile of v3, /device:TPU:9, one launch (start us, length us, event | category | flops | bytes accessed | tf_op | source)
XLA Modules:
  0.0 1277.7 jit_solution(3721418647545551526)
XLA Ops:
  24.2 46.2 %all-gather.32.cloned.1.call-done = bf16[8,97,1024]{2,1,0:T(8,128)(2,1)} async-done(((bf16[1,97,1024]{2,1,0:T(8,128)(2,1)}), bf16[8,97,1024]{2,1,0:T(8,128)(2,1)}) %all-gather.32.cloned.1.call-update) | async-done | bytes 1589264 | tf_op jit(solution)/shard_map/all_gather | solution.py:48
  142.3 33.3 %collective-permute-done.1 = bf16[512,2048]{1,0:T(8,128)(2,1)} collective-permute-done((bf16[512,2048]{1,0:T(8,128)(2,1)}, bf16[512,2048]{1,0:T(8,128)(2,1)}, u32[]{:S(2)}, u32[]{:S(2)}) %collective-permute-start.1) | collective-permute-done | bytes 2097184 | tf_op jit(solution)/shard_map/ppermute | solution.py:22
  188.8 84.6 %while.78 = (s32[]{:T(128)}, bf16[16,512,64]{1,2,0:T(8,128)(2,1)S(1)}, f32[16,512]{1,0:T(8,128)S(1)}, bf16[16,512,64]{1,2,0:T(8,128)(2,1)}, bf16[16,1024,64]{1,2...) while((s32[]{:T(128)}, ...), condition=%wide.region_5.6_spmd.clone.clone, body=%wide.region_2.5_spmd.clone.clone.sunk | while | flops 141557248 | bytes 6780557 | solution.py:245
  296.9 13.2 %fusion.171 = f32[512,4096]{1,0:T(8,128)} fusion(bf16[1024,2048]{1,0:T(8,128)(2,1)S(1)} %copy-done.2, bf16[1024,2048]{1,0:T(8,128)(2,1)} %reshape_reshape.46, pred[]{:T(512)S(6)} %eq.9, f32[512,1024]{1,0:T(8,128)S(1)} %get-tuple-element.1204, f32[1024]{0:T(1024)S(1)} %bitcast.493, f32[1024]{0:T(1024)S(1)} %bitcast.481, f32[512]{0:T(512)S(1)} %add_rsqrt_fusion, ...), kind=kOutput, calls=%fused_computation.256 | convolution fusion | flops 4335337472 | bytes 18886656 | tf_op jit(solution)/shard_map/dot_general | solution.py:255
  310.1 13.5 %fusion.193 = bf16[4096,1024]{1,0:T(8,128)(2,1)} fusion(f32[512,1024]{1,0:T(8,128)S(1)} %copy-done.26, f32[512]{0:T(512)S(1)} %compare_convert_fusion, f32[512,4096]{1,0:T(8,128)} %fusion.171, f32[4096]{0:T(1024)S(1)} %bitcast.487), kind=kOutput, calls=%fused_computation.308 | convolution fusion | flops 4316987392 | bytes 18892800 | tf_op jit(solution)/shard_map/dot_general | solution.py:136
  323.6 21.6 %fusion.210 = (bf16[4096]{0:T(1024)(128)(2,1)}, bf16[512,4096]{1,0:T(8,128)(2,1)}) fusion(f32[512,4096]{1,0:T(8,128)} %fusion.171, f32[4096]{0:T(1024)S(1)} %bitcast.488, bf16[2048,1024]{1,0:T(8,128)(2,1)} %convert_element_type.129, bf16[2048,1024]{1,0:T(8,128)(2,1)} %bitcast.460, pred[]{:T(512)S(6)} %eq.9, f32[512,1024]{1,0:T(8,128)} %param.29, ...), kind=kOutput, calls=%fused_computation.323 | convolution fusion | flops 4379897856 | bytes 23095296 | tf_op jit(solution)/shard_map/dot_general | solution.py:142
  372.4 35.3 %while.79 = (s32[]{:T(128)}, f32[4,512,64]{1,2,0:T(8,128)S(1)}, f32[4,1024,64]{1,2,0:T(8,128)S(1)}, f32[4,1024,64]{1,2,0:T(8,128)S(1)}, bf16[4,512,64]{1,2,0:T(8...) while((s32[]{:T(128)}, f32[4,512,64]{1,2,0:T(8,128)S(1)}, ...), condition=%wide.region_12.13_spmd.clone.clone, body=%wide.region_10.12_spmd.clone.clone.sunk | while | flops 343506432 | bytes 17062556 | solution.py:300
  410.9 37.3 %while.82 = (s32[]{:T(128)}, f32[4,512,64]{1,2,0:T(8,128)S(1)}, f32[4,1024,64]{1,2,0:T(8,128)}, f32[4,1024,64]{1,2,0:T(8,128)}, bf16[4,512,64]{1,2,0:T(8,128)(2,...) while((s32[]{:T(128)}, f32[4,512,64]{1,2,0:T(8,128)S(1)}, ...), condition=%wide.region_21.22_spmd.clone.clone, body=%wide.region_19.21_spmd.clone.clone.sunk | while | flops 343506432 | bytes 17062556 | solution.py:300
  449.5 37.3 %while.81 = (s32[]{:T(128)}, f32[4,512,64]{1,2,0:T(8,128)S(1)}, f32[4,1024,64]{1,2,0:T(8,128)}, f32[4,1024,64]{1,2,0:T(8,128)S(1)}, bf16[4,512,64]{1,2,0:T(8,128...) while((s32[]{:T(128)}, f32[4,512,64]{1,2,0:T(8,128)S(1)}, ...), condition=%wide.region_18.19_spmd.clone.clone, body=%wide.region_16.18_spmd.clone.clone.sunk | while | flops 343506432 | bytes 17062556 | solution.py:300
  489.0 36.9 %while.80 = (s32[]{:T(128)}, f32[4,512,64]{1,2,0:T(8,128)S(1)}, f32[4,1024,64]{1,2,0:T(8,128)}, f32[4,1024,64]{1,2,0:T(8,128)S(1)}, bf16[4,512,64]{1,2,0:T(8,128...) while((s32[]{:T(128)}, f32[4,512,64]{1,2,0:T(8,128)S(1)}, ...), condition=%wide.region_15.16_spmd.clone.clone, body=%wide.region_13.15_spmd.clone.clone.sunk | while | flops 343506432 | bytes 17062556 | solution.py:300
  534.4 42.7 %collective-permute-done.3 = bf16[512,2048]{0,1:T(8,128)(2,1)} collective-permute-done((bf16[512,2048]{0,1:T(8,128)(2,1)}, bf16[512,2048]{0,1:T(8,128)(2,1)}, u32[]{:S(2)}, u32[]{:S(2)}) %collective-permute-start.3) | collective-permute-done | bytes 2097184 | tf_op jit(solution)/shard_map/ppermute | solution.py:22
  625.8 13.3 %pad_maximum_fusion = bf16[2,2,8,97,1024]{4,1,3,0,2:T(2,128)(2,1)S(1)} fusion(bf16[2,2,8,1,1024]{4,1,3,0,2:T(2,128)(2,1)S(1)} %copy.187, bf16[2,2,8,96,1024]{4,1,3,0,2:T(2,128)(2,1)S(1)} %copy.186), kind=kLoop, calls=%fused_computation.200 | loop fusion | flops 3178496 | bytes 12713984 | tf_op jit(solution)/shard_map/concatenate | solution.py:103
  652.4 13.6 %concatenate.146 = bf16[2,2,8,128,1024]{4,3,2,1,0:T(8,128)(2,1)} reshape(bf16[2,1024,2048]{2,1,0:T(8,128)(2,1)} %bitcast.445) | data formatting | bytes 16777216 | tf_op jit(solution)/shard_map/concatenate | solution.py:103
  684.7 30.5 %reduce-scatter.13.cloned.1.call-done = bf16[1,4608,1024]{2,1,0:T(8,128)(2,1)} async-done(((bf16[2,4608,1024]{2,1,0:T(8,128)(2,1)}), bf16[1,4608,1024]{2,1,0:T(8,128)(2,1)}) %reduce-scatter.13.cloned.1.call-update) | async-done | bytes 9437200 | tf_op jit(solution)/shard_map/reduce_scatter | solution.py:106
  715.3 79.8 %reduce-scatter.9.cloned.1.call-done = bf16[1,194,1024]{2,1,0:T(8,128)(2,1)} async-done(((bf16[8,194,1024]{2,1,0:T(8,128)(2,1)}), bf16[1,194,1024]{2,1,0:T(8,128)(2,1)}) %reduce-scatter.9.cloned.1.call-update) | async-done | bytes 397328 | tf_op jit(solution)/shard_map/reduce_scatter | solution.py:108
  797.0 162.3 %reduce-scatter.15.cloned.1.call-done = bf16[1,576,1024]{2,1,0:T(8,128)(2,1)} async-done(((bf16[8,576,1024]{2,1,0:T(8,128)(2,1)}), bf16[1,576,1024]{2,1,0:T(8,128)(2,1)}) %reduce-scatter.15.cloned.1.call-update) | async-done | bytes 1179664 | tf_op jit(solution)/shard_map/reduce_scatter | solution.py:108
  959.4 16.7 %reduce-scatter.11.cloned.1.call-done = bf16[1,97,1024]{2,1,0:T(8,128)(2,1)} async-done(((bf16[2,97,1024]{2,1,0:T(8,128)(2,1)}), bf16[1,97,1024]{2,1,0:T(8,128)(2,1)}) %reduce-scatter.11.cloned.1.call-update) | async-done | bytes 198672 | tf_op jit(solution)/shard_map/reduce_scatter | solution.py:110
  978.2 21.9 %reduce-scatter.17.cloned.1.call-done = bf16[1,288,1024]{2,1,0:T(8,128)(2,1)} async-done(((bf16[2,288,1024]{2,1,0:T(8,128)(2,1)}), bf16[1,288,1024]{2,1,0:T(8,128)(2,1)}) %reduce-scatter.17.cloned.1.call-update) | async-done | bytes 589840 | tf_op jit(solution)/shard_map/reduce_scatter | solution.py:110
  1000.1 61.8 %all-gather.24.cloned.1.call-done = bf16[1,776,1024]{2,0,1:T(2,128)(2,1)} async-done(((bf16[1,97,1024]{2,0,1:T(2,128)(2,1)}), bf16[1,776,1024]{2,0,1:T(2,128)(2,1)}) %all-gather.24.cloned.1.call-update) | async-done | bytes 1589264 | tf_op jit(solution)/shard_map/all_gather | solution.py:112
  1065.6 75.4 %all-gather.28.cloned.1.call-done = bf16[1,2304,1024]{2,1,0:T(8,128)(2,1)} async-done(((bf16[1,288,1024]{2,1,0:T(8,128)(2,1)}), bf16[1,2304,1024]{2,1,0:T(8,128)(2,1)}) %all-gather.28.cloned.1.call-update) | async-done | bytes 4718608 | tf_op jit(solution)/shard_map/all_gather | solution.py:112
  1141.1 15.3 %add_add_fusion = f32[512,1024]{1,0:T(8,128)} fusion(f32[512,1024]{1,0:T(8,128)S(1)} %copy-done.13, bf16[2048,1024]{1,0:T(8,128)(2,1)} %convert_element_type.129, bf16[2048,1024]{1,0:T(8,128)(2,1)} %bitcast.461, pred[]{:T(512)S(6)} %eq.9, f32[1024]{0:T(1024)S(1)} %bitcast.490, f32[512,4096]{1,0:T(8,128)} %fusion.171, f32[4096]{0:T(1024)S(1)} %bitcast.489), kind=kOutput, calls=%fused_computation.242 | convolution fusion | flops 4354736128 | bytes 20992000 | tf_op jit(solution)/shard_map/dot_general | solution.py:257
  1178.9 15.8 %multiply_add_fusion.3 = (f32[512,3072]{1,0:T(8,128)}, f32[512,3072]{1,0:T(8,128)}, f32[512,3072]{1,0:T(8,128)}) fusion(f32[512,3072]{1,0:T(8,128)} %param.33, f32[512,3072]{1,0:T(8,128)} %param.31, f32[512,3072]{1,0:T(8,128)} %reshape_reshape.48, f32[512,3072]{1,0:T(8,128)} %param.32), kind=kLoop, calls=%fused_computation.202 | loop fusion | flops 14155776 | bytes 44040192 | tf_op jit(solution)/shard_map/add | solution.py:172
  1225.9 22.5 %multiply_add_fusion.1 = (f32[1024,2048]{1,0:T(8,128)}, f32[1024,2048]{1,0:T(8,128)}, f32[1024,2048]{1,0:T(8,128)}) fusion(f32[1024,2048]{1,0:T(8,128)} %param.39, f32[1024,2048]{1,0:T(8,128)} %param.37, f32[1024,2048]{1,0:T(8,128)} %reshape_reshape.50, f32[1024,2048]{1,0:T(8,128)} %param.38), kind=kLoop, calls=%fused_computation.196 | loop fusion | flops 18874368 | bytes 58720256 | tf_op jit(solution)/shard_map/add | solution.py:172
  1248.3 22.6 %multiply_add_fusion = (f32[2048,1024]{1,0:T(8,128)}, f32[2048,1024]{1,0:T(8,128)}, f32[2048,1024]{1,0:T(8,128)}) fusion(f32[2048,1024]{1,0:T(8,128)} %param.42, f32[2048,1024]{1,0:T(8,128)} %param.40, f32[16,128,1024]{2,1,0:T(8,128)} %get-tuple-element.1157, f32[2048,1024]{1,0:T(8,128)} %param.41), kind=kLoop, calls=%fused_computation.195 | loop fusion | flops 18874368 | bytes 58720256 | tf_op jit(solution)/shard_map/add | solution.py:172
  (517 shorter events, 539.5 us)
Async XLA Ops:
  7.2 63.3 %all-gather.32.cloned.1.call-start = ((), (), s32[]{:S(2)}) async-start(), calls=%async_computation.19 | async-start | bytes 1916928 | tf_op jit(solution)/shard_map/all_gather | solution.py:48
  17.2 56.8 %copy-start.8 = (f32[512,1024]{1,0:T(8,128)S(1)}, f32[512,1024]{1,0:T(8,128)}, u32[]{:S(2)}) copy-start(f32[512,1024]{1,0:T(8,128)} %param.34) | copy-start | bytes 6291460
  17.3 6.2 collective-permute-start
  24.2 82.2 %all-gather.18.cloned.1.call-start = ((), (), s32[]{:S(2)}) async-start(), calls=%async_computation.12 | async-start | bytes 4767744 | tf_op jit(solution)/shard_map/all_gather | solution.py:49
  74.0 113.7 %all-gather.20.cloned.1.call-start = ((), (), s32[]{:S(2)}) async-start(), calls=%async_computation.13 | async-start | bytes 5308416 | tf_op jit(solution)/shard_map/all_gather | solution.py:48
  92.6 12.3 collective-permute-start.2
  105.7 172.9 %all-gather.22.cloned.1.call-start = ((), (), s32[]{:S(2)}) async-start(), calls=%async_computation.14 | async-start | bytes 14155776 | tf_op jit(solution)/shard_map/all_gather | solution.py:49
  130.7 44.9 %collective-permute-start.1 = (bf16[512,2048]{1,0:T(8,128)(2,1)}, bf16[512,2048]{1,0:T(8,128)(2,1)}, u32[]{:S(2)}, u32[]{:S(2)}) collective-permute-start(bf16[512,2048]{1,0:T(8,128)(2,1)} %pad_maximum_fusion.2), channel_id=1, source_target_pairs={{0,1},{2,3},{4,5},{6,7},{8,9},{10,11},{12,13},{14,15},{16,17},{18,... | collective-permute-start | bytes 6291464 | tf_op jit(solution)/shard_map/ppermute | solution.py:22
  137.8 185.8 %copy-start.39 = (f32[1,8,4,128]{3,1,2,0:T(8,128)}, f32[1,8,4,128]{3,1,2,0:T(8,128)S(1)}, u32[]{:S(2)}) copy-start(f32[1,8,4,128]{3,1,2,0:T(8,128)S(1)} %copy.220) | copy-start | bytes 49156
  187.7 493.4 %reduce-scatter.7.cloned.1.call-start = ((), (), s32[]{:S(2)}) async-start(), calls=%async_computation.6 | async-start | bytes 9535488 | tf_op jit(solution)/shard_map/reduce_scatter | solution.py:106
  531.8 45.2 %collective-permute-start.3 = (bf16[512,2048]{0,1:T(8,128)(2,1)}, bf16[512,2048]{0,1:T(8,128)(2,1)}, u32[]{:S(2)}, u32[]{:S(2)}) collective-permute-start(bf16[512,2048]{0,1:T(8,128)(2,1)} %pad_maximum_fusion.5), channel_id=1, source_target_pairs={{1,0},{3,2},{5,4},{7,6},{9,8},{11,10},{13,12},{15,14},{17,16},{19,... | collective-permute-start | bytes 6291464 | tf_op jit(solution)/shard_map/ppermute | solution.py:22
  534.3 44.9 %slice-start.2 = ((f32[1024,16,64]{0,2,1:T(8,128)}), f32[512,16,64]{0,2,1:T(8,128)S(1)}, s32[]{:S(2)}) async-start(f32[1024,16,64]{0,2,1:T(8,128)} %copy-done.3), calls=%async_computation.22 | async-start | bytes 4194304 | tf_op jit(solution)/shard_map/slice | solution.py:324
  643.9 71.3 %reduce-scatter.13.cloned.1.call-start = ((), (), s32[]{:S(2)}) async-start(), calls=%async_computation.9 | async-start | bytes 28311552 | tf_op jit(solution)/shard_map/reduce_scatter | solution.py:106
  681.0 114.1 %reduce-scatter.9.cloned.1.call-start = ((), (), s32[]{:S(2)}) async-start(), calls=%async_computation.7 | async-start | bytes 3686400 | tf_op jit(solution)/shard_map/reduce_scatter | solution.py:108
  684.7 274.6 %reduce-scatter.15.cloned.1.call-start = ((), (), s32[]{:S(2)}) async-start(), calls=%async_computation.10 | async-start | bytes 10616832 | tf_op jit(solution)/shard_map/reduce_scatter | solution.py:108
  715.2 260.9 %reduce-scatter.11.cloned.1.call-start = ((), (), s32[]{:S(2)}) async-start(), calls=%async_computation.8 | async-start | bytes 638976 | tf_op jit(solution)/shard_map/reduce_scatter | solution.py:110
  797.0 203.1 %reduce-scatter.17.cloned.1.call-start = ((), (), s32[]{:S(2)}) async-start(), calls=%async_computation.11 | async-start | bytes 1769472 | tf_op jit(solution)/shard_map/reduce_scatter | solution.py:110
  959.3 102.6 %all-gather.24.cloned.1.call-start = ((), (), s32[]{:S(2)}) async-start(), calls=%async_computation.15 | async-start | bytes 3575808 | tf_op jit(solution)/shard_map/all_gather | solution.py:112
  978.1 162.9 %all-gather.28.cloned.1.call-start = ((), (), s32[]{:S(2)}) async-start(), calls=%async_computation.17 | async-start | bytes 5308416 | tf_op jit(solution)/shard_map/all_gather | solution.py:112
  1000.1 156.8 %all-gather.26.cloned.1.call-start = ((), (), s32[]{:S(2)}) async-start(), calls=%async_computation.16 | async-start | bytes 4767744 | tf_op jit(solution)/shard_map/all_gather | solution.py:113
  1065.6 75.5 %copy-start.13 = (f32[512,1024]{1,0:T(8,128)S(1)}, f32[512,1024]{1,0:T(8,128)}, u32[]{:S(2)}) copy-start(f32[512,1024]{1,0:T(8,128)} %copy-done.11) | copy-start | bytes 6291460
  1065.6 75.5 %copy-start.40 = (f32[1,8,4,128]{3,1,2,0:T(8,128)S(1)}, f32[1,8,4,128]{3,1,2,0:T(8,128)}, u32[]{:S(2)}) copy-start(f32[1,8,4,128]{3,1,2,0:T(8,128)} %copy-done.39) | copy-start | bytes 49156
  1065.6 75.5 %copy-start.44 = (f32[1,1024]{1,0:T(1,128)S(1)}, f32[1,1024]{1,0:T(1,128)}, u32[]{:S(2)}) copy-start(f32[1,1024]{1,0:T(1,128)} %get-tuple-element.1188) | copy-start | bytes 12292
  1065.6 129.0 %all-gather.30.cloned.1.call-start = ((), (), s32[]{:S(2)}) async-start(), calls=%async_computation.18 | async-start | bytes 14155776 | tf_op jit(solution)/shard_map/all_gather | solution.py:113
  (54 other events, 568.7 us)
Sparse Core Ops, SparseCore 0:
  24.3 46.1 all-gather.31
  74.1 12.6 all-gather.17
  105.9 78.8 all-gather.19
  187.8 27.7 all-gather.21
  644.0 20.5 reduce-scatter.6
  681.1 34.0 reduce-scatter.12
  719.4 75.7 reduce-scatter.8
  798.7 160.5 reduce-scatter.14
  962.1 13.9 reduce-scatter.10
  978.2 21.8 reduce-scatter.16
  1002.8 59.0 all-gather.23
  1064.0 77.0 all-gather.27
  1143.2 13.6 all-gather.25
  1158.3 22.7 all-gather.29

commit v4 on v3

--- a/solution.py
+++ b/solution.py
@@ -146,6 +146,10 @@
 
 def split_heads(field_in):
     return field_in.reshape(field_in.shape[0], HEADS, -1).transpose(1, 0, 2)
+
+
+def split_heads_n(field_in, heads):
+    return field_in.reshape(field_in.shape[0], heads, -1).transpose(1, 0, 2)
 
 
 def merge_heads(field_in):
@@ -225,12 +229,22 @@
     queries = (mapped[:, :model_width] + table[2]).astype(jnp.bfloat16)
     key_own = mapped[:, model_width : 2 * model_width].astype(jnp.bfloat16)
     value_own = (mapped[:, 2 * model_width :] + table[3]).astype(jnp.bfloat16)
-    received = passed_along(jnp.concatenate([key_own, value_own], 1), "shard", 1)
-    key_all = jnp.concatenate([received[:, :model_width], key_own], 0)
-    value_all = jnp.concatenate([received[:, model_width:], value_own], 0)
-    query_heads = split_heads(queries)
-    key_heads = split_heads(key_all)
-    value_heads = split_heads(value_all)
+    groups = 4
+    per_group = HEADS // groups
+    group_width = per_group * (model_width // HEADS)
+    query_groups, key_groups, value_groups = [], [], []
+    for group in range(groups):
+        cols = slice(group * group_width, (group + 1) * group_width)
+        received = passed_along(
+            jnp.concatenate([key_own[:, cols], value_own[:, cols]], 1), "shard", 1
+        )
+        query_groups.append(split_heads_n(queries[:, cols], per_group))
+        key_groups.append(
+            split_heads_n(jnp.concatenate([received[:, :group_width], key_own[:, cols]], 0), per_group)
+        )
+        value_groups.append(
+            split_heads_n(jnp.concatenate([received[:, group_width:], value_own[:, cols]], 0), per_group)
+        )
 
     def head_forward(head_item):
         head_query, head_keys, head_values, slope = head_item
@@ -242,7 +256,17 @@
         mixture = jnp.dot(probs_low, head_values, preferred_element_type=jnp.float32)
         return (mixture, (row_top + jnp.log(row_total))[:, 0])
 
-    mixture_heads, log_total = lax.map(head_forward, (query_heads, key_heads, value_heads, slopes))
+    fwd_parts = []
+    for group in range(groups):
+        chosen = slice(group * per_group, (group + 1) * per_group)
+        fwd_parts.append(
+            lax.map(
+                head_forward,
+                (query_groups[group], key_groups[group], value_groups[group], slopes[chosen]),
+            )
+        )
+    mixture_heads = jnp.concatenate([part[0] for part in fwd_parts], 0)
+    log_total = jnp.concatenate([part[1] for part in fwd_parts], 0)
     attended_low = merge_heads(mixture_heads).astype(jnp.bfloat16)
     resid_one = (
         tokens + jnp.dot(attended_low, out_full, preferred_element_type=jnp.float32) + table[4]
@@ -291,37 +315,33 @@
         grad_keys = contract_rows(grad_scores, head_query) * score_scale
         return (grad_query, grad_keys, grad_values)
 
-    groups = 4
-    per_group = HEADS // groups
-    parts = []
+    query_parts, key_parts, value_parts = [], [], []
     for group in range(groups):
         chosen = slice(group * per_group, (group + 1) * per_group)
-        parts.append(
-            lax.map(
-                head_backward,
-                (
-                    query_heads[chosen],
-                    key_heads[chosen],
-                    value_heads[chosen],
-                    grad_heads[chosen],
-                    log_total[chosen],
-                    slopes[chosen],
-                ),
-            )
-        )
-    query_grads, key_grads, value_grads = (
-        jnp.concatenate([part[index] for part in parts], 0) for index in range(3)
-    )
-    grad_query = merge_heads(query_grads)
-    grad_keys = merge_heads(key_grads)
-    grad_values = merge_heads(value_grads)
-    returned = passed_along(
-        jnp.concatenate([grad_keys[:tok_rows], grad_values[:tok_rows]], 1).astype(jnp.bfloat16),
-        "shard",
-        -1,
-    ).astype(jnp.float32)
-    grad_key_own = grad_keys[tok_rows:] + returned[:, :model_width]
-    grad_value_own = grad_values[tok_rows:] + returned[:, model_width:]
+        group_query, group_keys, group_values = lax.map(
+            head_backward,
+            (
+                query_groups[group],
+                key_groups[group],
+                value_groups[group],
+                grad_heads[chosen],
+                log_total[chosen],
+                slopes[chosen],
+            ),
+        )
+        returned = passed_along(
+            jnp.concatenate(
+                [merge_heads(group_keys[:, :tok_rows]), merge_heads(group_values[:, :tok_rows])], 1
+            ).astype(jnp.bfloat16),
+            "shard",
+            -1,
+        ).astype(jnp.float32)
+        query_parts.append(merge_heads(group_query))
+        key_parts.append(merge_heads(group_keys[:, tok_rows:]) + returned[:, :group_width])
+        value_parts.append(merge_heads(group_values[:, tok_rows:]) + returned[:, group_width:])
+    grad_query = jnp.concatenate(query_parts, 1)
+    grad_key_own = jnp.concatenate(key_parts, 1)
+    grad_value_own = jnp.concatenate(value_parts, 1)
     query_bias_grad = jnp.sum(grad_query, axis=0)
     value_bias_grad = jnp.sum(grad_value_own, axis=0)
     mapped_low = jnp.concatenate([grad_query, grad_key_own, grad_value_own], 1).astype(jnp.bfloat16)

time: 1300 us -> 1300 us (level)
  local copies, waits for them, and re-layouts: 218 us -> 287 us
  waiting for transfers between devices: 587 us -> 544 us
  matrix products: 304 us -> 263 us
    ppermute x2 -> x8, waiting for transfers between devices: 75.9 us -> 38.2 us  [passed_along(): lax.ppermute(value, axis, [(source, source + steps) for source in range(l...]
    slice x12 -> x26, local copies, waits for them, and re-layouts: 9.66 us -> 38.8 us  [the longest x4 7.49 us: body(): received[:, group_width:]]
    unnamed x125 -> x206, local copies, waits for them, and re-layouts: 9.68 us -> 35.7 us
    dot_general x52, matrix products: 150 us -> 134 us  [contract_cols(): lax.dot_general(left_side, right_side, (((1,), (1,)), ((), ())), preferre...]
    dot_general x16, matrix products: 21.6 us -> 7.26 us  [head_backward(): jnp.dot(grad_scores, head_keys, preferred_element_type=jnp.float32)]
  transfers between devices with their start and end apart: 18 -> 24, of which waited for: 13 -> 12; matrix products, arithmetic and copies ran while one was open for 20% -> 23% of each run, Pallas kernels for 0% -> 0%
where the time goes in v4:
time: 1300 us; the launch traced here: 1280 us
  waiting for transfers between devices  544 us (42%)
  local copies, waits for them, and re-layouts  287 us (22%)
  matrix products  263 us (20%)
  other arithmetic  150 us (12%)
  starting transfers between devices  18.9 us (1%)
  between operations  15.7 us (1%)
    reduce_scatter x2, waiting for transfers between devices, reduce_packed(): lax.psum_scatter(stacked, 'outer', scatter_dimension=0, tiled=True)  242 us
    all_gather x2, waiting for transfers between devices, reduce_packed(): stacked = lax.all_gather(stacked, 'outer', axis=0, tiled=True)  137 us
    dot_general x52, matrix products, contract_cols(): lax.dot_general(left_side, right_side, (((1,), (1,)), ((), ())), preferre...  134 us
    add x5, other arithmetic, nesterov(): average_new = AVERAGING * average_old + (1.0 - AVERAGING) * weight_new  68.2 us
    dot_general x36, matrix products, contract_rows(): lax.dot_general(left_side, right_side, (((0,), (0,)), ((), ())), preferre...  59.5 us
    all_gather x2, waiting for transfers between devices, gather_weights(): got = lax.all_gather(other, 'outer', axis=0, tiled=False)  46.2 us
    reduce_scatter x2, waiting for transfers between devices, reduce_packed(): lax.psum_scatter(stacked, 'shard', scatter_dimension=0, tiled=True)  38.7 us
    ppermute x8, waiting for transfers between devices, passed_along(): lax.ppermute(value, axis, [(source, source + steps) for source in range(l...  38.2 us
  transfers between devices with their start and end apart: 24, of which 12 were waited for; matrix products, arithmetic and copies ran while one was open for 23% of the time, Pallas kernels for 0%

profile of v4, /device:TPU:9, one launch (start us, length us, event | category | flops | bytes accessed | tf_op | source)
XLA Modules:
  0.0 1279.9 jit_solution(15430659233751641782)
XLA Ops:
  24.2 46.2 %all-gather.32.cloned.1.call-done = bf16[8,97,1024]{2,1,0:T(8,128)(2,1)} async-done(((bf16[1,97,1024]{2,1,0:T(8,128)(2,1)}), bf16[8,97,1024]{2,1,0:T(8,128)(2,1)}) %all-gather.32.cloned.1.call-update) | async-done | bytes 1589264 | tf_op jit(solution)/shard_map/all_gather | solution.py:48
  183.9 21.6 %while.121 = (s32[]{:T(128)}, bf16[4,512,64]{1,2,0:T(8,128)(2,1)S(1)}, f32[4,512]{1,0:T(4,128)S(1)}, bf16[4,512,64]{2,1,0:T(8,128)(2,1)}, bf16[4,1024,64]{2,1,0:...) while((s32[]{:T(128)}, ...), condition=%wide.region_9.10_spmd.clone.clone, body=%wide.region_6.9_spmd.clone.clone.sunk | while | flops 141557248 | bytes 7108237 | solution.py:263
  206.8 21.3 %while.122 = (s32[]{:T(128)}, bf16[4,512,64]{1,2,0:T(8,128)(2,1)S(1)}, f32[4,512]{1,0:T(4,128)S(1)}, bf16[4,512,64]{2,1,0:T(8,128)(2,1)S(1)}, bf16[4,1024,64]{2,...) while((s32[]{:T(128)}, ...), condition=%wide.region_13.14_spmd.clone.clone, body=%wide.region_10.13_spmd.clone.clone.sunk | while | flops 141557248 | bytes 7108237 | solution.py:263
  251.2 21.6 %while.123 = (s32[]{:T(128)}, bf16[4,512,64]{1,2,0:T(8,128)(2,1)S(1)}, f32[4,512]{1,0:T(4,128)S(1)}, bf16[4,512,64]{2,1,0:T(8,128)(2,1)}, bf16[4,1024,64]{2,1,0:...) while((s32[]{:T(128)}, ...), condition=%wide.region_17.18_spmd.clone.clone, body=%wide.region_14.17_spmd.clone.clone.sunk | while | flops 141557248 | bytes 7108237 | solution.py:263
  273.8 25.9 %while.120 = (s32[]{:T(128)}, bf16[4,512,64]{1,2,0:T(8,128)(2,1)}, f32[4,512]{1,0:T(4,128)S(1)}, bf16[4,512,64]{2,1,0:T(8,128)(2,1)}, bf16[4,1024,64]{2,1,0:T(8,...) while((s32[]{:T(128)}, bf16[4,512,64]{1,2,0:T(8,128)(2,1)}, ...), condition=%wide.region_5.6_spmd.clone.clone, body=%wide.region_2.5_spmd.clone.clone.sunk | while | flops 141557248 | bytes 9205445 | solution.py:263
  332.0 13.5 %fusion.238 = bf16[4096,1024]{1,0:T(8,128)(2,1)} fusion(f32[512,1024]{1,0:T(8,128)S(1)} %copy-done.52, f32[512]{0:T(512)S(1)} %compare_convert_fusion, f32[512,4096]{1,0:T(8,128)} %fusion.217, f32[4096]{0:T(1024)S(1)} %bitcast.658), kind=kOutput, calls=%fused_computation.396 | convolution fusion | flops 4316987392 | bytes 18892800 | tf_op jit(solution)/shard_map/dot_general | solution.py:136
  345.5 21.0 %fusion.262 = (bf16[4096]{0:T(1024)(128)(2,1)S(1)}, bf16[512,4096]{1,0:T(8,128)(2,1)}) fusion(f32[512,4096]{1,0:T(8,128)} %fusion.217, f32[4096]{0:T(1024)S(1)} %bitcast.659, bf16[2048,1024]{1,0:T(8,128)(2,1)} %convert_element_type.147, bf16[2048,1024]{1,0:T(8,128)(2,1)} %bitcast.608, pred[]{:T(512)S(6)} %eq.9, f32[512,1024]{1,0:T(8,128)} %param.35, ...), kind=kOutput, calls=%fused_computation.418 | convolution fusion | flops 4379897856 | bytes 23095296 | tf_op jit(solution)/shard_map/dot_general | solution.py:142
  394.6 24.1 %while.124 = (s32[]{:T(128)}, f32[4,512,64]{1,2,0:T(8,128)S(1)}, f32[4,1024,64]{1,2,0:T(8,128)S(1)}, f32[4,1024,64]{1,2,0:T(8,128)}, bf16[4,512,64]{2,1,0:T(8,12...) while((s32[]{:T(128)}, f32[4,512,64]{1,2,0:T(8,128)S(1)}, ...), condition=%wide.region_24.25_spmd.clone.clone, body=%wide.region_22.24_spmd.clone.clone.sunk | while | flops 343506432 | bytes 18634940 | solution.py:321
  426.2 29.7 %while.125 = (s32[]{:T(128)}, f32[4,512,64]{1,2,0:T(8,128)S(1)}, f32[4,1024,64]{1,2,0:T(8,128)}, f32[4,1024,64]{1,2,0:T(8,128)}, bf16[4,512,64]{2,1,0:T(8,128)(2...) while((s32[]{:T(128)}, f32[4,512,64]{1,2,0:T(8,128)S(1)}, ...), condition=%wide.region_27.28_spmd.clone.clone, body=%wide.region_25.27_spmd.clone.clone.sunk | while | flops 343506432 | bytes 18634940 | solution.py:321
  464.6 29.6 %while.126 = (s32[]{:T(128)}, f32[4,512,64]{1,2,0:T(8,128)S(1)}, f32[4,1024,64]{1,2,0:T(8,128)}, f32[4,1024,64]{1,2,0:T(8,128)}, bf16[4,512,64]{2,1,0:T(8,128)(2...) while((s32[]{:T(128)}, f32[4,512,64]{1,2,0:T(8,128)S(1)}, ...), condition=%wide.region_30.31_spmd.clone.clone, body=%wide.region_28.30_spmd.clone.clone.sunk | while | flops 343506432 | bytes 18634940 | solution.py:321
  502.9 30.0 %while.127 = (s32[]{:T(128)}, f32[4,512,64]{1,2,0:T(8,128)S(1)}, f32[4,1024,64]{1,2,0:T(8,128)}, f32[4,1024,64]{1,2,0:T(8,128)}, bf16[4,512,64]{2,1,0:T(8,128)(2...) while((s32[]{:T(128)}, f32[4,512,64]{1,2,0:T(8,128)S(1)}, ...), condition=%wide.region_33.34_spmd.clone.clone, body=%wide.region_31.33_spmd.clone.clone.sunk | while | flops 343506432 | bytes 18634940 | solution.py:321
  546.8 27.4 %collective-permute-done.7 = bf16[512,512]{0,1:T(8,128)(2,1)S(1)} collective-permute-done((bf16[512,512]{0,1:T(8,128)(2,1)S(1)}, bf16[512,512]{0,1:T(8,128)(2,1)S(1)}, u32[]{:S(2)}, u32[]{:S(2)}) %collective-permute-start.7) | collective-permute-done | bytes 524320 | tf_op jit(solution)/shard_map/ppermute | solution.py:22
  655.7 13.5 %concatenate.199 = bf16[2,2,8,128,1024]{4,3,2,1,0:T(8,128)(2,1)} reshape(bf16[2,1024,2048]{2,1,0:T(8,128)(2,1)} %bitcast.591) | data formatting | bytes 16777216 | tf_op jit(solution)/shard_map/concatenate | solution.py:103
  687.9 28.3 %reduce-scatter.13.cloned.1.call-done = bf16[1,4608,1024]{2,1,0:T(8,128)(2,1)} async-done(((bf16[2,4608,1024]{2,1,0:T(8,128)(2,1)}), bf16[1,4608,1024]{2,1,0:T(8,128)(2,1)}) %reduce-scatter.13.cloned.1.call-update) | async-done | bytes 9437200 | tf_op jit(solution)/shard_map/reduce_scatter | solution.py:106
  716.3 79.8 %reduce-scatter.9.cloned.1.call-done = bf16[1,194,1024]{2,1,0:T(8,128)(2,1)} async-done(((bf16[8,194,1024]{2,1,0:T(8,128)(2,1)}), bf16[1,194,1024]{2,1,0:T(8,128)(2,1)}) %reduce-scatter.9.cloned.1.call-update) | async-done | bytes 397328 | tf_op jit(solution)/shard_map/reduce_scatter | solution.py:108
  798.0 162.3 %reduce-scatter.15.cloned.1.call-done = bf16[1,576,1024]{2,1,0:T(8,128)(2,1)} async-done(((bf16[8,576,1024]{2,1,0:T(8,128)(2,1)}), bf16[1,576,1024]{2,1,0:T(8,128)(2,1)}) %reduce-scatter.15.cloned.1.call-update) | async-done | bytes 1179664 | tf_op jit(solution)/shard_map/reduce_scatter | solution.py:108
  960.3 16.8 %reduce-scatter.11.cloned.1.call-done = bf16[1,97,1024]{2,1,0:T(8,128)(2,1)} async-done(((bf16[2,97,1024]{2,1,0:T(8,128)(2,1)}), bf16[1,97,1024]{2,1,0:T(8,128)(2,1)}) %reduce-scatter.11.cloned.1.call-update) | async-done | bytes 198672 | tf_op jit(solution)/shard_map/reduce_scatter | solution.py:110
  979.1 21.9 %reduce-scatter.17.cloned.1.call-done = bf16[1,288,1024]{2,1,0:T(8,128)(2,1)} async-done(((bf16[2,288,1024]{2,1,0:T(8,128)(2,1)}), bf16[1,288,1024]{2,1,0:T(8,128)(2,1)}) %reduce-scatter.17.cloned.1.call-update) | async-done | bytes 589840 | tf_op jit(solution)/shard_map/reduce_scatter | solution.py:110
  1001.1 61.8 %all-gather.24.cloned.1.call-done = bf16[1,776,1024]{2,0,1:T(2,128)(2,1)} async-done(((bf16[1,97,1024]{2,0,1:T(2,128)(2,1)}), bf16[1,776,1024]{2,0,1:T(2,128)(2,1)}) %all-gather.24.cloned.1.call-update) | async-done | bytes 1589264 | tf_op jit(solution)/shard_map/all_gather | solution.py:112
  1066.6 75.4 %all-gather.28.cloned.1.call-done = bf16[1,2304,1024]{2,1,0:T(8,128)(2,1)} async-done(((bf16[1,288,1024]{2,1,0:T(8,128)(2,1)}), bf16[1,2304,1024]{2,1,0:T(8,128)(2,1)}) %all-gather.28.cloned.1.call-update) | async-done | bytes 4718608 | tf_op jit(solution)/shard_map/all_gather | solution.py:112
  1143.6 15.1 %add_add_fusion = f32[512,1024]{1,0:T(8,128)} fusion(f32[512,1024]{1,0:T(8,128)S(1)} %copy-done.8, bf16[2048,1024]{1,0:T(8,128)(2,1)} %convert_element_type.147, bf16[2048,1024]{1,0:T(8,128)(2,1)} %bitcast.609, pred[]{:T(512)S(6)} %eq.9, f32[1024]{0:T(1024)S(1)} %bitcast.661, f32[512,4096]{1,0:T(8,128)} %fusion.217, f32[4096]{0:T(1024)S(1)} %bitcast.660), kind=kOutput, calls=%fused_computation.286 | convolution fusion | flops 4354736128 | bytes 20992000 | tf_op jit(solution)/shard_map/dot_general | solution.py:281
  1180.8 15.8 %multiply_add_fusion.3 = (f32[512,3072]{1,0:T(8,128)}, f32[512,3072]{1,0:T(8,128)}, f32[512,3072]{1,0:T(8,128)}) fusion(f32[512,3072]{1,0:T(8,128)} %param.39, f32[512,3072]{1,0:T(8,128)} %param.37, f32[512,3072]{1,0:T(8,128)} %reshape_reshape.48, f32[512,3072]{1,0:T(8,128)} %param.38), kind=kLoop, calls=%fused_computation.258 | loop fusion | flops 14155776 | bytes 44040192 | tf_op jit(solution)/shard_map/add | solution.py:176
  1227.8 22.6 %multiply_add_fusion.1 = (f32[1024,2048]{1,0:T(8,128)}, f32[1024,2048]{1,0:T(8,128)}, f32[1024,2048]{1,0:T(8,128)}) fusion(f32[1024,2048]{1,0:T(8,128)} %param.45, f32[1024,2048]{1,0:T(8,128)} %param.43, f32[1024,2048]{1,0:T(8,128)} %reshape_reshape.50, f32[1024,2048]{1,0:T(8,128)} %param.44), kind=kLoop, calls=%fused_computation.252 | loop fusion | flops 18874368 | bytes 58720256 | tf_op jit(solution)/shard_map/add | solution.py:176
  1250.3 22.6 %multiply_add_fusion = (f32[2048,1024]{1,0:T(8,128)}, f32[2048,1024]{1,0:T(8,128)}, f32[2048,1024]{1,0:T(8,128)}) fusion(f32[2048,1024]{1,0:T(8,128)} %param.48, f32[2048,1024]{1,0:T(8,128)} %param.46, f32[16,128,1024]{2,1,0:T(8,128)} %get-tuple-element.1700, f32[2048,1024]{1,0:T(8,128)} %param.47), kind=kLoop, calls=%fused_computation.251 | loop fusion | flops 18874368 | bytes 58720256 | tf_op jit(solution)/shard_map/add | solution.py:176
  (709 shorter events, 618.4 us)
Async XLA Ops:
  7.2 63.2 %all-gather.32.cloned.1.call-start = ((), (), s32[]{:S(2)}) async-start(), calls=%async_computation.19 | async-start | bytes 1916928 | tf_op jit(solution)/shard_map/all_gather | solution.py:48
  17.2 6.2 collective-permute-start
  24.2 82.6 %all-gather.18.cloned.1.call-start = ((), (), s32[]{:S(2)}) async-start(), calls=%async_computation.12 | async-start | bytes 4767744 | tf_op jit(solution)/shard_map/all_gather | solution.py:49
  73.9 156.3 %all-gather.20.cloned.1.call-start = ((), (), s32[]{:S(2)}) async-start(), calls=%async_computation.13 | async-start | bytes 5308416 | tf_op jit(solution)/shard_map/all_gather | solution.py:48
  93.4 12.5 collective-permute-start.5
  106.7 195.1 %all-gather.22.cloned.1.call-start = ((), (), s32[]{:S(2)}) async-start(), calls=%async_computation.14 | async-start | bytes 14155776 | tf_op jit(solution)/shard_map/all_gather | solution.py:49
  129.8 27.6 %collective-permute-start.2 = (bf16[512,512]{1,0:T(8,128)(2,1)}, bf16[512,512]{1,0:T(8,128)(2,1)}, u32[]{:S(2)}, u32[]{:S(2)}) collective-permute-start(bf16[512,512]{1,0:T(8,128)(2,1)} %pad_maximum_fusion.5), channel_id=1, source_target_pairs={{0,1},{2,3},{4,5},{6,7},{8,9},{10,11},{12,13},{14,15},{16,17},{18,... | collective-permute-start | bytes 1572872 | tf_op jit(solution)/shard_map/ppermute | solution.py:22
  148.2 22.5 %collective-permute-start.3 = (bf16[512,512]{1,0:T(8,128)(2,1)}, bf16[512,512]{1,0:T(8,128)(2,1)}, u32[]{:S(2)}, u32[]{:S(2)}) collective-permute-start(bf16[512,512]{1,0:T(8,128)(2,1)} %pad_maximum_fusion.8), channel_id=1, source_target_pairs={{0,1},{2,3},{4,5},{6,7},{8,9},{10,11},{12,13},{14,15},{16,17},{18,... | collective-permute-start | bytes 1572872 | tf_op jit(solution)/shard_map/ppermute | solution.py:22
  152.1 76.1 %collective-permute-start.4 = (bf16[512,512]{1,0:T(8,128)(2,1)}, bf16[512,512]{1,0:T(8,128)(2,1)}, u32[]{:S(2)}, u32[]{:S(2)}) collective-permute-start(bf16[512,512]{1,0:T(8,128)(2,1)} %pad_maximum_fusion.11), channel_id=1, source_target_pairs={{0,1},{2,3},{4,5},{6,7},{8,9},{10,11},{12,13},{14,15},{16,17},{18,... | collective-permute-start | bytes 1572872 | tf_op jit(solution)/shard_map/ppermute | solution.py:22
  155.0 82.4 %collective-permute-start.1 = (bf16[512,512]{1,0:T(8,128)(2,1)}, bf16[512,512]{1,0:T(8,128)(2,1)}, u32[]{:S(2)}, u32[]{:S(2)}) collective-permute-start(bf16[512,512]{1,0:T(8,128)(2,1)} %pad_maximum_fusion.2), channel_id=1, source_target_pairs={{0,1},{2,3},{4,5},{6,7},{8,9},{10,11},{12,13},{14,15},{16,17},{18,... | collective-permute-start | bytes 1572872 | tf_op jit(solution)/shard_map/ppermute | solution.py:22
  230.3 454.0 %reduce-scatter.7.cloned.1.call-start = ((), (), s32[]{:S(2)}) async-start(), calls=%async_computation.6 | async-start | bytes 9535488 | tf_op jit(solution)/shard_map/reduce_scatter | solution.py:106
  540.0 47.0 %collective-permute-start.9 = (bf16[512,512]{0,1:T(8,128)(2,1)S(1)}, bf16[512,512]{0,1:T(8,128)(2,1)S(1)}, u32[]{:S(2)}, u32[]{:S(2)}) collective-permute-start(bf16[512,512]{0,1:T(8,128)(2,1)S(1)} %pad_maximum_fusion.17), channel_id=1, source_target_pairs={{1,0},{3,2},{5,4},{7,6},{9,8},{11,10},{13,12},{15,14},{17,16},{19,... | collective-permute-start | bytes 1572872 | tf_op jit(solution)/shard_map/ppermute | solution.py:22
  542.5 43.4 %collective-permute-start.8 = (bf16[512,512]{0,1:T(8,128)(2,1)S(1)}, bf16[512,512]{0,1:T(8,128)(2,1)S(1)}, u32[]{:S(2)}, u32[]{:S(2)}) collective-permute-start(bf16[512,512]{0,1:T(8,128)(2,1)S(1)} %pad_maximum_fusion.16), channel_id=1, source_target_pairs={{1,0},{3,2},{5,4},{7,6},{9,8},{11,10},{13,12},{15,14},{17,16},{19,... | collective-permute-start | bytes 1572872 | tf_op jit(solution)/shard_map/ppermute | solution.py:22
  543.9 30.3 %collective-permute-start.7 = (bf16[512,512]{0,1:T(8,128)(2,1)S(1)}, bf16[512,512]{0,1:T(8,128)(2,1)S(1)}, u32[]{:S(2)}, u32[]{:S(2)}) collective-permute-start(bf16[512,512]{0,1:T(8,128)(2,1)S(1)} %pad_maximum_fusion.15), channel_id=1, source_target_pairs={{1,0},{3,2},{5,4},{7,6},{9,8},{11,10},{13,12},{15,14},{17,16},{19,... | collective-permute-start | bytes 1572872 | tf_op jit(solution)/shard_map/ppermute | solution.py:22
  545.3 40.2 %collective-permute-start.6 = (bf16[512,512]{0,1:T(8,128)(2,1)S(1)}, bf16[512,512]{0,1:T(8,128)(2,1)S(1)}, u32[]{:S(2)}, u32[]{:S(2)}) collective-permute-start(bf16[512,512]{0,1:T(8,128)(2,1)S(1)} %pad_maximum_fusion.14), channel_id=1, source_target_pairs={{1,0},{3,2},{5,4},{7,6},{9,8},{11,10},{13,12},{15,14},{17,16},{19,... | collective-permute-start | bytes 1572872 | tf_op jit(solution)/shard_map/ppermute | solution.py:22
  647.2 69.0 %reduce-scatter.13.cloned.1.call-start = ((), (), s32[]{:S(2)}) async-start(), calls=%async_computation.9 | async-start | bytes 28311552 | tf_op jit(solution)/shard_map/reduce_scatter | solution.py:106
  684.2 111.8 %reduce-scatter.9.cloned.1.call-start = ((), (), s32[]{:S(2)}) async-start(), calls=%async_computation.7 | async-start | bytes 3686400 | tf_op jit(solution)/shard_map/reduce_scatter | solution.py:108
  687.9 272.3 %reduce-scatter.15.cloned.1.call-start = ((), (), s32[]{:S(2)}) async-start(), calls=%async_computation.10 | async-start | bytes 10616832 | tf_op jit(solution)/shard_map/reduce_scatter | solution.py:108
  716.2 260.8 %reduce-scatter.11.cloned.1.call-start = ((), (), s32[]{:S(2)}) async-start(), calls=%async_computation.8 | async-start | bytes 638976 | tf_op jit(solution)/shard_map/reduce_scatter | solution.py:110
  797.9 203.1 %reduce-scatter.17.cloned.1.call-start = ((), (), s32[]{:S(2)}) async-start(), calls=%async_computation.11 | async-start | bytes 1769472 | tf_op jit(solution)/shard_map/reduce_scatter | solution.py:110
  960.2 102.6 %all-gather.24.cloned.1.call-start = ((), (), s32[]{:S(2)}) async-start(), calls=%async_computation.15 | async-start | bytes 3575808 | tf_op jit(solution)/shard_map/all_gather | solution.py:112
  979.1 162.9 %all-gather.28.cloned.1.call-start = ((), (), s32[]{:S(2)}) async-start(), calls=%async_computation.17 | async-start | bytes 5308416 | tf_op jit(solution)/shard_map/all_gather | solution.py:112
  1001.0 157.7 %all-gather.26.cloned.1.call-start = ((), (), s32[]{:S(2)}) async-start(), calls=%async_computation.16 | async-start | bytes 4767744 | tf_op jit(solution)/shard_map/all_gather | solution.py:113
  1066.5 130.0 %all-gather.30.cloned.1.call-start = ((), (), s32[]{:S(2)}) async-start(), calls=%async_computation.18 | async-start | bytes 14155776 | tf_op jit(solution)/shard_map/all_gather | solution.py:113
  (114 other events, 926.5 us)
Sparse Core Ops, SparseCore 0:
  24.3 46.1 all-gather.31
  74.1 12.6 all-gather.17
  106.8 78.8 all-gather.19
  230.4 23.6 all-gather.21
  647.3 18.3 reduce-scatter.6
  684.4 31.7 reduce-scatter.12
  720.4 75.6 reduce-scatter.8
  799.6 160.5 reduce-scatter.14
  963.1 13.9 reduce-scatter.10
  979.1 21.8 reduce-scatter.16
  1003.8 59.0 all-gather.23
  1064.9 77.0 all-gather.27
  1144.1 13.6 all-gather.25
  1159.2 22.7 all-gather.29

commit v5 on v4

--- a/solution.py
+++ b/solution.py
@@ -22,102 +22,77 @@
     return lax.ppermute(value, axis, [(source, source + steps) for source in range(leading, last)])
 
 
-LANE = 1024
-
-
-def to_blocks(half, blocks):
-    flat = half.reshape(-1)
-    size = flat.shape[0]
-    padded = -(-size // (blocks * LANE)) * blocks * LANE
-    if padded != size:
-        flat = jnp.pad(flat, (0, padded - size))
-    return flat.reshape(blocks, -1, LANE)
-
-
-def gather_weights(halves):
+SMALL_WIDTH = 3072
+
+
+def small_rows(small_half, blocks):
+    flat = small_half.reshape(-1)
+    padded = blocks * SMALL_WIDTH
+    return jnp.pad(flat, (0, padded - flat.shape[0])).reshape(blocks, 1, SMALL_WIDTH)
+
+
+def gather_rows(row_arrays):
     cores = lax.axis_size("core")
     outer = lax.axis_size("outer")
     blocks = cores * outer
-    lows = [half.astype(jnp.bfloat16) for half, unused in halves]
-    packed = [to_blocks(low, blocks) for low in lows]
-    widths = [piece.shape[1] for piece in packed]
-    own = jnp.concatenate(packed, axis=1)
     place = lax.axis_index("core") * outer + lax.axis_index("outer")
-    mine = lax.dynamic_index_in_dim(own, place, 0, keepdims=False)
+    heights = [piece.shape[1] for piece in row_arrays]
+    mine = jnp.concatenate(
+        [lax.dynamic_index_in_dim(piece, place, 0, keepdims=False) for piece in row_arrays], 0
+    )
     other = lax.ppermute(mine, "shard", [(0, 1), (1, 0)])
     got = lax.all_gather(other, "outer", axis=0, tiled=False)
     got = lax.all_gather(got, "core", axis=0, tiled=False)
-    got = got.reshape(blocks, -1, LANE)
+    got = got.reshape(blocks, -1, got.shape[-1])
+    pieces = []
+    offset = 0
+    for height in heights:
+        pieces.append(got[:, offset : offset + height])
+        offset += height
+    return pieces
+
+
+def join_halves(own, other, dim):
     upper = lax.axis_index("shard") == 1
-    fulls = []
-    offset = 0
-    for (half, dim), low, width in zip(halves, lows, widths):
-        other_half = got[:, offset : offset + width].reshape(-1)[: low.size].reshape(low.shape)
-        offset += width
-        in_order = jnp.concatenate([low, other_half], axis=dim)
-        swapped = jnp.concatenate([other_half, low], axis=dim)
-        fulls.append(jnp.where(upper, swapped, in_order))
-    return fulls
-
-
-def pack_halves(grad_full, dim, blocks):
-    shard_count = lax.axis_size("shard")
-    rows, cols = grad_full.shape
-    if dim == 0:
-        halves = grad_full.reshape(shard_count, -1)
-    else:
-        halves = grad_full.reshape(rows, shard_count, cols // shard_count).transpose(1, 0, 2)
-        halves = halves.reshape(shard_count, -1)
-    half_size = halves.shape[1]
-    padded = -(-half_size // (blocks * LANE)) * blocks * LANE
-    if padded != half_size:
-        halves = jnp.pad(halves, ((0, 0), (0, padded - half_size)))
-    return halves.reshape(shard_count, blocks, -1, LANE), half_size
-
-
-def unpack_half(packed, half_size, half_shape):
-    return packed.reshape(-1)[:half_size].reshape(half_shape)
-
-
-def reduce_grads(grads):
+    in_order = jnp.concatenate([own, other], axis=dim)
+    swapped = jnp.concatenate([other, own], axis=dim)
+    return jnp.where(upper, swapped, in_order)
+
+
+def reduce_rows(row_grads):
     shard_count = lax.axis_size("shard")
     cores = lax.axis_size("core")
     outer = lax.axis_size("outer")
     blocks = cores * outer
-    packed, sizes, shapes = [], [], []
-    for grad_full, dim in grads:
-        piece, half_size = pack_halves(grad_full, dim, blocks)
-        packed.append(piece)
-        sizes.append(half_size)
-        rows, cols = grad_full.shape
-        shapes.append((rows // shard_count, cols) if dim == 0 else (rows, cols // shard_count))
-    widths = [piece.shape[2] for piece in packed]
-    return reduce_packed(packed, widths, sizes, shapes)
-
-
-def reduce_packed(packed, widths, sizes, shapes):
-    shard_count = lax.axis_size("shard")
-    cores = lax.axis_size("core")
-    outer = lax.axis_size("outer")
-    blocks = cores * outer
-    stacked = jnp.concatenate(packed, axis=2).astype(jnp.bfloat16)
-    stacked = stacked.reshape(shard_count, cores, outer, -1, LANE).transpose(1, 2, 0, 3, 4)
-    stacked = stacked.reshape(cores, -1, LANE)
+    heights = [piece.shape[3] for piece in row_grads]
+    width = row_grads[0].shape[-1]
+    stacked = jnp.concatenate(
+        [piece.astype(jnp.bfloat16).transpose(1, 2, 0, 3, 4) for piece in row_grads], 3
+    )
+    stacked = stacked.reshape(cores, -1, width)
     stacked = lax.psum_scatter(stacked, "core", scatter_dimension=0, tiled=True)
-    stacked = stacked.reshape(outer, -1, LANE)
+    stacked = stacked.reshape(outer, -1, width)
     stacked = lax.psum_scatter(stacked, "outer", scatter_dimension=0, tiled=True)
-    stacked = stacked.reshape(shard_count, -1, LANE)
+    stacked = stacked.reshape(shard_count, -1, width)
     stacked = lax.psum_scatter(stacked, "shard", scatter_dimension=0, tiled=True)
     stacked = stacked.reshape(stacked.shape[1:])
     stacked = lax.all_gather(stacked, "outer", axis=0, tiled=True)
     stacked = lax.all_gather(stacked, "core", axis=0, tiled=True)
-    stacked = stacked.reshape(blocks, -1, LANE).astype(jnp.float32)
-    totals = []
+    stacked = stacked.reshape(blocks, -1, width)
+    pieces = []
     offset = 0
-    for width, half_size, half_shape in zip(widths, sizes, shapes):
-        totals.append(unpack_half(stacked[:, offset : offset + width], half_size, half_shape))
-        offset += width
-    return totals
+    for height in heights:
+        pieces.append(stacked[:, offset : offset + height].astype(jnp.float32))
+        offset += height
+    return pieces
+
+
+def split_rows(grad_full):
+    shard_count = lax.axis_size("shard")
+    cores = lax.axis_size("core")
+    outer = lax.axis_size("outer")
+    rows, cols = grad_full.shape
+    return grad_full.reshape(shard_count, cores, outer, rows // (shard_count * cores * outer), cols)
 
 
 def norm_stats(field_in):
@@ -217,10 +192,25 @@
     head_size = model_width // HEADS
     score_scale = head_size ** (-0.5)
     slopes = 2.0 ** (-8.0 * (jnp.arange(HEADS, dtype=jnp.float32) + 1.0) / HEADS)
-    qkv_full, small_full = gather_weights([(qkv_weight, 0), (small_params, 1)])
-    out_full, up_full, down_full = gather_weights(
-        [(out_weight, 0), (up_weight, 1), (down_weight, 0)]
-    )
+    blocks = lax.axis_size("core") * lax.axis_size("outer")
+    qkv_own = qkv_weight.astype(jnp.bfloat16)
+    small_own = small_params.astype(jnp.bfloat16)
+    qkv_other, small_other = gather_rows(
+        [qkv_own.reshape(blocks, -1, qkv_own.shape[1]), small_rows(small_own, blocks)]
+    )
+    qkv_full = join_halves(qkv_own, qkv_other.reshape(qkv_own.shape), 0)
+    small_full = join_halves(
+        small_own, small_other.reshape(-1)[: small_own.size].reshape(small_own.shape), 1
+    )
+    out_own = out_weight.astype(jnp.bfloat16)
+    up_own_t = up_weight.astype(jnp.bfloat16).T
+    down_own = down_weight.astype(jnp.bfloat16)
+    out_other, up_other_t, down_other = gather_rows(
+        [piece.reshape(blocks, -1, piece.shape[1]) for piece in (out_own, up_own_t, down_own)],
+    )
+    out_full = join_halves(out_own, out_other.reshape(out_own.shape), 0)
+    up_full_t = join_halves(up_own_t, up_other_t.reshape(up_own_t.shape), 0)
+    down_full = join_halves(down_own, down_other.reshape(down_own.shape), 0)
     table = small_full.astype(jnp.float32)
     up_bias = table[8:12].reshape(FF)
     normed_one, inverse_one = norm_stats(tokens)
@@ -276,7 +266,7 @@
     grad_out = cotangent * row_live
     down_bias_grad = jnp.sum(grad_out, axis=0)
     grad_low = grad_out.astype(jnp.bfloat16)
-    pre_act = jnp.dot(inner_low, up_full, preferred_element_type=jnp.float32) + up_bias
+    pre_act = contract_cols(inner_low, up_full_t) + up_bias
     act_low = gelu_tanh(pre_act).astype(jnp.bfloat16)
     branch_out = jnp.dot(act_low, down_full, preferred_element_type=jnp.float32)
     block_out = resid_one + branch_out + table[7]
@@ -285,17 +275,22 @@
     grad_pre = gelu_back(pre_act, grad_act)
     up_bias_grad = jnp.sum(grad_pre, axis=0)
     pre_low = grad_pre.astype(jnp.bfloat16)
-    up_grad = contract_rows(inner_low, pre_low)
-    grad_inner = contract_cols(pre_low, up_full)
+    up_grad_t = contract_rows(pre_low, inner_low)
+    grad_inner = jnp.dot(pre_low, up_full_t, preferred_element_type=jnp.float32)
     gain_two_grad = jnp.sum(grad_inner * normed_two, axis=0)
     shift_two_grad = jnp.sum(grad_inner, axis=0)
     grad_resid = grad_out + norm_back(grad_inner * table[5], normed_two, inverse_two)
     resid_low = grad_resid.astype(jnp.bfloat16)
     out_grad = contract_rows(attended_low, resid_low)
-    grad_resid, resid_low, up_grad, down_grad, out_grad = lax.optimization_barrier(
-        (grad_resid, resid_low, up_grad, down_grad, out_grad)
-    )
-    up_total, down_total, out_total = reduce_grads([(up_grad, 1), (down_grad, 0), (out_grad, 0)])
+    grad_resid, resid_low, up_grad_t, down_grad, out_grad = lax.optimization_barrier(
+        (grad_resid, resid_low, up_grad_t, down_grad, out_grad)
+    )
+    out_sum, up_sum_t, down_sum = reduce_rows(
+        [split_rows(out_grad), split_rows(up_grad_t), split_rows(down_grad)]
+    )
+    out_total = out_sum.reshape(out_weight.shape)
+    up_total = up_sum_t.reshape(up_weight.shape[::-1]).T
+    down_total = down_sum.reshape(down_weight.shape)
     out_bias_grad = jnp.sum(grad_resid, axis=0)
     grad_mixture = contract_cols(resid_low, out_full).astype(jnp.bfloat16)
     grad_heads = split_heads(grad_mixture)
@@ -363,7 +358,13 @@
         ]
     )
     small_grad = jnp.concatenate([head_rows, up_bias_grad.reshape(4, model_width)], 0)
-    qkv_total, small_total = reduce_grads([(qkv_grad, 0), (small_grad, 1)])
+    small_halves = small_grad.reshape(small_grad.shape[0], shard_count, -1).transpose(1, 0, 2)
+    small_packed = jnp.stack(
+        [small_rows(small_halves[index], blocks) for index in range(shard_count)]
+    ).reshape(shard_count, lax.axis_size("core"), lax.axis_size("outer"), 1, SMALL_WIDTH)
+    qkv_sum, small_sum = reduce_rows([split_rows(qkv_grad), small_packed])
+    qkv_total = qkv_sum.reshape(qkv_weight.shape)
+    small_total = small_sum.reshape(-1)[: small_params.size].reshape(small_params.shape)
     rate = 2.0 / math.sqrt(model_width * tok_rows * shard_count * group_count)
     qkv_new = nesterov(qkv_total, qkv_weight, qkv_momentum, qkv_average, rate)
     out_new = nesterov(out_total, out_weight, out_momentum, out_average, rate)

time: 1300 us -> 1240 us (0.954)
  local copies, waits for them, and re-layouts: 287 us -> 228 us
    another operation x22 -> x20, local copies, waits for them, and re-layouts: 50.5 us -> 8.11 us  [the longest x2 18.2 us: unpack_half(): return packed.reshape(-1)[:half_size].reshape(half_shape)]
    concatenate x4 -> x0, local copies, waits for them, and re-layouts: 35.9 us -> none  [reduce_packed(): stacked = jnp.concatenate(packed, axis=2).astype(jnp.bfloat16)]
    convert_element_type x1 -> x4, local copies, waits for them, and re-layouts: 4.68 us -> 30.4 us  [reduce_rows(): piece.astype(jnp.bfloat16).transpose(1, 2, 0, 3, 4)]
    slice x10 -> x9, local copies, waits for them, and re-layouts: 36.7 us -> 16.4 us  [the longest x3 8.73 us: reduce_rows(): pieces.append(stacked[:, offset:offset + height].astype(jnp.float32))]
    unnamed x206 -> x221, local copies, waits for them, and re-layouts: 35.7 us -> 48.3 us
  transfers between devices with their start and end apart: 24 -> 24, of which waited for: 12 -> 11; matrix products, arithmetic and copies ran while one was open for 23% -> 23% of each run, Pallas kernels for 0% -> 0%
where the time goes in v5:
time: 1240 us; the launch traced here: 1230 us
  waiting for transfers between devices  544 us (44%)
  matrix products  266 us (21%)
  local copies, waits for them, and re-layouts  228 us (18%)
  other arithmetic  153 us (12%)
  starting transfers between devices  19.1 us (2%)
  between operations  15.6 us (1%)
    reduce_scatter x2, waiting for transfers between devices, reduce_rows(): lax.psum_scatter(stacked, 'outer', scatter_dimension=0, tiled=True)  246 us
    all_gather x2, waiting for transfers between devices, reduce_rows(): stacked = lax.all_gather(stacked, 'outer', axis=0, tiled=True)  138 us
    dot_general x52, matrix products, contract_cols(): lax.dot_general(left_side, right_side, (((1,), (1,)), ((), ())), preferre...  136 us
    add x5, other arithmetic, nesterov(): average_new = AVERAGING * average_old + (1.0 - AVERAGING) * weight_new  64.6 us
    dot_general x36, matrix products, contract_rows(): lax.dot_general(left_side, right_side, (((0,), (0,)), ((), ())), preferre...  60.1 us
    all_gather x2, waiting for transfers between devices, gather_rows(): got = lax.all_gather(other, 'outer', axis=0, tiled=False)  49 us
    unnamed x221, local copies, waits for them, and re-layouts  48.3 us
    reduce_scatter x2, waiting for transfers between devices, reduce_rows(): lax.psum_scatter(stacked, 'shard', scatter_dimension=0, tiled=True)  39.3 us
  transfers between devices with their start and end apart: 24, of which 11 were waited for; matrix products, arithmetic and copies ran while one was open for 23% of the time, Pallas kernels for 0%

profile of v5, /device:TPU:9, one launch (start us, length us, event | category | flops | bytes accessed | tf_op | source)
XLA Modules:
  0.0 1226.9 jit_solution(553349997312163846)
XLA Ops:
  19.2 49.0 %all-gather.32.cloned.1.call-done = bf16[8,33,3072]{2,1,0:T(8,128)(2,1)} async-done(((bf16[1,33,3072]{2,1,0:T(8,128)(2,1)}), bf16[8,33,3072]{2,1,0:T(8,128)(2,1)}) %all-gather.32.cloned.1.call-update) | async-done | bytes 1622032 | tf_op jit(solution)/shard_map/all_gather | solution.py:44
  172.1 21.6 %while.121 = (s32[]{:T(128)}, bf16[4,512,64]{1,2,0:T(8,128)(2,1)S(1)}, f32[4,512]{1,0:T(4,128)S(1)}, bf16[4,512,64]{2,1,0:T(8,128)(2,1)}, bf16[4,1024,64]{2,1,0:...) while((s32[]{:T(128)}, ...), condition=%wide.region_9.10_spmd.clone.clone, body=%wide.region_6.9_spmd.clone.clone.sunk | while | flops 141557248 | bytes 7108237 | solution.py:253
  194.4 21.3 %while.122 = (s32[]{:T(128)}, bf16[4,512,64]{1,2,0:T(8,128)(2,1)S(1)}, f32[4,512]{1,0:T(4,128)S(1)}, bf16[4,512,64]{2,1,0:T(8,128)(2,1)S(1)}, bf16[4,1024,64]{2,...) while((s32[]{:T(128)}, ...), condition=%wide.region_13.14_spmd.clone.clone, body=%wide.region_10.13_spmd.clone.clone.sunk | while | flops 141557248 | bytes 7108237 | solution.py:253
  239.1 21.2 %while.123 = (s32[]{:T(128)}, bf16[4,512,64]{1,2,0:T(8,128)(2,1)S(1)}, f32[4,512]{1,0:T(4,128)S(1)}, bf16[4,512,64]{2,1,0:T(8,128)(2,1)}, bf16[4,1024,64]{2,1,0:...) while((s32[]{:T(128)}, ...), condition=%wide.region_17.18_spmd.clone.clone, body=%wide.region_14.17_spmd.clone.clone.sunk | while | flops 141557248 | bytes 7108237 | solution.py:253
  261.3 25.9 %while.120 = (s32[]{:T(128)}, bf16[4,512,64]{1,2,0:T(8,128)(2,1)}, f32[4,512]{1,0:T(4,128)S(1)}, bf16[4,512,64]{2,1,0:T(8,128)(2,1)}, bf16[4,1024,64]{2,1,0:T(8,...) while((s32[]{:T(128)}, bf16[4,512,64]{1,2,0:T(8,128)(2,1)}, ...), condition=%wide.region_5.6_spmd.clone.clone, body=%wide.region_2.5_spmd.clone.clone.sunk | while | flops 141557248 | bytes 9205445 | solution.py:253
  314.1 14.0 %fusion.238 = bf16[4096,1024]{1,0:T(8,128)(2,1)} fusion(f32[512,1024]{1,0:T(8,128)} %param.35, f32[512]{0:T(512)S(1)} %copy-done.85, f32[512,4096]{1,0:T(8,128)} %fusion.221, f32[4096]{0:T(1024)S(1)} %bitcast.690), kind=kOutput, calls=%fused_computation.405 | convolution fusion | flops 4316987392 | bytes 18892800 | tf_op jit(solution)/shard_map/dot_general | solution.py:111
  328.1 20.9 %fusion.264 = (bf16[4096]{0:T(1024)(128)(2,1)S(1)}, bf16[512,4096]{1,0:T(8,128)(2,1)}) fusion(f32[512,4096]{1,0:T(8,128)} %fusion.221, f32[4096]{0:T(1024)S(1)} %bitcast.691, bf16[2048,1024]{1,0:T(8,128)(2,1)} %convert_element_type.170, bf16[2048,1024]{1,0:T(8,128)(2,1)} %bitcast.636, pred[]{:T(512)S(6)} %eq.6, f32[512,1024]{1,0:T(8,128)} %param.35, ...), kind=kOutput, calls=%fused_computation.427 | convolution fusion | flops 4379897856 | bytes 23095296 | tf_op jit(solution)/shard_map/dot_general | solution.py:117
  376.7 24.2 %while.124 = (s32[]{:T(128)}, f32[4,512,64]{1,2,0:T(8,128)S(1)}, f32[4,1024,64]{1,2,0:T(8,128)S(1)}, f32[4,1024,64]{1,2,0:T(8,128)}, bf16[4,512,64]{2,1,0:T(8,12...) while((s32[]{:T(128)}, f32[4,512,64]{1,2,0:T(8,128)S(1)}, ...), condition=%wide.region_24.25_spmd.clone.clone, body=%wide.region_22.24_spmd.clone.clone.sunk | while | flops 343506432 | bytes 18634940 | solution.py:316
  408.4 29.8 %while.125 = (s32[]{:T(128)}, f32[4,512,64]{1,2,0:T(8,128)S(1)}, f32[4,1024,64]{1,2,0:T(8,128)}, f32[4,1024,64]{1,2,0:T(8,128)}, bf16[4,512,64]{2,1,0:T(8,128)(2...) while((s32[]{:T(128)}, f32[4,512,64]{1,2,0:T(8,128)S(1)}, ...), condition=%wide.region_27.28_spmd.clone.clone, body=%wide.region_25.27_spmd.clone.clone.sunk | while | flops 343506432 | bytes 18634940 | solution.py:316
  446.9 29.7 %while.126 = (s32[]{:T(128)}, f32[4,512,64]{1,2,0:T(8,128)S(1)}, f32[4,1024,64]{1,2,0:T(8,128)}, f32[4,1024,64]{1,2,0:T(8,128)}, bf16[4,512,64]{2,1,0:T(8,128)(2...) while((s32[]{:T(128)}, f32[4,512,64]{1,2,0:T(8,128)S(1)}, ...), condition=%wide.region_30.31_spmd.clone.clone, body=%wide.region_28.30_spmd.clone.clone.sunk | while | flops 343506432 | bytes 18634940 | solution.py:316
  485.2 30.0 %while.127 = (s32[]{:T(128)}, f32[4,512,64]{1,2,0:T(8,128)S(1)}, f32[4,1024,64]{1,2,0:T(8,128)}, f32[4,1024,64]{1,2,0:T(8,128)}, bf16[4,512,64]{2,1,0:T(8,128)(2...) while((s32[]{:T(128)}, f32[4,512,64]{1,2,0:T(8,128)S(1)}, ...), condition=%wide.region_33.34_spmd.clone.clone, body=%wide.region_31.33_spmd.clone.clone.sunk | while | flops 343506432 | bytes 18634940 | solution.py:316
  529.2 28.1 %collective-permute-done.7 = bf16[512,512]{0,1:T(8,128)(2,1)S(1)} collective-permute-done((bf16[512,512]{0,1:T(8,128)(2,1)S(1)}, bf16[512,512]{0,1:T(8,128)(2,1)S(1)}, u32[]{:S(2)}, u32[]{:S(2)}) %collective-permute-start.7) | collective-permute-done | bytes 524320 | tf_op jit(solution)/shard_map/ppermute | solution.py:22
  635.6 14.2 %pad_maximum_fusion = bf16[2,8,2,288,1024]{4,3,2,1,0:T(8,128)(2,1)} fusion(bf16[2,8,2,128,1024]{4,3,2,1,0:T(8,128)(2,1)} %bitcast.610, bf16[2,8,2,128,1024]{4,3,2,1,0:T(8,128)(2,1)} %bitcast.609, bf16[2,8,2,32,1024]{4,3,2,1,0:T(8,128)(2,1)S(1)} %bitcast.618), kind=kLoop, calls=%fused_computation.232 | loop fusion | flops 56623104 | bytes 37748736 | tf_op jit(solution)/shard_map/concatenate | solution.py:69
  653.6 26.4 %reduce-scatter.13.cloned.1.call-done = bf16[1,4608,1024]{2,1,0:T(8,128)(2,1)} async-done(((bf16[2,4608,1024]{2,1,0:T(8,128)(2,1)}), bf16[1,4608,1024]{2,1,0:T(8,128)(2,1)}) %reduce-scatter.13.cloned.1.call-update) | async-done | bytes 9437200 | tf_op jit(solution)/shard_map/reduce_scatter | solution.py:73
  680.0 83.6 %reduce-scatter.9.cloned.1.call-done = bf16[1,66,3072]{2,1,0:T(8,128)(2,1)} async-done(((bf16[8,66,3072]{2,1,0:T(8,128)(2,1)}), bf16[1,66,3072]{2,1,0:T(8,128)(2,1)}) %reduce-scatter.9.cloned.1.call-update) | async-done | bytes 405520 | tf_op jit(solution)/shard_map/reduce_scatter | solution.py:75
  765.5 162.5 %reduce-scatter.15.cloned.1.call-done = bf16[1,576,1024]{2,1,0:T(8,128)(2,1)} async-done(((bf16[8,576,1024]{2,1,0:T(8,128)(2,1)}), bf16[1,576,1024]{2,1,0:T(8,128)(2,1)}) %reduce-scatter.15.cloned.1.call-update) | async-done | bytes 1179664 | tf_op jit(solution)/shard_map/reduce_scatter | solution.py:75
  928.1 17.5 %reduce-scatter.11.cloned.1.call-done = bf16[1,33,3072]{2,1,0:T(8,128)(2,1)} async-done(((bf16[2,33,3072]{2,1,0:T(8,128)(2,1)}), bf16[1,33,3072]{2,1,0:T(8,128)(2,1)}) %reduce-scatter.11.cloned.1.call-update) | async-done | bytes 202768 | tf_op jit(solution)/shard_map/reduce_scatter | solution.py:77
  947.7 21.9 %reduce-scatter.17.cloned.1.call-done = bf16[1,288,1024]{2,1,0:T(8,128)(2,1)} async-done(((bf16[2,288,1024]{2,1,0:T(8,128)(2,1)}), bf16[1,288,1024]{2,1,0:T(8,128)(2,1)}) %reduce-scatter.17.cloned.1.call-update) | async-done | bytes 589840 | tf_op jit(solution)/shard_map/reduce_scatter | solution.py:77
  969.6 62.4 %all-gather.24.cloned.1.call-done = bf16[1,264,3072]{2,0,1:T(2,128)(2,1)} async-done(((bf16[1,33,3072]{2,0,1:T(2,128)(2,1)}), bf16[1,264,3072]{2,0,1:T(2,128)(2,1)}) %all-gather.24.cloned.1.call-update) | async-done | bytes 1622032 | tf_op jit(solution)/shard_map/all_gather | solution.py:79
  1035.7 75.6 %all-gather.28.cloned.1.call-done = bf16[1,2304,1024]{2,1,0:T(8,128)(2,1)} async-done(((bf16[1,288,1024]{2,1,0:T(8,128)(2,1)}), bf16[1,2304,1024]{2,1,0:T(8,128)(2,1)}) %all-gather.28.cloned.1.call-update) | async-done | bytes 4718608 | tf_op jit(solution)/shard_map/all_gather | solution.py:79
  1112.9 15.0 %add_add_fusion = f32[512,1024]{1,0:T(8,128)} fusion(f32[512,1024]{1,0:T(8,128)S(1)} %copy-done.7, bf16[2048,1024]{1,0:T(8,128)(2,1)} %convert_element_type.170, bf16[2048,1024]{1,0:T(8,128)(2,1)} %bitcast.637, pred[]{:T(512)S(6)} %eq.6, f32[1024]{0:T(1024)S(1)} %bitcast.693, f32[512,4096]{1,0:T(8,128)} %fusion.221, f32[4096]{0:T(1024)S(1)} %bitcast.692), kind=kOutput, calls=%fused_computation.289 | convolution fusion | flops 4354736128 | bytes 20992000 | tf_op jit(solution)/shard_map/dot_general | solution.py:271
  1135.7 17.2 %multiply_add_fusion.2 = (f32[512,3072]{1,0:T(8,128)}, f32[512,3072]{1,0:T(8,128)}, f32[512,3072]{1,0:T(8,128)}) fusion(f32[512,3072]{1,0:T(8,128)} %param.39, f32[512,3072]{1,0:T(8,128)} %param.37, bf16[16,32,3072]{2,1,0:T(8,128)(2,1)S(1)} %slice.403, f32[512,3072]{1,0:T(8,128)} %param.38), kind=kLoop, calls=%fused_computation.263 | loop fusion | flops 15728640 | bytes 40894464 | tf_op jit(solution)/shard_map/add | solution.py:151
  1179.2 22.3 %multiply_add_fusion.1 = (f32[1024,2048]{1,0:T(8,128)}, f32[1024,2048]{1,0:T(8,128)}, f32[1024,2048]{1,0:T(8,128)}) fusion(f32[1024,2048]{1,0:T(8,128)} %param.45, f32[1024,2048]{1,0:T(8,128)} %param.43, f32[2048,1024]{0,1:T(8,128)} %copy.304, f32[1024,2048]{1,0:T(8,128)} %param.44), kind=kLoop, calls=%fused_computation.254 | loop fusion | flops 18874368 | bytes 58720256 | tf_op jit(solution)/shard_map/add | solution.py:151
  1201.6 18.6 %multiply_add_fusion = (f32[2048,1024]{1,0:T(8,128)}, f32[2048,1024]{1,0:T(8,128)}, f32[2048,1024]{1,0:T(8,128)}) fusion(f32[2048,1024]{1,0:T(8,128)} %param.48, f32[2048,1024]{1,0:T(8,128)} %param.46, bf16[16,128,1024]{2,1,0:T(8,128)(2,1)} %get-tuple-element.1702, f32[2048,1024]{1,0:T(8,128)} %param.47), kind=kLoop, calls=%fused_computation.253 | loop fusion | flops 20971520 | bytes 54525952 | tf_op jit(solution)/shard_map/add | solution.py:151
  (728 shorter events, 560.7 us)
Async XLA Ops:
  7.2 60.9 %all-gather.32.cloned.1.call-start = ((), (), s32[]{:S(2)}) async-start(), calls=%async_computation.19 | async-start | bytes 2211840 | tf_op jit(solution)/shard_map/all_gather | solution.py:44
  11.5 6.9 collective-permute-start
  19.1 82.3 %all-gather.18.cloned.1.call-start = ((), (), s32[]{:S(2)}) async-start(), calls=%async_computation.12 | async-start | bytes 4866048 | tf_op jit(solution)/shard_map/all_gather | solution.py:45
  71.8 146.1 %all-gather.20.cloned.1.call-start = ((), (), s32[]{:S(2)}) async-start(), calls=%async_computation.13 | async-start | bytes 5308416 | tf_op jit(solution)/shard_map/all_gather | solution.py:44
  87.3 13.3 %collective-permute-start.5 = (bf16[288,1024]{1,0:T(8,128)(2,1)S(1)}, bf16[288,1024]{1,0:T(8,128)(2,1)S(1)}, u32[]{:S(2)}, u32[]{:S(2)}) collective-permute-start(bf16[288,1024]{1,0:T(8,128)(2,1)S(1)} %pad_maximum_fusion.3), channel_id=1, source_target_pairs={{0,1},{1,0},{2,3},{3,2},{4,5},{5,4},{6,7},{7,6},{8,9},{9,8},{10,11... | collective-permute-start | bytes 1769480 | tf_op jit(solution)/shard_map/ppermute | solution.py:43
  101.4 187.9 %all-gather.22.cloned.1.call-start = ((), (), s32[]{:S(2)}) async-start(), calls=%async_computation.14 | async-start | bytes 14155776 | tf_op jit(solution)/shard_map/all_gather | solution.py:45
  117.9 27.5 %collective-permute-start.2 = (bf16[512,512]{1,0:T(8,128)(2,1)}, bf16[512,512]{1,0:T(8,128)(2,1)}, u32[]{:S(2)}, u32[]{:S(2)}) collective-permute-start(bf16[512,512]{1,0:T(8,128)(2,1)} %pad_maximum_fusion.7), channel_id=1, source_target_pairs={{0,1},{2,3},{4,5},{6,7},{8,9},{10,11},{12,13},{14,15},{16,17},{18,... | collective-permute-start | bytes 1572872 | tf_op jit(solution)/shard_map/ppermute | solution.py:22
  136.3 22.5 %collective-permute-start.3 = (bf16[512,512]{1,0:T(8,128)(2,1)}, bf16[512,512]{1,0:T(8,128)(2,1)}, u32[]{:S(2)}, u32[]{:S(2)}) collective-permute-start(bf16[512,512]{1,0:T(8,128)(2,1)} %pad_maximum_fusion.10), channel_id=1, source_target_pairs={{0,1},{2,3},{4,5},{6,7},{8,9},{10,11},{12,13},{14,15},{16,17},{18,... | collective-permute-start | bytes 1572872 | tf_op jit(solution)/shard_map/ppermute | solution.py:22
  140.1 75.7 %collective-permute-start.4 = (bf16[512,512]{1,0:T(8,128)(2,1)}, bf16[512,512]{1,0:T(8,128)(2,1)}, u32[]{:S(2)}, u32[]{:S(2)}) collective-permute-start(bf16[512,512]{1,0:T(8,128)(2,1)} %pad_maximum_fusion.13), channel_id=1, source_target_pairs={{0,1},{2,3},{4,5},{6,7},{8,9},{10,11},{12,13},{14,15},{16,17},{18,... | collective-permute-start | bytes 1572872 | tf_op jit(solution)/shard_map/ppermute | solution.py:22
  143.1 82.2 %collective-permute-start.1 = (bf16[512,512]{1,0:T(8,128)(2,1)}, bf16[512,512]{1,0:T(8,128)(2,1)}, u32[]{:S(2)}, u32[]{:S(2)}) collective-permute-start(bf16[512,512]{1,0:T(8,128)(2,1)} %pad_maximum_fusion.4), channel_id=1, source_target_pairs={{0,1},{2,3},{4,5},{6,7},{8,9},{10,11},{12,13},{14,15},{16,17},{18,... | collective-permute-start | bytes 1572872 | tf_op jit(solution)/shard_map/ppermute | solution.py:22
  218.0 431.9 %reduce-scatter.7.cloned.1.call-start = ((), (), s32[]{:S(2)}) async-start(), calls=%async_computation.6 | async-start | bytes 9732096 | tf_op jit(solution)/shard_map/reduce_scatter | solution.py:73
  522.3 47.8 %collective-permute-start.9 = (bf16[512,512]{0,1:T(8,128)(2,1)S(1)}, bf16[512,512]{0,1:T(8,128)(2,1)S(1)}, u32[]{:S(2)}, u32[]{:S(2)}) collective-permute-start(bf16[512,512]{0,1:T(8,128)(2,1)S(1)} %pad_maximum_fusion.19), channel_id=1, source_target_pairs={{1,0},{3,2},{5,4},{7,6},{9,8},{11,10},{13,12},{15,14},{17,16},{19,... | collective-permute-start | bytes 1572872 | tf_op jit(solution)/shard_map/ppermute | solution.py:22
  524.8 44.1 %collective-permute-start.8 = (bf16[512,512]{0,1:T(8,128)(2,1)S(1)}, bf16[512,512]{0,1:T(8,128)(2,1)S(1)}, u32[]{:S(2)}, u32[]{:S(2)}) collective-permute-start(bf16[512,512]{0,1:T(8,128)(2,1)S(1)} %pad_maximum_fusion.18), channel_id=1, source_target_pairs={{1,0},{3,2},{5,4},{7,6},{9,8},{11,10},{13,12},{15,14},{17,16},{19,... | collective-permute-start | bytes 1572872 | tf_op jit(solution)/shard_map/ppermute | solution.py:22
  526.2 31.0 %collective-permute-start.7 = (bf16[512,512]{0,1:T(8,128)(2,1)S(1)}, bf16[512,512]{0,1:T(8,128)(2,1)S(1)}, u32[]{:S(2)}, u32[]{:S(2)}) collective-permute-start(bf16[512,512]{0,1:T(8,128)(2,1)S(1)} %pad_maximum_fusion.17), channel_id=1, source_target_pairs={{1,0},{3,2},{5,4},{7,6},{9,8},{11,10},{13,12},{15,14},{17,16},{19,... | collective-permute-start | bytes 1572872 | tf_op jit(solution)/shard_map/ppermute | solution.py:22
  527.6 40.9 %collective-permute-start.6 = (bf16[512,512]{0,1:T(8,128)(2,1)S(1)}, bf16[512,512]{0,1:T(8,128)(2,1)S(1)}, u32[]{:S(2)}, u32[]{:S(2)}) collective-permute-start(bf16[512,512]{0,1:T(8,128)(2,1)S(1)} %pad_maximum_fusion.16), channel_id=1, source_target_pairs={{1,0},{3,2},{5,4},{7,6},{9,8},{11,10},{13,12},{15,14},{17,16},{19,... | collective-permute-start | bytes 1572872 | tf_op jit(solution)/shard_map/ppermute | solution.py:22
  615.5 64.4 %reduce-scatter.13.cloned.1.call-start = ((), (), s32[]{:S(2)}) async-start(), calls=%async_computation.9 | async-start | bytes 28311552 | tf_op jit(solution)/shard_map/reduce_scatter | solution.py:73
  649.8 113.8 %reduce-scatter.9.cloned.1.call-start = ((), (), s32[]{:S(2)}) async-start(), calls=%async_computation.7 | async-start | bytes 3981312 | tf_op jit(solution)/shard_map/reduce_scatter | solution.py:75
  653.5 274.5 %reduce-scatter.15.cloned.1.call-start = ((), (), s32[]{:S(2)}) async-start(), calls=%async_computation.10 | async-start | bytes 10616832 | tf_op jit(solution)/shard_map/reduce_scatter | solution.py:75
  680.0 265.7 %reduce-scatter.11.cloned.1.call-start = ((), (), s32[]{:S(2)}) async-start(), calls=%async_computation.8 | async-start | bytes 737280 | tf_op jit(solution)/shard_map/reduce_scatter | solution.py:77
  765.5 204.1 %reduce-scatter.17.cloned.1.call-start = ((), (), s32[]{:S(2)}) async-start(), calls=%async_computation.11 | async-start | bytes 1769472 | tf_op jit(solution)/shard_map/reduce_scatter | solution.py:77
  928.1 104.0 %all-gather.24.cloned.1.call-start = ((), (), s32[]{:S(2)}) async-start(), calls=%async_computation.15 | async-start | bytes 3649536 | tf_op jit(solution)/shard_map/all_gather | solution.py:79
  947.6 163.6 %all-gather.28.cloned.1.call-start = ((), (), s32[]{:S(2)}) async-start(), calls=%async_computation.17 | async-start | bytes 5308416 | tf_op jit(solution)/shard_map/all_gather | solution.py:79
  969.6 158.3 %all-gather.26.cloned.1.call-start = ((), (), s32[]{:S(2)}) async-start(), calls=%async_computation.16 | async-start | bytes 4866048 | tf_op jit(solution)/shard_map/all_gather | solution.py:80
  1035.7 117.2 %all-gather.30.cloned.1.call-start = ((), (), s32[]{:S(2)}) async-start(), calls=%async_computation.18 | async-start | bytes 14155776 | tf_op jit(solution)/shard_map/all_gather | solution.py:80
  (121 other events, 910.4 us)
Sparse Core Ops, SparseCore 0:
  19.2 48.8 all-gather.31
  71.9 12.4 all-gather.17
  101.5 78.4 all-gather.19
  218.1 23.5 all-gather.21
  615.6 17.7 reduce-scatter.6
  649.9 30.0 reduce-scatter.12
  684.1 79.3 reduce-scatter.8
  767.2 160.8 reduce-scatter.14
  930.9 14.6 reduce-scatter.10
  947.7 21.8 reduce-scatter.16
  972.3 59.7 all-gather.23
  1034.1 77.1 all-gather.27
  1113.4 13.7 all-gather.25
  1128.6 22.7 all-gather.29

commit v6 on v5

--- a/solution.py
+++ b/solution.py
@@ -14,6 +14,9 @@
 MOMENTUM = 0.9
 AVERAGING = 0.9
 NEG_FILL = -1e30
+SHARD = "shard"
+OUTER = "outer"
+CORE = "core"
 
 
 def passed_along(value, axis, steps):
@@ -32,17 +35,17 @@
 
 
 def gather_rows(row_arrays):
-    cores = lax.axis_size("core")
-    outer = lax.axis_size("outer")
+    cores = lax.axis_size(CORE)
+    outer = lax.axis_size(OUTER)
     blocks = cores * outer
-    place = lax.axis_index("core") * outer + lax.axis_index("outer")
+    place = lax.axis_index(CORE) * outer + lax.axis_index(OUTER)
     heights = [piece.shape[1] for piece in row_arrays]
     mine = jnp.concatenate(
         [lax.dynamic_index_in_dim(piece, place, 0, keepdims=False) for piece in row_arrays], 0
     )
-    other = lax.ppermute(mine, "shard", [(0, 1), (1, 0)])
-    got = lax.all_gather(other, "outer", axis=0, tiled=False)
-    got = lax.all_gather(got, "core", axis=0, tiled=False)
+    other = lax.ppermute(mine, SHARD, [(0, 1), (1, 0)])
+    got = lax.all_gather(other, OUTER, axis=0, tiled=False)
+    got = lax.all_gather(got, CORE, axis=0, tiled=False)
     got = got.reshape(blocks, -1, got.shape[-1])
     pieces = []
     offset = 0
@@ -53,31 +56,29 @@
 
 
 def join_halves(own, other, dim):
-    upper = lax.axis_index("shard") == 1
+    upper = lax.axis_index(SHARD) == 1
     in_order = jnp.concatenate([own, other], axis=dim)
     swapped = jnp.concatenate([other, own], axis=dim)
     return jnp.where(upper, swapped, in_order)
 
 
 def reduce_rows(row_grads):
-    shard_count = lax.axis_size("shard")
-    cores = lax.axis_size("core")
-    outer = lax.axis_size("outer")
+    shard_count = lax.axis_size(SHARD)
+    cores = lax.axis_size(CORE)
+    outer = lax.axis_size(OUTER)
     blocks = cores * outer
     heights = [piece.shape[3] for piece in row_grads]
     width = row_grads[0].shape[-1]
-    stacked = jnp.concatenate(
-        [piece.astype(jnp.bfloat16).transpose(1, 2, 0, 3, 4) for piece in row_grads], 3
-    )
+    stacked = jnp.concatenate([piece.astype(jnp.bfloat16) for piece in row_grads], 3)
     stacked = stacked.reshape(cores, -1, width)
-    stacked = lax.psum_scatter(stacked, "core", scatter_dimension=0, tiled=True)
+    stacked = lax.psum_scatter(stacked, CORE, scatter_dimension=0, tiled=True)
     stacked = stacked.reshape(outer, -1, width)
-    stacked = lax.psum_scatter(stacked, "outer", scatter_dimension=0, tiled=True)
+    stacked = lax.psum_scatter(stacked, OUTER, scatter_dimension=0, tiled=True)
     stacked = stacked.reshape(shard_count, -1, width)
-    stacked = lax.psum_scatter(stacked, "shard", scatter_dimension=0, tiled=True)
+    stacked = lax.psum_scatter(stacked, SHARD, scatter_dimension=0, tiled=True)
     stacked = stacked.reshape(stacked.shape[1:])
-    stacked = lax.all_gather(stacked, "outer", axis=0, tiled=True)
-    stacked = lax.all_gather(stacked, "core", axis=0, tiled=True)
+    stacked = lax.all_gather(stacked, OUTER, axis=0, tiled=True)
+    stacked = lax.all_gather(stacked, CORE, axis=0, tiled=True)
     stacked = stacked.reshape(blocks, -1, width)
     pieces = []
     offset = 0
@@ -88,11 +89,44 @@
 
 
 def split_rows(grad_full):
-    shard_count = lax.axis_size("shard")
-    cores = lax.axis_size("core")
-    outer = lax.axis_size("outer")
+    shard_count = lax.axis_size(SHARD)
+    cores = lax.axis_size(CORE)
+    outer = lax.axis_size(OUTER)
     rows, cols = grad_full.shape
-    return grad_full.reshape(shard_count, cores, outer, rows // (shard_count * cores * outer), cols)
+    split = grad_full.reshape(shard_count, cores, outer, rows // (shard_count * cores * outer), cols)
+    return split.transpose(1, 2, 0, 3, 4)
+
+
+def block_major(grad_perm):
+    shard_count = lax.axis_size(SHARD)
+    cores = lax.axis_size(CORE)
+    outer = lax.axis_size(OUTER)
+    rows, cols = grad_perm.shape
+    return grad_perm.reshape(cores, outer, shard_count, rows // (shard_count * cores * outer), cols)
+
+
+def ff_order(values, blocks):
+    shard_count = lax.axis_size(SHARD)
+    rest = values.shape[1:]
+    split = values.reshape((shard_count, blocks, values.shape[0] // (shard_count * blocks)) + rest)
+    return jnp.swapaxes(split, 0, 1).reshape(values.shape)
+
+
+def ff_natural(values, blocks):
+    shard_count = lax.axis_size(SHARD)
+    rest = values.shape[1:]
+    split = values.reshape((blocks, shard_count, values.shape[0] // (shard_count * blocks)) + rest)
+    return jnp.swapaxes(split, 0, 1).reshape(values.shape)
+
+
+def join_blocks(own, other, blocks):
+    upper = lax.axis_index(SHARD) == 1
+    own_b = own.reshape((blocks, -1) + own.shape[1:])
+    other_b = other.reshape((blocks, -1) + other.shape[1:])
+    in_order = jnp.stack([own_b, other_b], 1)
+    swapped = jnp.stack([other_b, own_b], 1)
+    joined = jnp.where(upper, swapped, in_order)
+    return joined.reshape((2 * own.shape[0],) + own.shape[1:])
 
 
 def norm_stats(field_in):
@@ -174,10 +208,10 @@
 ):
     tok_rows = tokens.shape[0]
     model_width = tokens.shape[1]
-    shard_count = lax.axis_size("shard")
-    group_count = lax.axis_size("outer") * lax.axis_size("core")
-    shard_place = lax.axis_index("shard")
-    group_place = lax.axis_index("outer") * lax.axis_size("core") + lax.axis_index("core")
+    shard_count = lax.axis_size(SHARD)
+    group_count = lax.axis_size(OUTER) * lax.axis_size(CORE)
+    shard_place = lax.axis_index(SHARD)
+    group_place = lax.axis_index(OUTER) * lax.axis_size(CORE) + lax.axis_index(CORE)
     upper_half = shard_place % 2
     seq_place = group_place * (shard_count // 2) + shard_place // 2
     seq_length = lax.dynamic_index_in_dim(lengths, seq_place, 0, keepdims=False)
@@ -192,7 +226,7 @@
     head_size = model_width // HEADS
     score_scale = head_size ** (-0.5)
     slopes = 2.0 ** (-8.0 * (jnp.arange(HEADS, dtype=jnp.float32) + 1.0) / HEADS)
-    blocks = lax.axis_size("core") * lax.axis_size("outer")
+    blocks = lax.axis_size(CORE) * lax.axis_size(OUTER)
     qkv_own = qkv_weight.astype(jnp.bfloat16)
     small_own = small_params.astype(jnp.bfloat16)
     qkv_other, small_other = gather_rows(
@@ -209,10 +243,10 @@
         [piece.reshape(blocks, -1, piece.shape[1]) for piece in (out_own, up_own_t, down_own)],
     )
     out_full = join_halves(out_own, out_other.reshape(out_own.shape), 0)
-    up_full_t = join_halves(up_own_t, up_other_t.reshape(up_own_t.shape), 0)
-    down_full = join_halves(down_own, down_other.reshape(down_own.shape), 0)
+    up_full_t = join_blocks(up_own_t, up_other_t.reshape(up_own_t.shape), blocks)
+    down_full = join_blocks(down_own, down_other.reshape(down_own.shape), blocks)
     table = small_full.astype(jnp.float32)
-    up_bias = table[8:12].reshape(FF)
+    up_bias = ff_order(table[8:12].reshape(FF), blocks)
     normed_one, inverse_one = norm_stats(tokens)
     entry_low = (normed_one * table[0] + table[1]).astype(jnp.bfloat16)
     mapped = jnp.dot(entry_low, qkv_full, preferred_element_type=jnp.float32)
@@ -226,7 +260,7 @@
     for group in range(groups):
         cols = slice(group * group_width, (group + 1) * group_width)
         received = passed_along(
-            jnp.concatenate([key_own[:, cols], value_own[:, cols]], 1), "shard", 1
+            jnp.concatenate([key_own[:, cols], value_own[:, cols]], 1), SHARD, 1
         )
         query_groups.append(split_heads_n(queries[:, cols], per_group))
         key_groups.append(
@@ -273,7 +307,7 @@
     grad_act = contract_cols(grad_low, down_full)
     down_grad = contract_rows(act_low, grad_low)
     grad_pre = gelu_back(pre_act, grad_act)
-    up_bias_grad = jnp.sum(grad_pre, axis=0)
+    up_bias_grad = ff_natural(jnp.sum(grad_pre, axis=0), blocks)
     pre_low = grad_pre.astype(jnp.bfloat16)
     up_grad_t = contract_rows(pre_low, inner_low)
     grad_inner = jnp.dot(pre_low, up_full_t, preferred_element_type=jnp.float32)
@@ -286,7 +320,7 @@
         (grad_resid, resid_low, up_grad_t, down_grad, out_grad)
     )
     out_sum, up_sum_t, down_sum = reduce_rows(
-        [split_rows(out_grad), split_rows(up_grad_t), split_rows(down_grad)]
+        [split_rows(out_grad), block_major(up_grad_t), block_major(down_grad)]
     )
     out_total = out_sum.reshape(out_weight.shape)
     up_total = up_sum_t.reshape(up_weight.shape[::-1]).T
@@ -328,7 +362,7 @@
             jnp.concatenate(
                 [merge_heads(group_keys[:, :tok_rows]), merge_heads(group_values[:, :tok_rows])], 1
             ).astype(jnp.bfloat16),
-            "shard",
+            SHARD,
             -1,
         ).astype(jnp.float32)
         query_parts.append(merge_heads(group_query))
@@ -361,7 +395,8 @@
     small_halves = small_grad.reshape(small_grad.shape[0], shard_count, -1).transpose(1, 0, 2)
     small_packed = jnp.stack(
         [small_rows(small_halves[index], blocks) for index in range(shard_count)]
-    ).reshape(shard_count, lax.axis_size("core"), lax.axis_size("outer"), 1, SMALL_WIDTH)
+    ).reshape(shard_count, lax.axis_size(CORE), lax.axis_size(OUTER), 1, SMALL_WIDTH)
+    small_packed = small_packed.transpose(1, 2, 0, 3, 4)
     qkv_sum, small_sum = reduce_rows([split_rows(qkv_grad), small_packed])
     qkv_total = qkv_sum.reshape(qkv_weight.shape)
     small_total = small_sum.reshape(-1)[: small_params.size].reshape(small_params.shape)
@@ -394,47 +429,47 @@
 
 def solution(mesh):
     cores = 2
-    devices = mesh.devices.reshape(mesh.shape["group"] // cores, cores, mesh.shape["shard"])
-    inner_mesh = jax.sharding.Mesh(devices, ("outer", "core", "shard"))
-    rows = P(("outer", "core", "shard"), None)
+    devices = mesh.devices.reshape(mesh.shape["group"] // cores, cores, mesh.shape[SHARD])
+    inner_mesh = jax.sharding.Mesh(devices, (OUTER, CORE, SHARD))
+    rows = P((OUTER, CORE, SHARD), None)
     in_specs = (
         rows,
         rows,
         P(),
-        P("shard", None),
-        P("shard", None),
-        P("shard", None),
-        P("shard", None),
-        P("shard", None),
-        P("shard", None),
-        P(None, "shard"),
-        P(None, "shard"),
-        P(None, "shard"),
-        P("shard", None),
-        P("shard", None),
-        P("shard", None),
-        P(None, "shard"),
-        P(None, "shard"),
-        P(None, "shard"),
+        P(SHARD, None),
+        P(SHARD, None),
+        P(SHARD, None),
+        P(SHARD, None),
+        P(SHARD, None),
+        P(SHARD, None),
+        P(None, SHARD),
+        P(None, SHARD),
+        P(None, SHARD),
+        P(SHARD, None),
+        P(SHARD, None),
+        P(SHARD, None),
+        P(None, SHARD),
+        P(None, SHARD),
+        P(None, SHARD),
     )
     out_specs = (
         rows,
         rows,
-        P("shard", None),
-        P("shard", None),
-        P("shard", None),
-        P("shard", None),
-        P("shard", None),
-        P("shard", None),
-        P(None, "shard"),
-        P(None, "shard"),
-        P(None, "shard"),
-        P("shard", None),
-        P("shard", None),
-        P("shard", None),
-        P(None, "shard"),
-        P(None, "shard"),
-        P(None, "shard"),
+        P(SHARD, None),
+        P(SHARD, None),
+        P(SHARD, None),
+        P(SHARD, None),
+        P(SHARD, None),
+        P(SHARD, None),
+        P(None, SHARD),
+        P(None, SHARD),
+        P(None, SHARD),
+        P(SHARD, None),
+        P(SHARD, None),
+        P(SHARD, None),
+        P(None, SHARD),
+        P(None, SHARD),
+        P(None, SHARD),
     )
 
     return jax.shard_map(body, mesh=inner_mesh, in_specs=in_specs, out_specs=out_specs, check_vma=False)

time: 1240 us -> 1200 us (0.968)
  local copies, waits for them, and re-layouts: 228 us -> 203 us
  matrix products: 266 us -> 249 us
    convert_element_type x4 -> x3, local copies, waits for them, and re-layouts: 30.4 us -> 12.4 us  [reduce_rows(): piece.astype(jnp.bfloat16)]
    unnamed x221 -> x212, local copies, waits for them, and re-layouts: 48.3 us -> 40.3 us
  transfers between devices with their start and end apart: 24 -> 24, of which waited for: 11 -> 12; matrix products, arithmetic and copies ran while one was open for 23% -> 21% of each run, Pallas kernels for 0% -> 0%
where the time goes in v6:
time: 1200 us; the launch traced here: 1190 us
  waiting for transfers between devices  546 us (46%)
  matrix products  249 us (21%)
  local copies, waits for them, and re-layouts  203 us (17%)
  other arithmetic  157 us (13%)
  starting transfers between devices  18.2 us (2%)
  between operations  15.6 us (1%)
    reduce_scatter x2, waiting for transfers between devices, reduce_rows(): stacked = lax.psum_scatter(stacked, OUTER, scatter_dimension=0, tiled=True)  246 us
    all_gather x2, waiting for transfers between devices, reduce_rows(): stacked = lax.all_gather(stacked, OUTER, axis=0, tiled=True)  138 us
    dot_general x52, matrix products, contract_cols(): lax.dot_general(left_side, right_side, (((1,), (1,)), ((), ())), preferre...  127 us
    add x5, other arithmetic, nesterov(): average_new = AVERAGING * average_old + (1.0 - AVERAGING) * weight_new  64.8 us
    dot_general x36, matrix products, contract_rows(): lax.dot_general(left_side, right_side, (((0,), (0,)), ((), ())), preferre...  59.9 us
    all_gather x2, waiting for transfers between devices, gather_rows(): got = lax.all_gather(other, OUTER, axis=0, tiled=False)  49 us
    unnamed x212, local copies, waits for them, and re-layouts  40.3 us
    reduce_scatter x2, waiting for transfers between devices, reduce_rows(): stacked = lax.psum_scatter(stacked, SHARD, scatter_dimension=0, tiled=True)  39.3 us
  transfers between devices with their start and end apart: 24, of which 12 were waited for; matrix products, arithmetic and copies ran while one was open for 21% of the time, Pallas kernels for 0%

profile of v6, /device:TPU:9, one launch (start us, length us, event | category | flops | bytes accessed | tf_op | source)
XLA Modules:
  0.0 1189.8 jit_solution(1100778352072112172)
XLA Ops:
  19.2 49.0 %all-gather.32.cloned.1.call-done = bf16[8,33,3072]{2,1,0:T(8,128)(2,1)} async-done(((bf16[1,33,3072]{2,1,0:T(8,128)(2,1)}), bf16[8,33,3072]{2,1,0:T(8,128)(2,1)}) %all-gather.32.cloned.1.call-update) | async-done | bytes 1622032 | tf_op jit(solution)/shard_map/all_gather | solution.py:47
  164.0 21.6 %while.121 = (s32[]{:T(128)}, bf16[4,512,64]{1,2,0:T(8,128)(2,1)S(1)}, f32[4,512]{1,0:T(4,128)S(1)}, bf16[4,512,64]{2,1,0:T(8,128)(2,1)}, bf16[4,1024,64]{2,1,0:...) while((s32[]{:T(128)}, ...), condition=%wide.region_9.10_spmd.clone.clone, body=%wide.region_6.9_spmd.clone.clone.sunk | while | flops 141557248 | bytes 7108237 | solution.py:287
  186.4 21.3 %while.122 = (s32[]{:T(128)}, bf16[4,512,64]{1,2,0:T(8,128)(2,1)S(1)}, f32[4,512]{1,0:T(4,128)S(1)}, bf16[4,512,64]{2,1,0:T(8,128)(2,1)S(1)}, bf16[4,1024,64]{2,...) while((s32[]{:T(128)}, ...), condition=%wide.region_13.14_spmd.clone.clone, body=%wide.region_10.13_spmd.clone.clone.sunk | while | flops 141557248 | bytes 7108237 | solution.py:287
  230.8 21.1 %while.123 = (s32[]{:T(128)}, bf16[4,512,64]{1,2,0:T(8,128)(2,1)S(1)}, f32[4,512]{1,0:T(4,128)S(1)}, bf16[4,512,64]{2,1,0:T(8,128)(2,1)}, bf16[4,1024,64]{2,1,0:...) while((s32[]{:T(128)}, ...), condition=%wide.region_17.18_spmd.clone.clone, body=%wide.region_14.17_spmd.clone.clone.sunk | while | flops 141557248 | bytes 7108237 | solution.py:287
  252.9 25.9 %while.120 = (s32[]{:T(128)}, bf16[4,512,64]{1,2,0:T(8,128)(2,1)}, f32[4,512]{1,0:T(4,128)S(1)}, bf16[4,512,64]{2,1,0:T(8,128)(2,1)}, bf16[4,1024,64]{2,1,0:T(8,...) while((s32[]{:T(128)}, bf16[4,512,64]{1,2,0:T(8,128)(2,1)}, ...), condition=%wide.region_5.6_spmd.clone.clone, body=%wide.region_2.5_spmd.clone.clone.sunk | while | flops 141557248 | bytes 9205445 | solution.py:287
  294.5 13.8 %fusion.234 = f32[512,4096]{1,0:T(8,128)} fusion(bf16[4096,1024]{1,0:T(8,128)(2,1)} %bitcast.629, f32[512,1024]{1,0:T(8,128)S(1)} %get-tuple-element.1762, f32[1024]{0:T(1024)S(1)} %bitcast.702, f32[1024]{0:T(1024)S(1)} %bitcast.689, f32[512]{0:T(512)S(1)} %add_rsqrt_fusion, f32[512]{0:T(512)S(1)} %broadcast_multiply_fusion.4), kind=kOutput, calls=%fused_computation.400 | convolution fusion | flops 4297588736 | bytes 18886656 | tf_op jit(solution)/shard_map/dot_general | solution.py:151
  308.4 13.4 %fusion.232 = bf16[4096,1024]{1,0:T(8,128)(2,1)} fusion(f32[512,1024]{1,0:T(8,128)S(1)} %copy-done.54, f32[512]{0:T(512)S(1)} %compare_convert_fusion, f32[512,4096]{1,0:T(8,128)} %fusion.234, f32[4096]{0:T(1024)S(1)} %bitcast.695), kind=kOutput, calls=%fused_computation.398 | convolution fusion | flops 4316987392 | bytes 18892800 | tf_op jit(solution)/shard_map/dot_general | solution.py:145
  357.0 24.2 %while.124 = (s32[]{:T(128)}, f32[4,512,64]{1,2,0:T(8,128)S(1)}, f32[4,1024,64]{1,2,0:T(8,128)S(1)}, f32[4,1024,64]{1,2,0:T(8,128)}, bf16[4,512,64]{2,1,0:T(8,12...) while((s32[]{:T(128)}, f32[4,512,64]{1,2,0:T(8,128)S(1)}, ...), condition=%wide.region_24.25_spmd.clone.clone, body=%wide.region_22.24_spmd.clone.clone.sunk | while | flops 343506432 | bytes 18634940 | solution.py:350
  388.6 29.7 %while.125 = (s32[]{:T(128)}, f32[4,512,64]{1,2,0:T(8,128)S(1)}, f32[4,1024,64]{1,2,0:T(8,128)}, f32[4,1024,64]{1,2,0:T(8,128)}, bf16[4,512,64]{2,1,0:T(8,128)(2...) while((s32[]{:T(128)}, f32[4,512,64]{1,2,0:T(8,128)S(1)}, ...), condition=%wide.region_27.28_spmd.clone.clone, body=%wide.region_25.27_spmd.clone.clone.sunk | while | flops 343506432 | bytes 18634940 | solution.py:350
  427.1 29.9 %while.126 = (s32[]{:T(128)}, f32[4,512,64]{1,2,0:T(8,128)S(1)}, f32[4,1024,64]{1,2,0:T(8,128)}, f32[4,1024,64]{1,2,0:T(8,128)}, bf16[4,512,64]{2,1,0:T(8,128)(2...) while((s32[]{:T(128)}, f32[4,512,64]{1,2,0:T(8,128)S(1)}, ...), condition=%wide.region_30.31_spmd.clone.clone, body=%wide.region_28.30_spmd.clone.clone.sunk | while | flops 343506432 | bytes 18634940 | solution.py:350
  465.7 29.6 %while.127 = (s32[]{:T(128)}, f32[4,512,64]{1,2,0:T(8,128)S(1)}, f32[4,1024,64]{1,2,0:T(8,128)}, f32[4,1024,64]{1,2,0:T(8,128)}, bf16[4,512,64]{2,1,0:T(8,128)(2...) while((s32[]{:T(128)}, f32[4,512,64]{1,2,0:T(8,128)S(1)}, ...), condition=%wide.region_33.34_spmd.clone.clone, body=%wide.region_31.33_spmd.clone.clone.sunk | while | flops 343506432 | bytes 18634940 | solution.py:350
  509.3 28.1 %collective-permute-done.7 = bf16[512,512]{0,1:T(8,128)(2,1)S(1)} collective-permute-done((bf16[512,512]{0,1:T(8,128)(2,1)S(1)}, bf16[512,512]{0,1:T(8,128)(2,1)S(1)}, u32[]{:S(2)}, u32[]{:S(2)}) %collective-permute-start.7) | collective-permute-done | bytes 524320 | tf_op jit(solution)/shard_map/ppermute | solution.py:25
  597.8 15.1 %pad_maximum_fusion = bf16[2,8,2,288,1024]{4,3,2,1,0:T(8,128)(2,1)} fusion(bf16[2,8,2,128,1024]{4,3,2,1,0:T(8,128)(2,1)} %bitcast.632, bf16[2,8,2,128,1024]{4,3,2,1,0:T(8,128)(2,1)} %bitcast.633, bf16[2,8,2,32,1024]{4,3,2,1,0:T(8,128)(2,1)S(1)} %bitcast.631), kind=kLoop, calls=%fused_computation.232 | loop fusion | flops 56623104 | bytes 37748736 | tf_op jit(solution)/shard_map/concatenate | solution.py:72
  616.7 26.7 %reduce-scatter.13.cloned.1.call-done = bf16[1,4608,1024]{2,1,0:T(8,128)(2,1)} async-done(((bf16[2,4608,1024]{2,1,0:T(8,128)(2,1)}), bf16[1,4608,1024]{2,1,0:T(8,128)(2,1)}) %reduce-scatter.13.cloned.1.call-update) | async-done | bytes 9437200 | tf_op jit(solution)/shard_map/reduce_scatter | solution.py:74
  643.4 83.6 %reduce-scatter.9.cloned.1.call-done = bf16[1,66,3072]{2,1,0:T(8,128)(2,1)} async-done(((bf16[8,66,3072]{2,1,0:T(8,128)(2,1)}), bf16[1,66,3072]{2,1,0:T(8,128)(2,1)}) %reduce-scatter.9.cloned.1.call-update) | async-done | bytes 405520 | tf_op jit(solution)/shard_map/reduce_scatter | solution.py:76
  728.9 162.5 %reduce-scatter.15.cloned.1.call-done = bf16[1,576,1024]{2,1,0:T(8,128)(2,1)} async-done(((bf16[8,576,1024]{2,1,0:T(8,128)(2,1)}), bf16[1,576,1024]{2,1,0:T(8,128)(2,1)}) %reduce-scatter.15.cloned.1.call-update) | async-done | bytes 1179664 | tf_op jit(solution)/shard_map/reduce_scatter | solution.py:76
  891.5 17.5 %reduce-scatter.11.cloned.1.call-done = bf16[1,33,3072]{2,1,0:T(8,128)(2,1)} async-done(((bf16[2,33,3072]{2,1,0:T(8,128)(2,1)}), bf16[1,33,3072]{2,1,0:T(8,128)(2,1)}) %reduce-scatter.11.cloned.1.call-update) | async-done | bytes 202768 | tf_op jit(solution)/shard_map/reduce_scatter | solution.py:78
  911.1 21.9 %reduce-scatter.17.cloned.1.call-done = bf16[1,288,1024]{2,1,0:T(8,128)(2,1)} async-done(((bf16[2,288,1024]{2,1,0:T(8,128)(2,1)}), bf16[1,288,1024]{2,1,0:T(8,128)(2,1)}) %reduce-scatter.17.cloned.1.call-update) | async-done | bytes 589840 | tf_op jit(solution)/shard_map/reduce_scatter | solution.py:78
  933.0 62.4 %all-gather.24.cloned.1.call-done = bf16[1,264,3072]{2,0,1:T(2,128)(2,1)} async-done(((bf16[1,33,3072]{2,0,1:T(2,128)(2,1)}), bf16[1,264,3072]{2,0,1:T(2,128)(2,1)}) %all-gather.24.cloned.1.call-update) | async-done | bytes 1622032 | tf_op jit(solution)/shard_map/all_gather | solution.py:80
  999.3 75.4 %all-gather.28.cloned.1.call-done = bf16[1,2304,1024]{2,1,0:T(8,128)(2,1)} async-done(((bf16[1,288,1024]{2,1,0:T(8,128)(2,1)}), bf16[1,2304,1024]{2,1,0:T(8,128)(2,1)}) %all-gather.28.cloned.1.call-update) | async-done | bytes 4718608 | tf_op jit(solution)/shard_map/all_gather | solution.py:80
  1076.3 12.5 %add_add_fusion = f32[512,1024]{1,0:T(8,128)} fusion(f32[512,1024]{1,0:T(8,128)S(1)} %copy-done.9, bf16[4096,1024]{1,0:T(8,128)(2,1)} %bitcast.628, f32[1024]{0:T(1024)S(1)} %bitcast.699, f32[512,4096]{1,0:T(8,128)} %fusion.234, f32[4096]{0:T(1024)S(1)} %bitcast.697), kind=kOutput, calls=%fused_computation.290 | convolution fusion | flops 4316987392 | bytes 20992000 | tf_op jit(solution)/shard_map/dot_general | solution.py:305
  1098.3 17.5 %multiply_add_fusion.2 = (f32[512,3072]{1,0:T(8,128)}, f32[512,3072]{1,0:T(8,128)}, f32[512,3072]{1,0:T(8,128)}) fusion(f32[512,3072]{1,0:T(8,128)} %param.39, f32[512,3072]{1,0:T(8,128)} %param.37, bf16[16,32,3072]{2,1,0:T(8,128)(2,1)S(1)} %slice.403, f32[512,3072]{1,0:T(8,128)} %param.38), kind=kLoop, calls=%fused_computation.261 | loop fusion | flops 15728640 | bytes 40894464 | tf_op jit(solution)/shard_map/add | solution.py:185
  1142.1 22.3 %multiply_add_fusion.1 = (f32[1024,2048]{1,0:T(8,128)}, f32[1024,2048]{1,0:T(8,128)}, f32[1024,2048]{1,0:T(8,128)}) fusion(f32[1024,2048]{1,0:T(8,128)} %param.45, f32[1024,2048]{1,0:T(8,128)} %param.43, f32[2048,1024]{0,1:T(8,128)} %copy.314, f32[1024,2048]{1,0:T(8,128)} %param.44), kind=kLoop, calls=%fused_computation.252 | loop fusion | flops 18874368 | bytes 58720256 | tf_op jit(solution)/shard_map/add | solution.py:185
  1164.4 18.6 %multiply_add_fusion = (f32[2048,1024]{1,0:T(8,128)}, f32[2048,1024]{1,0:T(8,128)}, f32[2048,1024]{1,0:T(8,128)}) fusion(f32[2048,1024]{1,0:T(8,128)} %param.48, f32[2048,1024]{1,0:T(8,128)} %param.46, bf16[16,128,1024]{2,1,0:T(8,128)(2,1)} %get-tuple-element.1702, f32[2048,1024]{1,0:T(8,128)} %param.47), kind=kLoop, calls=%fused_computation.251 | loop fusion | flops 20971520 | bytes 54525952 | tf_op jit(solution)/shard_map/add | solution.py:185
  (726 shorter events, 532.7 us)
Async XLA Ops:
  7.2 60.9 %all-gather.32.cloned.1.call-start = ((), (), s32[]{:S(2)}) async-start(), calls=%async_computation.19 | async-start | bytes 2211840 | tf_op jit(solution)/shard_map/all_gather | solution.py:47
  11.5 6.9 collective-permute-start
  19.1 74.6 %all-gather.18.cloned.1.call-start = ((), (), s32[]{:S(2)}) async-start(), calls=%async_computation.12 | async-start | bytes 4866048 | tf_op jit(solution)/shard_map/all_gather | solution.py:48
  71.8 138.1 %all-gather.20.cloned.1.call-start = ((), (), s32[]{:S(2)}) async-start(), calls=%async_computation.13 | async-start | bytes 5308416 | tf_op jit(solution)/shard_map/all_gather | solution.py:47
  90.6 23.9 %collective-permute-start.5 = (bf16[288,1024]{1,0:T(8,128)(2,1)}, bf16[288,1024]{1,0:T(8,128)(2,1)}, u32[]{:S(2)}, u32[]{:S(2)}) collective-permute-start(bf16[288,1024]{1,0:T(8,128)(2,1)} %pad_maximum_fusion.3), channel_id=1, source_target_pairs={{0,1},{1,0},{2,3},{3,2},{4,5},{5,4},{6,7},{7,6},{8,9},{9,8},{10,11... | collective-permute-start | bytes 1769480 | tf_op jit(solution)/shard_map/ppermute | solution.py:46
  110.1 27.2 %collective-permute-start.2 = (bf16[512,512]{1,0:T(8,128)(2,1)}, bf16[512,512]{1,0:T(8,128)(2,1)}, u32[]{:S(2)}, u32[]{:S(2)}) collective-permute-start(bf16[512,512]{1,0:T(8,128)(2,1)} %pad_maximum_fusion.7), channel_id=1, source_target_pairs={{0,1},{2,3},{4,5},{6,7},{8,9},{10,11},{12,13},{14,15},{16,17},{18,... | collective-permute-start | bytes 1572872 | tf_op jit(solution)/shard_map/ppermute | solution.py:25
  114.5 166.3 %all-gather.22.cloned.1.call-start = ((), (), s32[]{:S(2)}) async-start(), calls=%async_computation.14 | async-start | bytes 14155776 | tf_op jit(solution)/shard_map/all_gather | solution.py:48
  128.2 22.5 %collective-permute-start.3 = (bf16[512,512]{1,0:T(8,128)(2,1)}, bf16[512,512]{1,0:T(8,128)(2,1)}, u32[]{:S(2)}, u32[]{:S(2)}) collective-permute-start(bf16[512,512]{1,0:T(8,128)(2,1)} %pad_maximum_fusion.10), channel_id=1, source_target_pairs={{0,1},{2,3},{4,5},{6,7},{8,9},{10,11},{12,13},{14,15},{16,17},{18,... | collective-permute-start | bytes 1572872 | tf_op jit(solution)/shard_map/ppermute | solution.py:25
  132.1 75.7 %collective-permute-start.4 = (bf16[512,512]{1,0:T(8,128)(2,1)}, bf16[512,512]{1,0:T(8,128)(2,1)}, u32[]{:S(2)}, u32[]{:S(2)}) collective-permute-start(bf16[512,512]{1,0:T(8,128)(2,1)} %pad_maximum_fusion.13), channel_id=1, source_target_pairs={{0,1},{2,3},{4,5},{6,7},{8,9},{10,11},{12,13},{14,15},{16,17},{18,... | collective-permute-start | bytes 1572872 | tf_op jit(solution)/shard_map/ppermute | solution.py:25
  135.0 82.0 %collective-permute-start.1 = (bf16[512,512]{1,0:T(8,128)(2,1)}, bf16[512,512]{1,0:T(8,128)(2,1)}, u32[]{:S(2)}, u32[]{:S(2)}) collective-permute-start(bf16[512,512]{1,0:T(8,128)(2,1)} %pad_maximum_fusion.4), channel_id=1, source_target_pairs={{0,1},{2,3},{4,5},{6,7},{8,9},{10,11},{12,13},{14,15},{16,17},{18,... | collective-permute-start | bytes 1572872 | tf_op jit(solution)/shard_map/ppermute | solution.py:25
  210.0 403.0 %reduce-scatter.7.cloned.1.call-start = ((), (), s32[]{:S(2)}) async-start(), calls=%async_computation.6 | async-start | bytes 9732096 | tf_op jit(solution)/shard_map/reduce_scatter | solution.py:74
  502.4 47.8 %collective-permute-start.9 = (bf16[512,512]{0,1:T(8,128)(2,1)S(1)}, bf16[512,512]{0,1:T(8,128)(2,1)S(1)}, u32[]{:S(2)}, u32[]{:S(2)}) collective-permute-start(bf16[512,512]{0,1:T(8,128)(2,1)S(1)} %pad_maximum_fusion.19), channel_id=1, source_target_pairs={{1,0},{3,2},{5,4},{7,6},{9,8},{11,10},{13,12},{15,14},{17,16},{19,... | collective-permute-start | bytes 1572872 | tf_op jit(solution)/shard_map/ppermute | solution.py:25
  504.9 44.1 %collective-permute-start.8 = (bf16[512,512]{0,1:T(8,128)(2,1)S(1)}, bf16[512,512]{0,1:T(8,128)(2,1)S(1)}, u32[]{:S(2)}, u32[]{:S(2)}) collective-permute-start(bf16[512,512]{0,1:T(8,128)(2,1)S(1)} %pad_maximum_fusion.18), channel_id=1, source_target_pairs={{1,0},{3,2},{5,4},{7,6},{9,8},{11,10},{13,12},{15,14},{17,16},{19,... | collective-permute-start | bytes 1572872 | tf_op jit(solution)/shard_map/ppermute | solution.py:25
  506.3 31.1 %collective-permute-start.7 = (bf16[512,512]{0,1:T(8,128)(2,1)S(1)}, bf16[512,512]{0,1:T(8,128)(2,1)S(1)}, u32[]{:S(2)}, u32[]{:S(2)}) collective-permute-start(bf16[512,512]{0,1:T(8,128)(2,1)S(1)} %pad_maximum_fusion.17), channel_id=1, source_target_pairs={{1,0},{3,2},{5,4},{7,6},{9,8},{11,10},{13,12},{15,14},{17,16},{19,... | collective-permute-start | bytes 1572872 | tf_op jit(solution)/shard_map/ppermute | solution.py:25
  507.7 40.9 %collective-permute-start.6 = (bf16[512,512]{0,1:T(8,128)(2,1)S(1)}, bf16[512,512]{0,1:T(8,128)(2,1)S(1)}, u32[]{:S(2)}, u32[]{:S(2)}) collective-permute-start(bf16[512,512]{0,1:T(8,128)(2,1)S(1)} %pad_maximum_fusion.16), channel_id=1, source_target_pairs={{1,0},{3,2},{5,4},{7,6},{9,8},{11,10},{13,12},{15,14},{17,16},{19,... | collective-permute-start | bytes 1572872 | tf_op jit(solution)/shard_map/ppermute | solution.py:25
  595.9 47.4 %reduce-scatter.13.cloned.1.call-start = ((), (), s32[]{:S(2)}) async-start(), calls=%async_computation.9 | async-start | bytes 28311552 | tf_op jit(solution)/shard_map/reduce_scatter | solution.py:74
  612.8 114.1 %reduce-scatter.9.cloned.1.call-start = ((), (), s32[]{:S(2)}) async-start(), calls=%async_computation.7 | async-start | bytes 3981312 | tf_op jit(solution)/shard_map/reduce_scatter | solution.py:76
  616.6 274.9 %reduce-scatter.15.cloned.1.call-start = ((), (), s32[]{:S(2)}) async-start(), calls=%async_computation.10 | async-start | bytes 10616832 | tf_op jit(solution)/shard_map/reduce_scatter | solution.py:76
  643.4 265.7 %reduce-scatter.11.cloned.1.call-start = ((), (), s32[]{:S(2)}) async-start(), calls=%async_computation.8 | async-start | bytes 737280 | tf_op jit(solution)/shard_map/reduce_scatter | solution.py:78
  728.9 204.1 %reduce-scatter.17.cloned.1.call-start = ((), (), s32[]{:S(2)}) async-start(), calls=%async_computation.11 | async-start | bytes 1769472 | tf_op jit(solution)/shard_map/reduce_scatter | solution.py:78
  891.5 104.0 %all-gather.24.cloned.1.call-start = ((), (), s32[]{:S(2)}) async-start(), calls=%async_computation.15 | async-start | bytes 3649536 | tf_op jit(solution)/shard_map/all_gather | solution.py:80
  911.1 163.6 %all-gather.28.cloned.1.call-start = ((), (), s32[]{:S(2)}) async-start(), calls=%async_computation.17 | async-start | bytes 5308416 | tf_op jit(solution)/shard_map/all_gather | solution.py:80
  933.0 157.6 %all-gather.26.cloned.1.call-start = ((), (), s32[]{:S(2)}) async-start(), calls=%async_computation.16 | async-start | bytes 4866048 | tf_op jit(solution)/shard_map/all_gather | solution.py:81
  999.1 116.7 %all-gather.30.cloned.1.call-start = ((), (), s32[]{:S(2)}) async-start(), calls=%async_computation.18 | async-start | bytes 14155776 | tf_op jit(solution)/shard_map/all_gather | solution.py:81
  (118 other events, 952.1 us)
Sparse Core Ops, SparseCore 0:
  19.2 48.8 all-gather.31
  71.9 12.4 all-gather.17
  114.7 76.5 all-gather.19
  210.0 22.0 all-gather.21
  596.0 16.3 reduce-scatter.6
  614.6 28.6 reduce-scatter.12
  647.5 79.4 reduce-scatter.8
  730.6 160.8 reduce-scatter.14
  894.3 14.6 reduce-scatter.10
  911.1 21.8 reduce-scatter.16
  935.7 59.7 all-gather.23
  997.5 77.1 all-gather.27
  1076.8 13.7 all-gather.25
  1092.0 22.7 all-gather.29

commit v7 on v6

--- a/solution.py
+++ b/solution.py
@@ -1,8 +1,11 @@
+import functools
 import math
 
 import jax
 import jax.numpy as jnp
 from jax import lax
+from jax.experimental import pallas as pl
+from jax.experimental.pallas import tpu as pltpu
 from jax.sharding import PartitionSpec as P
 
 
@@ -17,6 +20,120 @@
 SHARD = "shard"
 OUTER = "outer"
 CORE = "core"
+
+
+def _scores(info_ref, slope_ref, q, k, score_scale):
+    upper = info_ref[0]
+    seq_length = info_ref[1]
+    rows, cols = q.shape[0], k.shape[0]
+    own = cols - rows
+    raw = lax.dot_general(q, k, (((1,), (1,)), ((), ())), preferred_element_type=jnp.float32)
+    query_pos = upper * rows + lax.broadcasted_iota(jnp.int32, (rows, cols), 0)
+    key_index = lax.broadcasted_iota(jnp.int32, (rows, cols), 1)
+    key_pos = jnp.where(key_index < own, key_index, upper * rows + key_index - own)
+    allowed = ((key_index >= own) | (upper == 1)) & (key_pos < seq_length) & (key_pos <= query_pos)
+    distance = (query_pos - key_pos).astype(jnp.float32)
+    slope = slope_ref[0][:, 0:1]
+    raw = raw * score_scale - slope * distance
+    return jnp.where(allowed, raw, NEG_FILL)
+
+
+def _fwd_kernel(score_scale, info_ref, slope_ref, q_ref, k_ref, v_ref, mix_ref, lse_ref):
+    scores = _scores(info_ref, slope_ref, q_ref[0], k_ref[0], score_scale)
+    row_top = jnp.max(scores, axis=-1, keepdims=True)
+    weights = jnp.exp(scores - row_top)
+    row_total = jnp.sum(weights, axis=-1, keepdims=True)
+    probs_low = (weights / row_total).astype(jnp.bfloat16)
+    mix = jnp.dot(probs_low, v_ref[0], preferred_element_type=jnp.float32)
+    mix_ref[0] = mix.astype(mix_ref.dtype)
+    lse_ref[0] = row_top + jnp.log(row_total)
+
+
+def _bwd_kernel(score_scale, info_ref, slope_ref, q_ref, k_ref, v_ref, g_ref, lse_ref, dq_ref, dk_ref, dv_ref):
+    q = q_ref[0]
+    k = k_ref[0]
+    grad = g_ref[0]
+    scores = _scores(info_ref, slope_ref, q, k, score_scale)
+    probs = jnp.exp(scores - lse_ref[0])
+    probs_low = probs.astype(jnp.bfloat16)
+    dv_ref[0] = lax.dot_general(probs_low, grad, (((0,), (0,)), ((), ())), preferred_element_type=jnp.float32)
+    grad_probs = lax.dot_general(grad, v_ref[0], (((1,), (1,)), ((), ())), preferred_element_type=jnp.float32)
+    row_delta = jnp.sum(probs * grad_probs, axis=-1, keepdims=True)
+    grad_scores = (probs * (grad_probs - row_delta)).astype(jnp.bfloat16)
+    dq_ref[0] = jnp.dot(grad_scores, k, preferred_element_type=jnp.float32) * score_scale
+    dk_ref[0] = lax.dot_general(grad_scores, q, (((0,), (0,)), ((), ())), preferred_element_type=jnp.float32) * score_scale
+
+
+def _slope_rows(slopes):
+    return jnp.broadcast_to(slopes[:, None, None], (slopes.shape[0], 1, 128)).astype(jnp.float32)
+
+
+def attention_fwd(info, slopes, queries, keys, values, score_scale):
+    heads, rows, width = queries.shape
+    cols = keys.shape[1]
+    head_map = lambda h, info_ref: (h, 0, 0)
+    flops = 4 * heads * rows * cols * width
+    return pl.pallas_call(
+        functools.partial(_fwd_kernel, score_scale),
+        grid_spec=pltpu.PrefetchScalarGridSpec(
+            num_scalar_prefetch=1,
+            grid=(heads,),
+            in_specs=[
+                pl.BlockSpec((1, 1, 128), head_map),
+                pl.BlockSpec((1, rows, width), head_map),
+                pl.BlockSpec((1, cols, width), head_map),
+                pl.BlockSpec((1, cols, width), head_map),
+            ],
+            out_specs=[
+                pl.BlockSpec((1, rows, width), head_map),
+                pl.BlockSpec((1, rows, 1), head_map),
+            ],
+        ),
+        out_shape=[
+            jax.ShapeDtypeStruct((heads, rows, width), jnp.bfloat16),
+            jax.ShapeDtypeStruct((heads, rows, 1), jnp.float32),
+        ],
+        compiler_params=pltpu.CompilerParams(vmem_limit_bytes=48 * 1024 * 1024),
+        cost_estimate=pl.CostEstimate(
+            flops=flops, transcendentals=heads * rows * cols, bytes_accessed=2 * heads * (rows + 2 * cols) * width * 2
+        ),
+    )(info, _slope_rows(slopes), queries, keys, values)
+
+
+def attention_bwd(info, slopes, queries, keys, values, grads, lse, score_scale):
+    heads, rows, width = queries.shape
+    cols = keys.shape[1]
+    head_map = lambda h, info_ref: (h, 0, 0)
+    flops = 8 * heads * rows * cols * width
+    return pl.pallas_call(
+        functools.partial(_bwd_kernel, score_scale),
+        grid_spec=pltpu.PrefetchScalarGridSpec(
+            num_scalar_prefetch=1,
+            grid=(heads,),
+            in_specs=[
+                pl.BlockSpec((1, 1, 128), head_map),
+                pl.BlockSpec((1, rows, width), head_map),
+                pl.BlockSpec((1, cols, width), head_map),
+                pl.BlockSpec((1, cols, width), head_map),
+                pl.BlockSpec((1, rows, width), head_map),
+                pl.BlockSpec((1, rows, 1), head_map),
+            ],
+            out_specs=[
+                pl.BlockSpec((1, rows, width), head_map),
+                pl.BlockSpec((1, cols, width), head_map),
+                pl.BlockSpec((1, cols, width), head_map),
+            ],
+        ),
+        out_shape=[
+            jax.ShapeDtypeStruct((heads, rows, width), jnp.float32),
+            jax.ShapeDtypeStruct((heads, cols, width), jnp.float32),
+            jax.ShapeDtypeStruct((heads, cols, width), jnp.float32),
+        ],
+        compiler_params=pltpu.CompilerParams(vmem_limit_bytes=48 * 1024 * 1024),
+        cost_estimate=pl.CostEstimate(
+            flops=flops, transcendentals=heads * rows * cols, bytes_accessed=heads * (rows + 2 * cols) * width * 6
+        ),
+    )(info, _slope_rows(slopes), queries, keys, values, grads, lse)
 
 
 def passed_along(value, axis, steps):
@@ -172,11 +289,6 @@
 def gelu_back(pre_act, grad_act):
     _, pull_back = jax.vjp(gelu_tanh, pre_act)
     return pull_back(grad_act)[0]
-
-
-def head_scores(queries, key_block, slope, allowed, distance, score_scale):
-    raw = contract_cols(queries, key_block) * score_scale - slope * distance
-    return jnp.where(allowed, raw, NEG_FILL)
 
 
 def nesterov(grad_total, weight_old, moment_old, average_old, rate):
@@ -220,7 +332,6 @@
     key_pos = jnp.concatenate([local_pos, query_pos])
     prev_live = jnp.full((tok_rows,), upper_half == 1)
     key_live = jnp.concatenate([prev_live, jnp.ones((tok_rows,), bool)]) & (key_pos < seq_length)
-    allowed = key_live[None, :] & (key_pos[None, :] <= query_pos[:, None])
     distance = (query_pos[:, None] - key_pos[None, :]).astype(jnp.float32)
     row_live = (query_pos < seq_length).astype(jnp.float32)[:, None]
     head_size = model_width // HEADS
@@ -270,23 +381,18 @@
             split_heads_n(jnp.concatenate([received[:, group_width:], value_own[:, cols]], 0), per_group)
         )
 
-    def head_forward(head_item):
-        head_query, head_keys, head_values, slope = head_item
-        scores = head_scores(head_query, head_keys, slope, allowed, distance, score_scale)
-        row_top = jnp.max(scores, axis=-1, keepdims=True)
-        weights = jnp.exp(scores - row_top)
-        row_total = jnp.sum(weights, axis=-1, keepdims=True)
-        probs_low = (weights / row_total).astype(jnp.bfloat16)
-        mixture = jnp.dot(probs_low, head_values, preferred_element_type=jnp.float32)
-        return (mixture, (row_top + jnp.log(row_total))[:, 0])
-
+    info = jnp.stack([upper_half, seq_length]).astype(jnp.int32)
     fwd_parts = []
     for group in range(groups):
         chosen = slice(group * per_group, (group + 1) * per_group)
         fwd_parts.append(
-            lax.map(
-                head_forward,
-                (query_groups[group], key_groups[group], value_groups[group], slopes[chosen]),
+            attention_fwd(
+                info,
+                slopes[chosen],
+                query_groups[group],
+                key_groups[group],
+                value_groups[group],
+                score_scale,
             )
         )
     mixture_heads = jnp.concatenate([part[0] for part in fwd_parts], 0)
@@ -329,34 +435,18 @@
     grad_mixture = contract_cols(resid_low, out_full).astype(jnp.bfloat16)
     grad_heads = split_heads(grad_mixture)
 
-    def head_backward(head_item):
-        head_query, head_keys, head_values, head_grad, head_lse, slope = head_item
-        scores = head_scores(head_query, head_keys, slope, allowed, distance, score_scale)
-        probs = jnp.exp(scores - head_lse[:, None])
-        probs_low = probs.astype(jnp.bfloat16)
-        grad_values = contract_rows(probs_low, head_grad)
-        grad_probs = contract_cols(head_grad, head_values)
-        row_delta = jnp.sum(probs * grad_probs, axis=-1, keepdims=True)
-        grad_scores = (probs * (grad_probs - row_delta)).astype(jnp.bfloat16)
-        grad_query = (
-            jnp.dot(grad_scores, head_keys, preferred_element_type=jnp.float32) * score_scale
-        )
-        grad_keys = contract_rows(grad_scores, head_query) * score_scale
-        return (grad_query, grad_keys, grad_values)
-
     query_parts, key_parts, value_parts = [], [], []
     for group in range(groups):
         chosen = slice(group * per_group, (group + 1) * per_group)
-        group_query, group_keys, group_values = lax.map(
-            head_backward,
-            (
-                query_groups[group],
-                key_groups[group],
-                value_groups[group],
-                grad_heads[chosen],
-                log_total[chosen],
-                slopes[chosen],
-            ),
+        group_query, group_keys, group_values = attention_bwd(
+            info,
+            slopes[chosen],
+            query_groups[group],
+            key_groups[group],
+            value_groups[group],
+            grad_heads[chosen],
+            log_total[chosen],
+            score_scale,
         )
         returned = passed_along(
             jnp.concatenate(

time: 1200 us -> 1170 us (0.975)
  matrix products: 249 us -> 105 us
  Pallas kernels: 0 us -> 75 us
  waiting for transfers between devices: 546 us -> 598 us
    dot_general x52 -> x4, matrix products: 127 us -> 40.6 us  [contract_cols(): lax.dot_general(left_side, right_side, (((1,), (1,)), ((), ())), preferre...]
    pallas_call x0 -> x8, Pallas kernels: none -> 75 us  [the longest x4 42.7 us: attention_bwd(): pl.pallas_call(functools.partial(_bwd_kernel, score_scale), grid_spec=plt...]
    transpose x0 -> x37, local copies, waits for them, and re-layouts: none -> 60.3 us  [merge_heads(): return field_in.transpose(1, 0, 2).reshape(field_in.shape[1], -1)]
    all_gather x2, waiting for transfers between devices: 49 us -> 92.5 us  [gather_rows(): got = lax.all_gather(other, OUTER, axis=0, tiled=False)]
    dot_general x32 -> x0, matrix products: 32.6 us -> none  [the longest x16 25.3 us: head_forward(): jnp.dot(probs_low, head_values, preferred_element_type=jnp.float32)]
    dot_general x36 -> x4, matrix products: 59.9 us -> 29.9 us  [contract_rows(): lax.dot_general(left_side, right_side, (((0,), (0,)), ((), ())), preferre...]
    dynamic_slice x48 -> x0, local copies, waits for them, and re-layouts: 27.2 us -> none  [the longest x32 18.8 us: body(): lax.map(head_forward, (query_groups[group], key_groups[group], value_grou...]
    slice x16 -> x0, local copies, waits for them, and re-layouts: 23 us -> none  [the longest x4 7.39 us: body(): group_values[:, :tok_rows]]
  transfers between devices with their start and end apart: 24 -> 24, of which waited for: 12 -> 17; matrix products, arithmetic and copies ran while one was open for 21% -> 16% of each run, Pallas kernels for 0% -> 3%
where the time goes in v7:
time: 1170 us; the launch traced here: 1160 us
  waiting for transfers between devices  598 us (51%)
  local copies, waits for them, and re-layouts  193 us (16%)
  other arithmetic  152 us (13%)
  matrix products  105 us (9%)
  Pallas kernels  75 us (6%)
  starting transfers between devices  18.1 us (2%)
  between operations  15.8 us (1%)
    reduce_scatter x2, waiting for transfers between devices, reduce_rows(): stacked = lax.psum_scatter(stacked, OUTER, scatter_dimension=0, tiled=True)  246 us
    all_gather x2, waiting for transfers between devices, reduce_rows(): stacked = lax.all_gather(stacked, OUTER, axis=0, tiled=True)  138 us
    all_gather x2, waiting for transfers between devices, gather_rows(): got = lax.all_gather(other, OUTER, axis=0, tiled=False)  92.5 us
    add x5, other arithmetic, nesterov(): average_new = AVERAGING * average_old + (1.0 - AVERAGING) * weight_new  64.8 us
    transpose x37, local copies, waits for them, and re-layouts, merge_heads(): return field_in.transpose(1, 0, 2).reshape(field_in.shape[1], -1)  60.3 us
    pallas_call x4, Pallas kernels, attention_bwd(): pl.pallas_call(functools.partial(_bwd_kernel, score_scale), grid_spec=plt...  42.7 us
    dot_general x4, matrix products, contract_cols(): lax.dot_general(left_side, right_side, (((1,), (1,)), ((), ())), preferre...  40.6 us
    reduce_scatter x2, waiting for transfers between devices, reduce_rows(): stacked = lax.psum_scatter(stacked, SHARD, scatter_dimension=0, tiled=True)  39.4 us
  transfers between devices with their start and end apart: 24, of which 17 were waited for; matrix products, arithmetic and copies ran while one was open for 16% of the time, Pallas kernels for 3%

profile of v7, /device:TPU:9, one launch (start us, length us, event | category | flops | bytes accessed | tf_op | source)
XLA Modules:
  0.0 1157.1 jit_solution(13566692912082871838)
XLA Ops:
  40.7 12.3 %collective-permute-done.5 = bf16[288,1024]{1,0:T(8,128)(2,1)S(1)} collective-permute-done((bf16[288,1024]{1,0:T(8,128)(2,1)S(1)}, bf16[288,1024]{1,0:T(8,128)(2,1)S(1)}, u32[]{:S(2)}, u32[]{:S(2)}) %collective-permute-start.5) | collective-permute-done | bytes 589856 | tf_op jit(solution)/shard_map/ppermute | solution.py:163
  53.9 16.9 %all-gather.32.cloned.1.call-done = bf16[8,33,3072]{2,1,0:T(8,128)(2,1)} async-done(((bf16[1,33,3072]{2,1,0:T(8,128)(2,1)}), bf16[8,33,3072]{2,1,0:T(8,128)(2,1)}) %all-gather.32.cloned.1.call-update) | async-done | bytes 1622032 | tf_op jit(solution)/shard_map/all_gather | solution.py:164
  74.5 75.6 %all-gather.20.cloned.1.call-done = bf16[2304,1024]{1,0:T(8,128)(2,1)} async-done(((bf16[288,1024]{1,0:T(8,128)(2,1)}), bf16[2304,1024]{1,0:T(8,128)(2,1)}) %all-gather.20.cloned.1.call-update) | async-done | bytes 4718608 | tf_op jit(solution)/shard_map/all_gather | solution.py:164
  151.4 14.6 %all-gather.18.cloned.1.call-done = bf16[16,33,3072]{2,0,1:T(8,128)(2,1)} async-done(((bf16[8,33,3072]{2,0,1:T(8,128)(2,1)}), bf16[16,33,3072]{2,0,1:T(8,128)(2,1)}) %all-gather.18.cloned.1.call-update) | async-done | bytes 3244048 | tf_op jit(solution)/shard_map/all_gather | solution.py:165
  305.4 18.7 %fusion.43 = f32[512,4096]{1,0:T(8,128)} fusion(bf16[4096,1024]{1,0:T(8,128)(2,1)} %bitcast.245, f32[512,1024]{1,0:T(8,128)S(1)} %get-tuple-element.150, f32[1024]{0:T(1024)S(1)} %bitcast.311, f32[1024]{0:T(1024)S(1)} %bitcast.298, f32[512]{0:T(512)S(1)} %add_rsqrt_fusion, f32[512]{0:T(512)S(1)} %broadcast_multiply_fusion.4), kind=kOutput, calls=%fused_computation.183 | convolution fusion | flops 4297588736 | bytes 18886656 | tf_op jit(solution)/shard_map/dot_general | solution.py:268
  324.1 14.2 %fusion.41 = bf16[4096,1024]{1,0:T(8,128)(2,1)} fusion(f32[512,1024]{1,0:T(8,128)} %param.19, f32[512]{0:T(512)S(1)} %fusion.36, f32[512,4096]{1,0:T(8,128)} %fusion.43, f32[4096]{0:T(1024)S(1)} %bitcast.304), kind=kOutput, calls=%fused_computation.181 | convolution fusion | flops 4316987392 | bytes 18892800 | tf_op jit(solution)/shard_map/dot_general | solution.py:262
  338.3 14.3 %fusion.63 = (bf16[4096]{0:T(1024)(128)(2,1)S(1)}, bf16[512,4096]{1,0:T(8,128)(2,1)}) fusion(f32[512,4096]{1,0:T(8,128)} %fusion.43, f32[4096]{0:T(1024)S(1)} %bitcast.305, bf16[4096,1024]{1,0:T(8,128)(2,1)S(1)} %bitcast.243, f32[512,1024]{1,0:T(8,128)} %param.19, f32[512]{0:T(512)S(1)} %fusion.36), kind=kOutput, calls=%fused_computation.199 | convolution fusion | flops 4342149120 | bytes 23095296 | tf_op jit(solution)/shard_map/dot_general | solution.py:268
  384.3 10.6 shard_map.312
  401.7 11.0 shard_map.311
  419.4 10.6 shard_map.310
  436.5 10.6 shard_map.309
  537.9 11.9 %copy.335 = bf16[2,2,8,32,3072]{4,1,3,0,2:T(2,128)(2,1)S(1)} copy(bf16[2,2,8,32,3072]{4,3,2,1,0:T(8,128)(2,1)} %bitcast.251) | data formatting | bytes 12582912 | tf_op jit(solution)/shard_map/convert_element_type | solution.py:189
  565.0 15.2 %pad_maximum_fusion = bf16[2,8,2,288,1024]{4,3,2,1,0:T(8,128)(2,1)} fusion(bf16[2,8,2,128,1024]{4,3,2,1,0:T(8,128)(2,1)} %bitcast.249, bf16[2,8,2,128,1024]{4,3,2,1,0:T(8,128)(2,1)} %bitcast.250, bf16[2,8,2,32,1024]{4,3,2,1,0:T(8,128)(2,1)S(1)} %bitcast.247), kind=kLoop, calls=%fused_computation | loop fusion | flops 56623104 | bytes 37748736 | tf_op jit(solution)/shard_map/concatenate | solution.py:189
  584.1 26.1 %reduce-scatter.13.cloned.1.call-done = bf16[1,4608,1024]{2,1,0:T(8,128)(2,1)} async-done(((bf16[2,4608,1024]{2,1,0:T(8,128)(2,1)}), bf16[1,4608,1024]{2,1,0:T(8,128)(2,1)}) %reduce-scatter.13.cloned.1.call-update) | async-done | bytes 9437200 | tf_op jit(solution)/shard_map/reduce_scatter | solution.py:191
  610.3 83.6 %reduce-scatter.9.cloned.1.call-done = bf16[1,66,3072]{2,1,0:T(8,128)(2,1)} async-done(((bf16[8,66,3072]{2,1,0:T(8,128)(2,1)}), bf16[1,66,3072]{2,1,0:T(8,128)(2,1)}) %reduce-scatter.9.cloned.1.call-update) | async-done | bytes 405520 | tf_op jit(solution)/shard_map/reduce_scatter | solution.py:193
  695.8 162.5 %reduce-scatter.15.cloned.1.call-done = bf16[1,576,1024]{2,1,0:T(8,128)(2,1)} async-done(((bf16[8,576,1024]{2,1,0:T(8,128)(2,1)}), bf16[1,576,1024]{2,1,0:T(8,128)(2,1)}) %reduce-scatter.15.cloned.1.call-update) | async-done | bytes 1179664 | tf_op jit(solution)/shard_map/reduce_scatter | solution.py:193
  858.4 17.5 %reduce-scatter.11.cloned.1.call-done = bf16[1,33,3072]{2,1,0:T(8,128)(2,1)} async-done(((bf16[2,33,3072]{2,1,0:T(8,128)(2,1)}), bf16[1,33,3072]{2,1,0:T(8,128)(2,1)}) %reduce-scatter.11.cloned.1.call-update) | async-done | bytes 202768 | tf_op jit(solution)/shard_map/reduce_scatter | solution.py:195
  878.0 21.9 %reduce-scatter.17.cloned.1.call-done = bf16[1,288,1024]{2,1,0:T(8,128)(2,1)} async-done(((bf16[2,288,1024]{2,1,0:T(8,128)(2,1)}), bf16[1,288,1024]{2,1,0:T(8,128)(2,1)}) %reduce-scatter.17.cloned.1.call-update) | async-done | bytes 589840 | tf_op jit(solution)/shard_map/reduce_scatter | solution.py:195
  900.0 62.4 %all-gather.24.cloned.1.call-done = bf16[1,264,3072]{2,0,1:T(2,128)(2,1)} async-done(((bf16[1,33,3072]{2,0,1:T(2,128)(2,1)}), bf16[1,264,3072]{2,0,1:T(2,128)(2,1)}) %all-gather.24.cloned.1.call-update) | async-done | bytes 1622032 | tf_op jit(solution)/shard_map/all_gather | solution.py:197
  966.0 75.6 %all-gather.28.cloned.1.call-done = bf16[1,2304,1024]{2,1,0:T(8,128)(2,1)} async-done(((bf16[1,288,1024]{2,1,0:T(8,128)(2,1)}), bf16[1,2304,1024]{2,1,0:T(8,128)(2,1)}) %all-gather.28.cloned.1.call-update) | async-done | bytes 4718608 | tf_op jit(solution)/shard_map/all_gather | solution.py:197
  1041.6 12.6 %add_add_fusion = f32[512,1024]{1,0:T(8,128)} fusion(f32[512,1024]{1,0:T(8,128)S(1)} %copy-done.39, bf16[4096,1024]{1,0:T(8,128)(2,1)} %bitcast.244, f32[1024]{0:T(1024)S(1)} %bitcast.308, f32[512,4096]{1,0:T(8,128)} %fusion.43, f32[4096]{0:T(1024)S(1)} %bitcast.306), kind=kOutput, calls=%fused_computation.59 | convolution fusion | flops 4316987392 | bytes 20992000 | tf_op jit(solution)/shard_map/dot_general | solution.py:411
  1065.5 17.4 %multiply_add_fusion.2 = (f32[512,3072]{1,0:T(8,128)}, f32[512,3072]{1,0:T(8,128)}, f32[512,3072]{1,0:T(8,128)}) fusion(f32[512,3072]{1,0:T(8,128)} %param.23, f32[512,3072]{1,0:T(8,128)} %param.21, bf16[16,32,3072]{2,1,0:T(8,128)(2,1)S(1)} %slice.403, f32[512,3072]{1,0:T(8,128)} %param.22), kind=kLoop, calls=%fused_computation.29 | loop fusion | flops 15728640 | bytes 40894464 | tf_op jit(solution)/shard_map/add | solution.py:297
  1109.2 22.3 %multiply_add_fusion.1 = (f32[1024,2048]{1,0:T(8,128)}, f32[1024,2048]{1,0:T(8,128)}, f32[1024,2048]{1,0:T(8,128)}) fusion(f32[1024,2048]{1,0:T(8,128)} %param.29, f32[1024,2048]{1,0:T(8,128)} %param.27, f32[2048,1024]{0,1:T(8,128)} %copy.331, f32[1024,2048]{1,0:T(8,128)} %param.28), kind=kLoop, calls=%fused_computation.20 | loop fusion | flops 18874368 | bytes 58720256 | tf_op jit(solution)/shard_map/add | solution.py:297
  1131.5 18.6 %multiply_add_fusion = (f32[2048,1024]{1,0:T(8,128)}, f32[2048,1024]{1,0:T(8,128)}, f32[2048,1024]{1,0:T(8,128)}) fusion(f32[2048,1024]{1,0:T(8,128)} %param.32, f32[2048,1024]{1,0:T(8,128)} %param.30, bf16[16,128,1024]{2,1,0:T(8,128)(2,1)} %get-tuple-element.94, f32[2048,1024]{1,0:T(8,128)} %param.31), kind=kLoop, calls=%fused_computation.19 | loop fusion | flops 20971520 | bytes 54525952 | tf_op jit(solution)/shard_map/add | solution.py:297
  (444 shorter events, 384.5 us)
Async XLA Ops:
  7.2 63.7 %all-gather.32.cloned.1.call-start = ((), (), s32[]{:S(2)}) async-start(), calls=%async_computation.19 | async-start | bytes 2211840 | tf_op jit(solution)/shard_map/all_gather | solution.py:164
  14.2 6.9 collective-permute-start
  21.8 128.3 %all-gather.20.cloned.1.call-start = ((), (), s32[]{:S(2)}) async-start(), calls=%async_computation.13 | async-start | bytes 5308416 | tf_op jit(solution)/shard_map/all_gather | solution.py:164
  39.5 13.6 %collective-permute-start.5 = (bf16[288,1024]{1,0:T(8,128)(2,1)S(1)}, bf16[288,1024]{1,0:T(8,128)(2,1)S(1)}, u32[]{:S(2)}, u32[]{:S(2)}) collective-permute-start(bf16[288,1024]{1,0:T(8,128)(2,1)S(1)} %pad_maximum_fusion.2), channel_id=1, source_target_pairs={{0,1},{1,0},{2,3},{3,2},{4,5},{5,4},{6,7},{7,6},{8,9},{9,8},{10,11... | collective-permute-start | bytes 1769480 | tf_op jit(solution)/shard_map/ppermute | solution.py:163
  53.9 112.1 %all-gather.18.cloned.1.call-start = ((), (), s32[]{:S(2)}) async-start(), calls=%async_computation.12 | async-start | bytes 4866048 | tf_op jit(solution)/shard_map/all_gather | solution.py:165
  74.5 216.3 %all-gather.22.cloned.1.call-start = ((), (), s32[]{:S(2)}) async-start(), calls=%async_computation.14 | async-start | bytes 14155776 | tf_op jit(solution)/shard_map/all_gather | solution.py:165
  150.1 430.2 %reduce-scatter.7.cloned.1.call-start = ((), (), s32[]{:S(2)}) async-start(), calls=%async_computation.6 | async-start | bytes 9732096 | tf_op jit(solution)/shard_map/reduce_scatter | solution.py:191
  181.6 17.5 %collective-permute-start.2 = (bf16[512,512]{1,0:T(8,128)(2,1)}, bf16[512,512]{1,0:T(8,128)(2,1)}, u32[]{:S(2)}, u32[]{:S(2)}) collective-permute-start(bf16[512,512]{1,0:T(8,128)(2,1)} %pad_maximum_fusion.6), channel_id=1, source_target_pairs={{0,1},{2,3},{4,5},{6,7},{8,9},{10,11},{12,13},{14,15},{16,17},{18,... | collective-permute-start | bytes 1572872 | tf_op jit(solution)/shard_map/ppermute | solution.py:142
  191.7 15.6 %collective-permute-start.3 = (bf16[512,512]{1,0:T(8,128)(2,1)S(1)}, bf16[512,512]{1,0:T(8,128)(2,1)S(1)}, u32[]{:S(2)}, u32[]{:S(2)}) collective-permute-start(bf16[512,512]{1,0:T(8,128)(2,1)S(1)} %pad_maximum_fusion.9), channel_id=1, source_target_pairs={{0,1},{2,3},{4,5},{6,7},{8,9},{10,11},{12,13},{14,15},{16,17},{18,... | collective-permute-start | bytes 1572872 | tf_op jit(solution)/shard_map/ppermute | solution.py:142
  193.9 24.8 %collective-permute-start.4 = (bf16[512,512]{1,0:T(8,128)(2,1)}, bf16[512,512]{1,0:T(8,128)(2,1)}, u32[]{:S(2)}, u32[]{:S(2)}) collective-permute-start(bf16[512,512]{1,0:T(8,128)(2,1)} %pad_maximum_fusion.12), channel_id=1, source_target_pairs={{0,1},{2,3},{4,5},{6,7},{8,9},{10,11},{12,13},{14,15},{16,17},{18,... | collective-permute-start | bytes 1572872 | tf_op jit(solution)/shard_map/ppermute | solution.py:142
  196.8 36.0 %collective-permute-start.1 = (bf16[512,512]{1,0:T(8,128)(2,1)}, bf16[512,512]{1,0:T(8,128)(2,1)}, u32[]{:S(2)}, u32[]{:S(2)}) collective-permute-start(bf16[512,512]{1,0:T(8,128)(2,1)} %pad_maximum_fusion.3), channel_id=1, source_target_pairs={{0,1},{2,3},{4,5},{6,7},{8,9},{10,11},{12,13},{14,15},{16,17},{18,... | collective-permute-start | bytes 1572872 | tf_op jit(solution)/shard_map/ppermute | solution.py:142
  464.5 52.1 %collective-permute-start.9 = (bf16[512,512]{0,1:T(8,128)(2,1)}, bf16[512,512]{0,1:T(8,128)(2,1)}, u32[]{:S(2)}, u32[]{:S(2)}) collective-permute-start(bf16[512,512]{0,1:T(8,128)(2,1)} %pad_maximum_fusion.18), channel_id=1, source_target_pairs={{1,0},{3,2},{5,4},{7,6},{9,8},{11,10},{13,12},{15,14},{17,16},{19,... | collective-permute-start | bytes 1572872 | tf_op jit(solution)/shard_map/ppermute | solution.py:142
  476.7 38.5 %collective-permute-start.8 = (bf16[512,512]{0,1:T(8,128)(2,1)}, bf16[512,512]{0,1:T(8,128)(2,1)}, u32[]{:S(2)}, u32[]{:S(2)}) collective-permute-start(bf16[512,512]{0,1:T(8,128)(2,1)} %pad_maximum_fusion.17), channel_id=1, source_target_pairs={{1,0},{3,2},{5,4},{7,6},{9,8},{11,10},{13,12},{15,14},{17,16},{19,... | collective-permute-start | bytes 1572872 | tf_op jit(solution)/shard_map/ppermute | solution.py:142
  486.6 17.0 %collective-permute-start.7 = (bf16[512,512]{0,1:T(8,128)(2,1)}, bf16[512,512]{0,1:T(8,128)(2,1)}, u32[]{:S(2)}, u32[]{:S(2)}) collective-permute-start(bf16[512,512]{0,1:T(8,128)(2,1)} %pad_maximum_fusion.16), channel_id=1, source_target_pairs={{1,0},{3,2},{5,4},{7,6},{9,8},{11,10},{13,12},{15,14},{17,16},{19,... | collective-permute-start | bytes 1572872 | tf_op jit(solution)/shard_map/ppermute | solution.py:142
  496.3 18.4 %collective-permute-start.6 = (bf16[512,512]{0,1:T(8,128)(2,1)S(1)}, bf16[512,512]{0,1:T(8,128)(2,1)S(1)}, u32[]{:S(2)}, u32[]{:S(2)}) collective-permute-start(bf16[512,512]{0,1:T(8,128)(2,1)S(1)} %pad_maximum_fusion.15), channel_id=1, source_target_pairs={{1,0},{3,2},{5,4},{7,6},{9,8},{11,10},{13,12},{15,14},{17,16},{19,... | collective-permute-start | bytes 1572872 | tf_op jit(solution)/shard_map/ppermute | solution.py:142
  563.2 47.0 %reduce-scatter.13.cloned.1.call-start = ((), (), s32[]{:S(2)}) async-start(), calls=%async_computation.9 | async-start | bytes 28311552 | tf_op jit(solution)/shard_map/reduce_scatter | solution.py:191
  580.3 113.6 %reduce-scatter.9.cloned.1.call-start = ((), (), s32[]{:S(2)}) async-start(), calls=%async_computation.7 | async-start | bytes 3981312 | tf_op jit(solution)/shard_map/reduce_scatter | solution.py:193
  584.0 274.3 %reduce-scatter.15.cloned.1.call-start = ((), (), s32[]{:S(2)}) async-start(), calls=%async_computation.10 | async-start | bytes 10616832 | tf_op jit(solution)/shard_map/reduce_scatter | solution.py:193
  610.2 265.7 %reduce-scatter.11.cloned.1.call-start = ((), (), s32[]{:S(2)}) async-start(), calls=%async_computation.8 | async-start | bytes 737280 | tf_op jit(solution)/shard_map/reduce_scatter | solution.py:195
  695.8 204.1 %reduce-scatter.17.cloned.1.call-start = ((), (), s32[]{:S(2)}) async-start(), calls=%async_computation.11 | async-start | bytes 1769472 | tf_op jit(solution)/shard_map/reduce_scatter | solution.py:195
  858.4 104.0 %all-gather.24.cloned.1.call-start = ((), (), s32[]{:S(2)}) async-start(), calls=%async_computation.15 | async-start | bytes 3649536 | tf_op jit(solution)/shard_map/all_gather | solution.py:197
  878.0 163.6 %all-gather.28.cloned.1.call-start = ((), (), s32[]{:S(2)}) async-start(), calls=%async_computation.17 | async-start | bytes 5308416 | tf_op jit(solution)/shard_map/all_gather | solution.py:197
  899.9 157.6 %all-gather.26.cloned.1.call-start = ((), (), s32[]{:S(2)}) async-start(), calls=%async_computation.16 | async-start | bytes 4866048 | tf_op jit(solution)/shard_map/all_gather | solution.py:198
  966.0 116.9 %all-gather.30.cloned.1.call-start = ((), (), s32[]{:S(2)}) async-start(), calls=%async_computation.18 | async-start | bytes 14155776 | tf_op jit(solution)/shard_map/all_gather | solution.py:198
  (87 other events, 910.7 us)
Sparse Core Ops, SparseCore 0:
  21.9 48.8 all-gather.31
  73.6 76.4 all-gather.19
  152.2 13.7 all-gather.17
  167.4 22.7 all-gather.21
  563.3 15.9 reduce-scatter.6
  581.5 28.6 reduce-scatter.12
  614.4 79.4 reduce-scatter.8
  697.5 160.8 reduce-scatter.14
  861.2 14.6 reduce-scatter.10
  878.0 21.8 reduce-scatter.16
  902.6 59.7 all-gather.23
  964.4 77.1 all-gather.27
  1043.7 13.7 all-gather.25
  1058.9 22.7 all-gather.29

commit v8 on v7

--- a/solution.py
+++ b/solution.py
@@ -236,6 +236,13 @@
     return jnp.swapaxes(split, 0, 1).reshape(values.shape)
 
 
+def col_order(values, blocks):
+    shard_count = lax.axis_size(SHARD)
+    rows, cols = values.shape
+    split = values.reshape(rows, shard_count, blocks, cols // (shard_count * blocks))
+    return jnp.swapaxes(split, 1, 2).reshape(rows, cols)
+
+
 def join_blocks(own, other, blocks):
     upper = lax.axis_index(SHARD) == 1
     own_b = own.reshape((blocks, -1) + own.shape[1:])
@@ -464,7 +471,7 @@
     query_bias_grad = jnp.sum(grad_query, axis=0)
     value_bias_grad = jnp.sum(grad_value_own, axis=0)
     mapped_low = jnp.concatenate([grad_query, grad_key_own, grad_value_own], 1).astype(jnp.bfloat16)
-    qkv_grad = contract_rows(entry_low, mapped_low)
+    qkv_grad = contract_rows(col_order(entry_low, blocks), mapped_low)
     grad_entry = contract_cols(mapped_low, qkv_full)
     gain_one_grad = jnp.sum(grad_entry * normed_one, axis=0)
     shift_one_grad = jnp.sum(grad_entry, axis=0)
@@ -487,7 +494,7 @@
         [small_rows(small_halves[index], blocks) for index in range(shard_count)]
     ).reshape(shard_count, lax.axis_size(CORE), lax.axis_size(OUTER), 1, SMALL_WIDTH)
     small_packed = small_packed.transpose(1, 2, 0, 3, 4)
-    qkv_sum, small_sum = reduce_rows([split_rows(qkv_grad), small_packed])
+    qkv_sum, small_sum = reduce_rows([block_major(qkv_grad), small_packed])
     qkv_total = qkv_sum.reshape(qkv_weight.shape)
     small_total = small_sum.reshape(-1)[: small_params.size].reshape(small_params.shape)
     rate = 2.0 / math.sqrt(model_width * tok_rows * shard_count * group_count)

time: 1170 us -> 1180 us (level)
  local copies, waits for them, and re-layouts: 193 us -> 217 us
    reshape x0 -> x20, local copies, waits for them, and re-layouts: none -> 17.1 us  [merge_heads(): return field_in.transpose(1, 0, 2).reshape(field_in.shape[1], -1)]
    ppermute x8, waiting for transfers between devices: 19.9 us -> 3.92 us  [passed_along(): lax.ppermute(value, axis, [(source, source + steps) for source in range(l...]
    concatenate x0 -> x1, local copies, waits for them, and re-layouts: none -> 13.9 us  [reduce_rows(): jnp.concatenate([piece.astype(jnp.bfloat16) for piece in row_grads], 3)]
    convert_element_type x3 -> x1, local copies, waits for them, and re-layouts: 12.4 us -> 0.26 us  [reduce_rows(): piece.astype(jnp.bfloat16)]
  transfers between devices with their start and end apart: 24 -> 24, of which waited for: 17 -> 16; matrix products, arithmetic and copies ran while one was open for 16% -> 17% of each run, Pallas kernels for 3% -> 3%
where the time goes in v8:
time: 1180 us; the launch traced here: 1170 us
  waiting for transfers between devices  587 us (50%)
  local copies, waits for them, and re-layouts  217 us (18%)
  other arithmetic  150 us (13%)
  matrix products  107 us (9%)
  Pallas kernels  74.5 us (6%)
  starting transfers between devices  18.2 us (2%)
  between operations  15.8 us (1%)
    reduce_scatter x2, waiting for transfers between devices, reduce_rows(): stacked = lax.psum_scatter(stacked, OUTER, scatter_dimension=0, tiled=True)  246 us
    all_gather x2, waiting for transfers between devices, reduce_rows(): stacked = lax.all_gather(stacked, OUTER, axis=0, tiled=True)  138 us
    all_gather x2, waiting for transfers between devices, gather_rows(): got = lax.all_gather(other, OUTER, axis=0, tiled=False)  92.5 us
    add x5, other arithmetic, nesterov(): average_new = AVERAGING * average_old + (1.0 - AVERAGING) * weight_new  64.8 us
    transpose x37, local copies, waits for them, and re-layouts, merge_heads(): return field_in.transpose(1, 0, 2).reshape(field_in.shape[1], -1)  55 us
    pallas_call x4, Pallas kernels, attention_bwd(): pl.pallas_call(functools.partial(_bwd_kernel, score_scale), grid_spec=plt...  42.4 us
    dot_general x4, matrix products, contract_cols(): lax.dot_general(left_side, right_side, (((1,), (1,)), ((), ())), preferre...  42.2 us
    reduce_scatter x2, waiting for transfers between devices, reduce_rows(): stacked = lax.psum_scatter(stacked, SHARD, scatter_dimension=0, tiled=True)  39.4 us
  transfers between devices with their start and end apart: 24, of which 16 were waited for; matrix products, arithmetic and copies ran while one was open for 17% of the time, Pallas kernels for 3%

profile of v8, /device:TPU:9, one launch (start us, length us, event | category | flops | bytes accessed | tf_op | source)
XLA Modules:
  0.0 1169.0 jit_solution(3422046553104518244)
XLA Ops:
  40.7 12.3 %collective-permute-done.5 = bf16[288,1024]{1,0:T(8,128)(2,1)S(1)} collective-permute-done((bf16[288,1024]{1,0:T(8,128)(2,1)S(1)}, bf16[288,1024]{1,0:T(8,128)(2,1)S(1)}, u32[]{:S(2)}, u32[]{:S(2)}) %collective-permute-start.5) | collective-permute-done | bytes 589856 | tf_op jit(solution)/shard_map/ppermute | solution.py:163
  53.9 16.9 %all-gather.32.cloned.1.call-done = bf16[8,33,3072]{2,1,0:T(8,128)(2,1)} async-done(((bf16[1,33,3072]{2,1,0:T(8,128)(2,1)}), bf16[8,33,3072]{2,1,0:T(8,128)(2,1)}) %all-gather.32.cloned.1.call-update) | async-done | bytes 1622032 | tf_op jit(solution)/shard_map/all_gather | solution.py:164
  74.5 75.6 %all-gather.20.cloned.1.call-done = bf16[2304,1024]{1,0:T(8,128)(2,1)} async-done(((bf16[288,1024]{1,0:T(8,128)(2,1)}), bf16[2304,1024]{1,0:T(8,128)(2,1)}) %all-gather.20.cloned.1.call-update) | async-done | bytes 4718608 | tf_op jit(solution)/shard_map/all_gather | solution.py:164
  151.4 14.5 %all-gather.18.cloned.1.call-done = bf16[16,33,3072]{2,0,1:T(8,128)(2,1)} async-done(((bf16[8,33,3072]{2,0,1:T(8,128)(2,1)}), bf16[16,33,3072]{2,0,1:T(8,128)(2,1)}) %all-gather.18.cloned.1.call-update) | async-done | bytes 3244048 | tf_op jit(solution)/shard_map/all_gather | solution.py:165
  307.1 18.7 %fusion.48 = f32[512,4096]{1,0:T(8,128)} fusion(bf16[4096,1024]{1,0:T(8,128)(2,1)} %bitcast.246, f32[512,1024]{1,0:T(8,128)S(1)} %get-tuple-element.150, f32[1024]{0:T(1024)S(1)} %bitcast.319, f32[1024]{0:T(1024)S(1)} %bitcast.307, f32[512]{0:T(512)S(1)} %add_rsqrt_fusion, f32[512]{0:T(512)S(1)} %broadcast_multiply_fusion.4), kind=kOutput, calls=%fused_computation.183 | convolution fusion | flops 4297588736 | bytes 18886656 | tf_op jit(solution)/shard_map/dot_general | solution.py:275
  325.9 14.1 %fusion.46 = bf16[4096,1024]{1,0:T(8,128)(2,1)} fusion(f32[512,1024]{1,0:T(8,128)} %param.19, f32[512]{0:T(512)S(1)} %fusion.41, f32[512,4096]{1,0:T(8,128)} %fusion.48, f32[4096]{0:T(1024)S(1)} %bitcast.314), kind=kOutput, calls=%fused_computation.181 | convolution fusion | flops 4316987392 | bytes 18892800 | tf_op jit(solution)/shard_map/dot_general | solution.py:269
  339.9 14.1 %fusion.68 = (bf16[4096]{0:T(1024)(128)(2,1)S(1)}, bf16[512,4096]{1,0:T(8,128)(2,1)}) fusion(f32[512,4096]{1,0:T(8,128)} %fusion.48, f32[4096]{0:T(1024)S(1)} %bitcast.315, bf16[4096,1024]{1,0:T(8,128)(2,1)S(1)} %bitcast.244, f32[512,1024]{1,0:T(8,128)} %param.19, f32[512]{0:T(512)S(1)} %fusion.41), kind=kOutput, calls=%fused_computation.199 | convolution fusion | flops 4342149120 | bytes 23095296 | tf_op jit(solution)/shard_map/dot_general | solution.py:275
  385.9 10.5 shard_map.312
  405.6 10.9 shard_map.311
  424.5 10.5 shard_map.310
  443.9 10.5 shard_map.309
  548.5 13.9 %copy.440 = bf16[2,8,2,33,3072]{4,0,3,2,1:T(2,128)(2,1)} copy(bf16[2,8,2,33,3072]{4,3,2,1,0:T(8,128)(2,1)S(1)} %pad_maximum_fusion.1) | data formatting | bytes 12976128 | tf_op jit(solution)/shard_map/concatenate | solution.py:189
  571.8 15.2 %pad_maximum_fusion = bf16[2,8,2,288,1024]{4,3,2,1,0:T(8,128)(2,1)} fusion(bf16[2,8,2,128,1024]{4,3,2,1,0:T(8,128)(2,1)} %bitcast.250, bf16[2,8,2,128,1024]{4,3,2,1,0:T(8,128)(2,1)} %bitcast.251, bf16[2,8,2,32,1024]{4,3,2,1,0:T(8,128)(2,1)S(1)} %bitcast.248), kind=kLoop, calls=%fused_computation | loop fusion | flops 56623104 | bytes 37748736 | tf_op jit(solution)/shard_map/concatenate | solution.py:189
  595.0 27.1 %reduce-scatter.13.cloned.1.call-done = bf16[1,4608,1024]{2,1,0:T(8,128)(2,1)} async-done(((bf16[2,4608,1024]{2,1,0:T(8,128)(2,1)}), bf16[1,4608,1024]{2,1,0:T(8,128)(2,1)}) %reduce-scatter.13.cloned.1.call-update) | async-done | bytes 9437200 | tf_op jit(solution)/shard_map/reduce_scatter | solution.py:191
  622.2 83.6 %reduce-scatter.9.cloned.1.call-done = bf16[1,66,3072]{2,1,0:T(8,128)(2,1)} async-done(((bf16[8,66,3072]{2,1,0:T(8,128)(2,1)}), bf16[1,66,3072]{2,1,0:T(8,128)(2,1)}) %reduce-scatter.9.cloned.1.call-update) | async-done | bytes 405520 | tf_op jit(solution)/shard_map/reduce_scatter | solution.py:193
  707.7 162.5 %reduce-scatter.15.cloned.1.call-done = bf16[1,576,1024]{2,1,0:T(8,128)(2,1)} async-done(((bf16[8,576,1024]{2,1,0:T(8,128)(2,1)}), bf16[1,576,1024]{2,1,0:T(8,128)(2,1)}) %reduce-scatter.15.cloned.1.call-update) | async-done | bytes 1179664 | tf_op jit(solution)/shard_map/reduce_scatter | solution.py:193
  870.3 17.5 %reduce-scatter.11.cloned.1.call-done = bf16[1,33,3072]{2,1,0:T(8,128)(2,1)} async-done(((bf16[2,33,3072]{2,1,0:T(8,128)(2,1)}), bf16[1,33,3072]{2,1,0:T(8,128)(2,1)}) %reduce-scatter.11.cloned.1.call-update) | async-done | bytes 202768 | tf_op jit(solution)/shard_map/reduce_scatter | solution.py:195
  889.9 21.9 %reduce-scatter.17.cloned.1.call-done = bf16[1,288,1024]{2,1,0:T(8,128)(2,1)} async-done(((bf16[2,288,1024]{2,1,0:T(8,128)(2,1)}), bf16[1,288,1024]{2,1,0:T(8,128)(2,1)}) %reduce-scatter.17.cloned.1.call-update) | async-done | bytes 589840 | tf_op jit(solution)/shard_map/reduce_scatter | solution.py:195
  911.8 62.4 %all-gather.24.cloned.1.call-done = bf16[1,264,3072]{2,0,1:T(2,128)(2,1)} async-done(((bf16[1,33,3072]{2,0,1:T(2,128)(2,1)}), bf16[1,264,3072]{2,0,1:T(2,128)(2,1)}) %all-gather.24.cloned.1.call-update) | async-done | bytes 1622032 | tf_op jit(solution)/shard_map/all_gather | solution.py:197
  977.9 75.6 %all-gather.28.cloned.1.call-done = bf16[1,2304,1024]{2,1,0:T(8,128)(2,1)} async-done(((bf16[1,288,1024]{2,1,0:T(8,128)(2,1)}), bf16[1,2304,1024]{2,1,0:T(8,128)(2,1)}) %all-gather.28.cloned.1.call-update) | async-done | bytes 4718608 | tf_op jit(solution)/shard_map/all_gather | solution.py:197
  1053.5 12.6 %add_add_fusion = f32[512,1024]{1,0:T(8,128)} fusion(f32[512,1024]{1,0:T(8,128)S(1)} %copy-done.39, bf16[4096,1024]{1,0:T(8,128)(2,1)} %bitcast.245, f32[1024]{0:T(1024)S(1)} %bitcast.318, f32[512,4096]{1,0:T(8,128)} %fusion.48, f32[4096]{0:T(1024)S(1)} %bitcast.316), kind=kOutput, calls=%fused_computation.59 | convolution fusion | flops 4316987392 | bytes 20992000 | tf_op jit(solution)/shard_map/dot_general | solution.py:418
  1077.3 17.4 %multiply_add_fusion.2 = (f32[512,3072]{1,0:T(8,128)}, f32[512,3072]{1,0:T(8,128)}, f32[512,3072]{1,0:T(8,128)}) fusion(f32[512,3072]{1,0:T(8,128)} %param.23, f32[512,3072]{1,0:T(8,128)} %param.21, bf16[16,32,3072]{2,1,0:T(8,128)(2,1)S(1)} %slice.403, f32[512,3072]{1,0:T(8,128)} %param.22), kind=kLoop, calls=%fused_computation.28 | loop fusion | flops 15728640 | bytes 40894464 | tf_op jit(solution)/shard_map/add | solution.py:304
  1121.1 22.3 %multiply_add_fusion.1 = (f32[1024,2048]{1,0:T(8,128)}, f32[1024,2048]{1,0:T(8,128)}, f32[1024,2048]{1,0:T(8,128)}) fusion(f32[1024,2048]{1,0:T(8,128)} %param.29, f32[1024,2048]{1,0:T(8,128)} %param.27, f32[2048,1024]{0,1:T(8,128)} %copy.447, f32[1024,2048]{1,0:T(8,128)} %param.28), kind=kLoop, calls=%fused_computation.20 | loop fusion | flops 18874368 | bytes 58720256 | tf_op jit(solution)/shard_map/add | solution.py:304
  1143.4 18.6 %multiply_add_fusion = (f32[2048,1024]{1,0:T(8,128)}, f32[2048,1024]{1,0:T(8,128)}, f32[2048,1024]{1,0:T(8,128)}) fusion(f32[2048,1024]{1,0:T(8,128)} %param.32, f32[2048,1024]{1,0:T(8,128)} %param.30, bf16[16,128,1024]{2,1,0:T(8,128)(2,1)} %get-tuple-element.102, f32[2048,1024]{1,0:T(8,128)} %param.31), kind=kLoop, calls=%fused_computation.19 | loop fusion | flops 20971520 | bytes 54525952 | tf_op jit(solution)/shard_map/add | solution.py:304
  (480 shorter events, 394.1 us)
Async XLA Ops:
  7.2 63.7 %all-gather.32.cloned.1.call-start = ((), (), s32[]{:S(2)}) async-start(), calls=%async_computation.19 | async-start | bytes 2211840 | tf_op jit(solution)/shard_map/all_gather | solution.py:164
  14.2 6.9 collective-permute-start
  21.8 128.3 %all-gather.20.cloned.1.call-start = ((), (), s32[]{:S(2)}) async-start(), calls=%async_computation.13 | async-start | bytes 5308416 | tf_op jit(solution)/shard_map/all_gather | solution.py:164
  39.5 13.6 %collective-permute-start.5 = (bf16[288,1024]{1,0:T(8,128)(2,1)S(1)}, bf16[288,1024]{1,0:T(8,128)(2,1)S(1)}, u32[]{:S(2)}, u32[]{:S(2)}) collective-permute-start(bf16[288,1024]{1,0:T(8,128)(2,1)S(1)} %pad_maximum_fusion.2), channel_id=1, source_target_pairs={{0,1},{1,0},{2,3},{3,2},{4,5},{5,4},{6,7},{7,6},{8,9},{9,8},{10,11... | collective-permute-start | bytes 1769480 | tf_op jit(solution)/shard_map/ppermute | solution.py:163
  53.9 112.1 %all-gather.18.cloned.1.call-start = ((), (), s32[]{:S(2)}) async-start(), calls=%async_computation.12 | async-start | bytes 4866048 | tf_op jit(solution)/shard_map/all_gather | solution.py:165
  74.5 218.0 %all-gather.22.cloned.1.call-start = ((), (), s32[]{:S(2)}) async-start(), calls=%async_computation.14 | async-start | bytes 14155776 | tf_op jit(solution)/shard_map/all_gather | solution.py:165
  150.1 441.1 %reduce-scatter.7.cloned.1.call-start = ((), (), s32[]{:S(2)}) async-start(), calls=%async_computation.6 | async-start | bytes 9732096 | tf_op jit(solution)/shard_map/reduce_scatter | solution.py:191
  183.2 20.9 %collective-permute-start.2 = (bf16[512,512]{1,0:T(8,128)(2,1)}, bf16[512,512]{1,0:T(8,128)(2,1)}, u32[]{:S(2)}, u32[]{:S(2)}) collective-permute-start(bf16[512,512]{1,0:T(8,128)(2,1)} %pad_maximum_fusion.6), channel_id=1, source_target_pairs={{0,1},{2,3},{4,5},{6,7},{8,9},{10,11},{12,13},{14,15},{16,17},{18,... | collective-permute-start | bytes 1572872 | tf_op jit(solution)/shard_map/ppermute | solution.py:142
  196.8 12.4 %collective-permute-start.3 = (bf16[512,512]{1,0:T(8,128)(2,1)S(1)}, bf16[512,512]{1,0:T(8,128)(2,1)S(1)}, u32[]{:S(2)}, u32[]{:S(2)}) collective-permute-start(bf16[512,512]{1,0:T(8,128)(2,1)S(1)} %pad_maximum_fusion.9), channel_id=1, source_target_pairs={{0,1},{2,3},{4,5},{6,7},{8,9},{10,11},{12,13},{14,15},{16,17},{18,... | collective-permute-start | bytes 1572872 | tf_op jit(solution)/shard_map/ppermute | solution.py:142
  198.9 21.5 %collective-permute-start.4 = (bf16[512,512]{1,0:T(8,128)(2,1)}, bf16[512,512]{1,0:T(8,128)(2,1)}, u32[]{:S(2)}, u32[]{:S(2)}) collective-permute-start(bf16[512,512]{1,0:T(8,128)(2,1)} %pad_maximum_fusion.12), channel_id=1, source_target_pairs={{0,1},{2,3},{4,5},{6,7},{8,9},{10,11},{12,13},{14,15},{16,17},{18,... | collective-permute-start | bytes 1572872 | tf_op jit(solution)/shard_map/ppermute | solution.py:142
  201.9 32.8 %collective-permute-start.1 = (bf16[512,512]{1,0:T(8,128)(2,1)}, bf16[512,512]{1,0:T(8,128)(2,1)}, u32[]{:S(2)}, u32[]{:S(2)}) collective-permute-start(bf16[512,512]{1,0:T(8,128)(2,1)} %pad_maximum_fusion.3), channel_id=1, source_target_pairs={{0,1},{2,3},{4,5},{6,7},{8,9},{10,11},{12,13},{14,15},{16,17},{18,... | collective-permute-start | bytes 1572872 | tf_op jit(solution)/shard_map/ppermute | solution.py:142
  465.5 49.7 %collective-permute-start.8 = (bf16[512,512]{1,0:T(8,128)(2,1)}, bf16[512,512]{1,0:T(8,128)(2,1)}, u32[]{:S(2)}, u32[]{:S(2)}) collective-permute-start(bf16[512,512]{1,0:T(8,128)(2,1)} %pad_maximum_fusion.17), channel_id=1, source_target_pairs={{1,0},{3,2},{5,4},{7,6},{9,8},{11,10},{13,12},{15,14},{17,16},{19,... | collective-permute-start | bytes 1572872 | tf_op jit(solution)/shard_map/ppermute | solution.py:142
  470.9 45.5 %collective-permute-start.7 = (bf16[512,512]{1,0:T(8,128)(2,1)}, bf16[512,512]{1,0:T(8,128)(2,1)}, u32[]{:S(2)}, u32[]{:S(2)}) collective-permute-start(bf16[512,512]{1,0:T(8,128)(2,1)} %pad_maximum_fusion.16), channel_id=1, source_target_pairs={{1,0},{3,2},{5,4},{7,6},{9,8},{11,10},{13,12},{15,14},{17,16},{19,... | collective-permute-start | bytes 1572872 | tf_op jit(solution)/shard_map/ppermute | solution.py:142
  478.7 34.6 %collective-permute-start.6 = (bf16[512,512]{1,0:T(8,128)(2,1)}, bf16[512,512]{1,0:T(8,128)(2,1)}, u32[]{:S(2)}, u32[]{:S(2)}) collective-permute-start(bf16[512,512]{1,0:T(8,128)(2,1)} %pad_maximum_fusion.15), channel_id=1, source_target_pairs={{1,0},{3,2},{5,4},{7,6},{9,8},{11,10},{13,12},{15,14},{17,16},{19,... | collective-permute-start | bytes 1572872 | tf_op jit(solution)/shard_map/ppermute | solution.py:142
  495.1 24.1 %collective-permute-start.9 = (bf16[512,512]{1,0:T(8,128)(2,1)}, bf16[512,512]{1,0:T(8,128)(2,1)}, u32[]{:S(2)}, u32[]{:S(2)}) collective-permute-start(bf16[512,512]{1,0:T(8,128)(2,1)} %pad_maximum_fusion.18), channel_id=1, source_target_pairs={{1,0},{3,2},{5,4},{7,6},{9,8},{11,10},{13,12},{15,14},{17,16},{19,... | collective-permute-start | bytes 1572872 | tf_op jit(solution)/shard_map/ppermute | solution.py:142
  569.9 52.2 %reduce-scatter.13.cloned.1.call-start = ((), (), s32[]{:S(2)}) async-start(), calls=%async_computation.9 | async-start | bytes 28311552 | tf_op jit(solution)/shard_map/reduce_scatter | solution.py:191
  587.0 118.8 %reduce-scatter.9.cloned.1.call-start = ((), (), s32[]{:S(2)}) async-start(), calls=%async_computation.7 | async-start | bytes 3981312 | tf_op jit(solution)/shard_map/reduce_scatter | solution.py:193
  594.9 275.3 %reduce-scatter.15.cloned.1.call-start = ((), (), s32[]{:S(2)}) async-start(), calls=%async_computation.10 | async-start | bytes 10616832 | tf_op jit(solution)/shard_map/reduce_scatter | solution.py:193
  622.2 265.6 %reduce-scatter.11.cloned.1.call-start = ((), (), s32[]{:S(2)}) async-start(), calls=%async_computation.8 | async-start | bytes 737280 | tf_op jit(solution)/shard_map/reduce_scatter | solution.py:195
  707.7 204.1 %reduce-scatter.17.cloned.1.call-start = ((), (), s32[]{:S(2)}) async-start(), calls=%async_computation.11 | async-start | bytes 1769472 | tf_op jit(solution)/shard_map/reduce_scatter | solution.py:195
  870.3 104.0 %all-gather.24.cloned.1.call-start = ((), (), s32[]{:S(2)}) async-start(), calls=%async_computation.15 | async-start | bytes 3649536 | tf_op jit(solution)/shard_map/all_gather | solution.py:197
  889.8 163.6 %all-gather.28.cloned.1.call-start = ((), (), s32[]{:S(2)}) async-start(), calls=%async_computation.17 | async-start | bytes 5308416 | tf_op jit(solution)/shard_map/all_gather | solution.py:197
  911.8 157.6 %all-gather.26.cloned.1.call-start = ((), (), s32[]{:S(2)}) async-start(), calls=%async_computation.16 | async-start | bytes 4866048 | tf_op jit(solution)/shard_map/all_gather | solution.py:198
  977.9 116.9 %all-gather.30.cloned.1.call-start = ((), (), s32[]{:S(2)}) async-start(), calls=%async_computation.18 | async-start | bytes 14155776 | tf_op jit(solution)/shard_map/all_gather | solution.py:198
  (96 other events, 1001.2 us)
Sparse Core Ops, SparseCore 0:
  21.9 48.8 all-gather.31
  73.6 76.4 all-gather.19
  152.2 13.7 all-gather.17
  167.4 22.7 all-gather.21
  570.1 21.1 reduce-scatter.6
  593.4 28.6 reduce-scatter.12
  626.3 79.3 reduce-scatter.8
  709.3 160.8 reduce-scatter.14
  873.1 14.6 reduce-scatter.10
  889.9 21.8 reduce-scatter.16
  914.5 59.6 all-gather.23
  976.3 77.1 all-gather.27
  1055.6 13.7 all-gather.25
  1070.8 22.7 all-gather.29

commit v9 on v7

--- a/solution.py
+++ b/solution.py
@@ -151,7 +151,22 @@
     return jnp.pad(flat, (0, padded - flat.shape[0])).reshape(blocks, 1, SMALL_WIDTH)
 
 
-def gather_rows(row_arrays):
+def gather_ring(piece, axis):
+    count = lax.axis_size(axis)
+    place = lax.axis_index(axis)
+    held = piece[None]
+    step = 1
+    while step < count:
+        received = lax.ppermute(held, axis, [(index, index ^ step) for index in range(count)])
+        first = (place & step) == 0
+        held = jnp.where(
+            first, jnp.concatenate([held, received], 0), jnp.concatenate([received, held], 0)
+        )
+        step *= 2
+    return held
+
+
+def gather_rows(row_arrays, on_dma=False):
     cores = lax.axis_size(CORE)
     outer = lax.axis_size(OUTER)
     blocks = cores * outer
@@ -161,8 +176,11 @@
         [lax.dynamic_index_in_dim(piece, place, 0, keepdims=False) for piece in row_arrays], 0
     )
     other = lax.ppermute(mine, SHARD, [(0, 1), (1, 0)])
-    got = lax.all_gather(other, OUTER, axis=0, tiled=False)
-    got = lax.all_gather(got, CORE, axis=0, tiled=False)
+    if on_dma:
+        got = gather_ring(gather_ring(other, OUTER), CORE)
+    else:
+        got = lax.all_gather(other, OUTER, axis=0, tiled=False)
+        got = lax.all_gather(got, CORE, axis=0, tiled=False)
     got = got.reshape(blocks, -1, got.shape[-1])
     pieces = []
     offset = 0
@@ -341,7 +359,7 @@
     qkv_own = qkv_weight.astype(jnp.bfloat16)
     small_own = small_params.astype(jnp.bfloat16)
     qkv_other, small_other = gather_rows(
-        [qkv_own.reshape(blocks, -1, qkv_own.shape[1]), small_rows(small_own, blocks)]
+        [qkv_own.reshape(blocks, -1, qkv_own.shape[1]), small_rows(small_own, blocks)], on_dma=True
     )
     qkv_full = join_halves(qkv_own, qkv_other.reshape(qkv_own.shape), 0)
     small_full = join_halves(

time: 1170 us -> 1170 us (level)
    ppermute x0 -> x4, waiting for transfers between devices: none -> 48.1 us  [gather_ring(): lax.ppermute(held, axis, [(index, index ^ step) for index in range(count)])]
    all_gather x2 -> x1, waiting for transfers between devices: 92.5 us -> 63.9 us  [gather_rows(): got = lax.all_gather(other, OUTER, axis=0, tiled=False)]
    all_gather x2 -> x1, waiting for transfers between devices: 14.6 us -> 0.01 us  [gather_rows(): got = lax.all_gather(got, CORE, axis=0, tiled=False)]
  transfers between devices with their start and end apart: 24 -> 26, of which waited for: 17 -> 18; matrix products, arithmetic and copies ran while one was open for 16% -> 15% of each run, Pallas kernels for 3% -> 3%
where the time goes in v9:
time: 1170 us; the launch traced here: 1160 us
  waiting for transfers between devices  602 us (51%)
  local copies, waits for them, and re-layouts  192 us (16%)
  other arithmetic  152 us (13%)
  matrix products  98.7 us (8%)
  Pallas kernels  74.5 us (6%)
  starting transfers between devices  23.5 us (2%)
  between operations  16.1 us (1%)
    reduce_scatter x2, waiting for transfers between devices, reduce_rows(): stacked = lax.psum_scatter(stacked, OUTER, scatter_dimension=0, tiled=True)  246 us
    all_gather x2, waiting for transfers between devices, reduce_rows(): stacked = lax.all_gather(stacked, OUTER, axis=0, tiled=True)  138 us
    add x5, other arithmetic, nesterov(): average_new = AVERAGING * average_old + (1.0 - AVERAGING) * weight_new  64.8 us
    all_gather x1, waiting for transfers between devices, gather_rows(): got = lax.all_gather(other, OUTER, axis=0, tiled=False)  63.9 us
    transpose x37, local copies, waits for them, and re-layouts, merge_heads(): return field_in.transpose(1, 0, 2).reshape(field_in.shape[1], -1)  60.3 us
    ppermute x4, waiting for transfers between devices, gather_ring(): lax.ppermute(held, axis, [(index, index ^ step) for index in range(count)])  48.1 us
    pallas_call x4, Pallas kernels, attention_bwd(): pl.pallas_call(functools.partial(_bwd_kernel, score_scale), grid_spec=plt...  42.4 us
    reduce_scatter x2, waiting for transfers between devices, reduce_rows(): stacked = lax.psum_scatter(stacked, SHARD, scatter_dimension=0, tiled=True)  39.5 us
  transfers between devices with their start and end apart: 26, of which 18 were waited for; matrix products, arithmetic and copies ran while one was open for 15% of the time, Pallas kernels for 3%

profile of v9, /device:TPU:9, one launch (start us, length us, event | category | flops | bytes accessed | tf_op | source)
XLA Modules:
  0.0 1159.6 jit_solution(15655216274377808809)
XLA Ops:
  27.2 13.0 %collective-permute-done.9 = bf16[288,1024]{1,0:T(8,128)(2,1)S(1)} collective-permute-done((bf16[288,1024]{1,0:T(8,128)(2,1)S(1)}, bf16[288,1024]{1,0:T(8,128)(2,1)S(1)}, u32[]{:S(2)}, u32[]{:S(2)}) %collective-permute-start.9) | collective-permute-done | bytes 589856 | tf_op jit(solution)/shard_map/ppermute | solution.py:178
  53.4 10.8 collective-permute-done.1
  65.1 63.9 %all-gather.13.cloned.1.call-done = bf16[2304,1024]{1,0:T(8,128)(2,1)} async-done(((bf16[288,1024]{1,0:T(8,128)(2,1)}), bf16[2304,1024]{1,0:T(8,128)(2,1)}) %all-gather.13.cloned.1.call-update) | async-done | bytes 4718608 | tf_op jit(solution)/shard_map/all_gather | solution.py:182
  132.9 35.1 %collective-permute-done.3 = bf16[4,33,3072]{2,0,1:T(4,128)(2,1)S(1)} collective-permute-done((bf16[4,33,3072]{2,0,1:T(4,128)(2,1)S(1)}, bf16[4,33,3072]{2,0,1:T(4,128)(2,1)S(1)}, u32[]{:S(2)}, u32[]{:S(2)}) %collective-permute-start.3) | collective-permute-done | bytes 811040 | tf_op jit(solution)/shard_map/ppermute | solution.py:160
  313.8 13.4 %fusion.43 = f32[512,4096]{1,0:T(8,128)} fusion(bf16[4096,1024]{1,0:T(8,128)(2,1)} %bitcast.253, f32[512,1024]{1,0:T(8,128)S(1)} %get-tuple-element.150, f32[1024]{0:T(1024)S(1)} %bitcast.321, f32[1024]{0:T(1024)S(1)} %bitcast.308, f32[512]{0:T(512)S(1)} %add_rsqrt_fusion, f32[512]{0:T(512)S(1)} %broadcast_multiply_fusion.4), kind=kOutput, calls=%fused_computation.188 | convolution fusion | flops 4297588736 | bytes 18886656 | tf_op jit(solution)/shard_map/dot_general | solution.py:286
  327.1 14.0 %fusion.41 = bf16[4096,1024]{1,0:T(8,128)(2,1)} fusion(f32[512,1024]{1,0:T(8,128)} %param.19, f32[512]{0:T(512)S(1)} %fusion.36, f32[512,4096]{1,0:T(8,128)} %fusion.43, f32[4096]{0:T(1024)S(1)} %bitcast.314), kind=kOutput, calls=%fused_computation.186 | convolution fusion | flops 4316987392 | bytes 18892800 | tf_op jit(solution)/shard_map/dot_general | solution.py:280
  341.1 14.1 %fusion.63 = (bf16[4096]{0:T(1024)(128)(2,1)S(1)}, bf16[512,4096]{1,0:T(8,128)(2,1)}) fusion(f32[512,4096]{1,0:T(8,128)} %fusion.43, f32[4096]{0:T(1024)S(1)} %bitcast.315, bf16[4096,1024]{1,0:T(8,128)(2,1)S(1)} %bitcast.251, f32[512,1024]{1,0:T(8,128)} %param.19, f32[512]{0:T(512)S(1)} %fusion.36), kind=kOutput, calls=%fused_computation.204 | convolution fusion | flops 4342149120 | bytes 23095296 | tf_op jit(solution)/shard_map/dot_general | solution.py:286
  387.1 10.5 shard_map.312
  404.3 10.9 shard_map.311
  421.9 10.5 shard_map.310
  439.0 10.5 shard_map.309
  540.1 11.9 %copy.287 = bf16[2,2,8,32,3072]{4,1,3,0,2:T(2,128)(2,1)S(1)} copy(bf16[2,2,8,32,3072]{4,3,2,1,0:T(8,128)(2,1)} %bitcast.259) | data formatting | bytes 12582912 | tf_op jit(solution)/shard_map/convert_element_type | solution.py:207
  567.3 15.0 %pad_maximum_fusion = bf16[2,8,2,288,1024]{4,3,2,1,0:T(8,128)(2,1)} fusion(bf16[2,8,2,128,1024]{4,3,2,1,0:T(8,128)(2,1)} %bitcast.257, bf16[2,8,2,128,1024]{4,3,2,1,0:T(8,128)(2,1)} %bitcast.258, bf16[2,8,2,32,1024]{4,3,2,1,0:T(8,128)(2,1)S(1)} %bitcast.255), kind=kLoop, calls=%fused_computation | loop fusion | flops 56623104 | bytes 37748736 | tf_op jit(solution)/shard_map/concatenate | solution.py:207
  586.2 26.5 %reduce-scatter.13.cloned.1.call-done = bf16[1,4608,1024]{2,1,0:T(8,128)(2,1)} async-done(((bf16[2,4608,1024]{2,1,0:T(8,128)(2,1)}), bf16[1,4608,1024]{2,1,0:T(8,128)(2,1)}) %reduce-scatter.13.cloned.1.call-update) | async-done | bytes 9437200 | tf_op jit(solution)/shard_map/reduce_scatter | solution.py:209
  612.7 83.4 %reduce-scatter.9.cloned.1.call-done = bf16[1,66,3072]{2,1,0:T(8,128)(2,1)} async-done(((bf16[8,66,3072]{2,1,0:T(8,128)(2,1)}), bf16[1,66,3072]{2,1,0:T(8,128)(2,1)}) %reduce-scatter.9.cloned.1.call-update) | async-done | bytes 405520 | tf_op jit(solution)/shard_map/reduce_scatter | solution.py:211
  698.1 162.4 %reduce-scatter.15.cloned.1.call-done = bf16[1,576,1024]{2,1,0:T(8,128)(2,1)} async-done(((bf16[8,576,1024]{2,1,0:T(8,128)(2,1)}), bf16[1,576,1024]{2,1,0:T(8,128)(2,1)}) %reduce-scatter.15.cloned.1.call-update) | async-done | bytes 1179664 | tf_op jit(solution)/shard_map/reduce_scatter | solution.py:211
  860.5 17.4 %reduce-scatter.11.cloned.1.call-done = bf16[1,33,3072]{2,1,0:T(8,128)(2,1)} async-done(((bf16[2,33,3072]{2,1,0:T(8,128)(2,1)}), bf16[1,33,3072]{2,1,0:T(8,128)(2,1)}) %reduce-scatter.11.cloned.1.call-update) | async-done | bytes 202768 | tf_op jit(solution)/shard_map/reduce_scatter | solution.py:213
  880.1 22.0 %reduce-scatter.17.cloned.1.call-done = bf16[1,288,1024]{2,1,0:T(8,128)(2,1)} async-done(((bf16[2,288,1024]{2,1,0:T(8,128)(2,1)}), bf16[1,288,1024]{2,1,0:T(8,128)(2,1)}) %reduce-scatter.17.cloned.1.call-update) | async-done | bytes 589840 | tf_op jit(solution)/shard_map/reduce_scatter | solution.py:213
  902.2 62.4 %all-gather.17.cloned.1.call-done = bf16[1,264,3072]{2,0,1:T(2,128)(2,1)} async-done(((bf16[1,33,3072]{2,0,1:T(2,128)(2,1)}), bf16[1,264,3072]{2,0,1:T(2,128)(2,1)}) %all-gather.17.cloned.1.call-update) | async-done | bytes 1622032 | tf_op jit(solution)/shard_map/all_gather | solution.py:215
  968.3 75.5 %all-gather.21.cloned.1.call-done = bf16[1,2304,1024]{2,1,0:T(8,128)(2,1)} async-done(((bf16[1,288,1024]{2,1,0:T(8,128)(2,1)}), bf16[1,2304,1024]{2,1,0:T(8,128)(2,1)}) %all-gather.21.cloned.1.call-update) | async-done | bytes 4718608 | tf_op jit(solution)/shard_map/all_gather | solution.py:215
  1043.9 12.6 %add_add_fusion = f32[512,1024]{1,0:T(8,128)} fusion(f32[512,1024]{1,0:T(8,128)S(1)} %copy-done.39, bf16[4096,1024]{1,0:T(8,128)(2,1)} %bitcast.252, f32[1024]{0:T(1024)S(1)} %bitcast.318, f32[512,4096]{1,0:T(8,128)} %fusion.43, f32[4096]{0:T(1024)S(1)} %bitcast.316), kind=kOutput, calls=%fused_computation.60 | convolution fusion | flops 4316987392 | bytes 20992000 | tf_op jit(solution)/shard_map/dot_general | solution.py:429
  1067.7 17.4 %multiply_add_fusion.2 = (f32[512,3072]{1,0:T(8,128)}, f32[512,3072]{1,0:T(8,128)}, f32[512,3072]{1,0:T(8,128)}) fusion(f32[512,3072]{1,0:T(8,128)} %param.23, f32[512,3072]{1,0:T(8,128)} %param.21, bf16[16,32,3072]{2,1,0:T(8,128)(2,1)S(1)} %slice.403, f32[512,3072]{1,0:T(8,128)} %param.22), kind=kLoop, calls=%fused_computation.29 | loop fusion | flops 15728640 | bytes 40894464 | tf_op jit(solution)/shard_map/add | solution.py:315
  1111.4 22.3 %multiply_add_fusion.1 = (f32[1024,2048]{1,0:T(8,128)}, f32[1024,2048]{1,0:T(8,128)}, f32[1024,2048]{1,0:T(8,128)}) fusion(f32[1024,2048]{1,0:T(8,128)} %param.29, f32[1024,2048]{1,0:T(8,128)} %param.27, f32[2048,1024]{0,1:T(8,128)} %copy.282, f32[1024,2048]{1,0:T(8,128)} %param.28), kind=kLoop, calls=%fused_computation.20 | loop fusion | flops 18874368 | bytes 58720256 | tf_op jit(solution)/shard_map/add | solution.py:315
  1133.7 18.6 %multiply_add_fusion = (f32[2048,1024]{1,0:T(8,128)}, f32[2048,1024]{1,0:T(8,128)}, f32[2048,1024]{1,0:T(8,128)}) fusion(f32[2048,1024]{1,0:T(8,128)} %param.32, f32[2048,1024]{1,0:T(8,128)} %param.30, bf16[16,128,1024]{2,1,0:T(8,128)(2,1)} %get-tuple-element.94, f32[2048,1024]{1,0:T(8,128)} %param.31), kind=kLoop, calls=%fused_computation.19 | loop fusion | flops 20971520 | bytes 54525952 | tf_op jit(solution)/shard_map/add | solution.py:315
  (454 shorter events, 389.3 us)
Async XLA Ops:
  7.2 121.8 %all-gather.13.cloned.1.call-start = ((), (), s32[]{:S(2)}) async-start(), calls=%async_computation.12 | async-start | bytes 5308416 | tf_op jit(solution)/shard_map/all_gather | solution.py:182
  25.9 14.3 %collective-permute-start.9 = (bf16[288,1024]{1,0:T(8,128)(2,1)S(1)}, bf16[288,1024]{1,0:T(8,128)(2,1)S(1)}, u32[]{:S(2)}, u32[]{:S(2)}) collective-permute-start(bf16[288,1024]{1,0:T(8,128)(2,1)S(1)} %pad_maximum_fusion.2), channel_id=1, source_target_pairs={{0,1},{1,0},{2,3},{3,2},{4,5},{5,4},{6,7},{7,6},{8,9},{9,8},{10,11... | collective-permute-start | bytes 1769480 | tf_op jit(solution)/shard_map/ppermute | solution.py:178
  41.0 258.1 %all-gather.15.cloned.1.call-start = ((), (), s32[]{:S(2)}) async-start(), calls=%async_computation.13 | async-start | bytes 14155776 | tf_op jit(solution)/shard_map/all_gather | solution.py:183
  52.2 12.1 %collective-permute-start.1 = (bf16[1,33,3072]{2,1,0:T(8,128)(2,1)S(1)}, bf16[1,33,3072]{2,1,0:T(8,128)(2,1)S(1)}, u32[]{:S(2)}, u32[]{:S(2)}) collective-permute-start(bf16[1,33,3072]{2,1,0:T(8,128)(2,1)S(1)} %bitcast.301), channel_id=1, source_target_pairs={{0,4},{4,0},{8,12},{12,8},{16,20},{20,16},{24,28},{28,24},{1,5},{5... | collective-permute-start | bytes 608264 | tf_op jit(solution)/shard_map/ppermute | solution.py:160
  64.4 64.7 %collective-permute-start.2 = (bf16[2,33,3072]{2,1,0:T(8,128)(2,1)S(1)}, bf16[2,33,3072]{2,1,0:T(8,128)(2,1)S(1)}, u32[]{:S(2)}, u32[]{:S(2)}) collective-permute-start(bf16[2,33,3072]{2,1,0:T(8,128)(2,1)S(1)} %maximum_select_fusion.9), channel_id=1, source_target_pairs={{0,8},{4,12},{8,0},{12,4},{16,24},{20,28},{24,16},{28,20},{1,9},{5... | collective-permute-start | bytes 1216520 | tf_op jit(solution)/shard_map/ppermute | solution.py:160
  129.0 453.4 %reduce-scatter.7.cloned.1.call-start = ((), (), s32[]{:S(2)}) async-start(), calls=%async_computation.6 | async-start | bytes 9732096 | tf_op jit(solution)/shard_map/reduce_scatter | solution.py:209
  129.9 38.0 %collective-permute-start.3 = (bf16[4,33,3072]{2,0,1:T(4,128)(2,1)S(1)}, bf16[4,33,3072]{2,0,1:T(4,128)(2,1)S(1)}, u32[]{:S(2)}, u32[]{:S(2)}) collective-permute-start(bf16[4,33,3072]{2,0,1:T(4,128)(2,1)S(1)} %copy.218), channel_id=1, source_target_pairs={{0,16},{4,20},{8,24},{12,28},{16,0},{20,4},{24,8},{28,12},{1,17},{... | collective-permute-start | bytes 2433032 | tf_op jit(solution)/shard_map/ppermute | solution.py:160
  190.3 17.6 %collective-permute-start.6 = (bf16[512,512]{1,0:T(8,128)(2,1)}, bf16[512,512]{1,0:T(8,128)(2,1)}, u32[]{:S(2)}, u32[]{:S(2)}) collective-permute-start(bf16[512,512]{1,0:T(8,128)(2,1)} %pad_maximum_fusion.6), channel_id=1, source_target_pairs={{0,1},{2,3},{4,5},{6,7},{8,9},{10,11},{12,13},{14,15},{16,17},{18,... | collective-permute-start | bytes 1572872 | tf_op jit(solution)/shard_map/ppermute | solution.py:142
  200.4 15.4 %collective-permute-start.7 = (bf16[512,512]{1,0:T(8,128)(2,1)S(1)}, bf16[512,512]{1,0:T(8,128)(2,1)S(1)}, u32[]{:S(2)}, u32[]{:S(2)}) collective-permute-start(bf16[512,512]{1,0:T(8,128)(2,1)S(1)} %pad_maximum_fusion.9), channel_id=1, source_target_pairs={{0,1},{2,3},{4,5},{6,7},{8,9},{10,11},{12,13},{14,15},{16,17},{18,... | collective-permute-start | bytes 1572872 | tf_op jit(solution)/shard_map/ppermute | solution.py:142
  202.9 24.2 %collective-permute-start.8 = (bf16[512,512]{1,0:T(8,128)(2,1)}, bf16[512,512]{1,0:T(8,128)(2,1)}, u32[]{:S(2)}, u32[]{:S(2)}) collective-permute-start(bf16[512,512]{1,0:T(8,128)(2,1)} %pad_maximum_fusion.12), channel_id=1, source_target_pairs={{0,1},{2,3},{4,5},{6,7},{8,9},{10,11},{12,13},{14,15},{16,17},{18,... | collective-permute-start | bytes 1572872 | tf_op jit(solution)/shard_map/ppermute | solution.py:142
  205.9 35.4 %collective-permute-start.5 = (bf16[512,512]{1,0:T(8,128)(2,1)}, bf16[512,512]{1,0:T(8,128)(2,1)}, u32[]{:S(2)}, u32[]{:S(2)}) collective-permute-start(bf16[512,512]{1,0:T(8,128)(2,1)} %pad_maximum_fusion.3), channel_id=1, source_target_pairs={{0,1},{2,3},{4,5},{6,7},{8,9},{10,11},{12,13},{14,15},{16,17},{18,... | collective-permute-start | bytes 1572872 | tf_op jit(solution)/shard_map/ppermute | solution.py:142
  466.9 52.1 %collective-permute-start.13 = (bf16[512,512]{0,1:T(8,128)(2,1)}, bf16[512,512]{0,1:T(8,128)(2,1)}, u32[]{:S(2)}, u32[]{:S(2)}) collective-permute-start(bf16[512,512]{0,1:T(8,128)(2,1)} %pad_maximum_fusion.18), channel_id=1, source_target_pairs={{1,0},{3,2},{5,4},{7,6},{9,8},{11,10},{13,12},{15,14},{17,16},{19,... | collective-permute-start | bytes 1572872 | tf_op jit(solution)/shard_map/ppermute | solution.py:142
  479.0 38.4 %collective-permute-start.12 = (bf16[512,512]{0,1:T(8,128)(2,1)}, bf16[512,512]{0,1:T(8,128)(2,1)}, u32[]{:S(2)}, u32[]{:S(2)}) collective-permute-start(bf16[512,512]{0,1:T(8,128)(2,1)} %pad_maximum_fusion.17), channel_id=1, source_target_pairs={{1,0},{3,2},{5,4},{7,6},{9,8},{11,10},{13,12},{15,14},{17,16},{19,... | collective-permute-start | bytes 1572872 | tf_op jit(solution)/shard_map/ppermute | solution.py:142
  489.0 16.5 %collective-permute-start.11 = (bf16[512,512]{0,1:T(8,128)(2,1)}, bf16[512,512]{0,1:T(8,128)(2,1)}, u32[]{:S(2)}, u32[]{:S(2)}) collective-permute-start(bf16[512,512]{0,1:T(8,128)(2,1)} %pad_maximum_fusion.16), channel_id=1, source_target_pairs={{1,0},{3,2},{5,4},{7,6},{9,8},{11,10},{13,12},{15,14},{17,16},{19,... | collective-permute-start | bytes 1572872 | tf_op jit(solution)/shard_map/ppermute | solution.py:142
  498.6 18.3 %collective-permute-start.10 = (bf16[512,512]{0,1:T(8,128)(2,1)S(1)}, bf16[512,512]{0,1:T(8,128)(2,1)S(1)}, u32[]{:S(2)}, u32[]{:S(2)}) collective-permute-start(bf16[512,512]{0,1:T(8,128)(2,1)S(1)} %pad_maximum_fusion.15), channel_id=1, source_target_pairs={{1,0},{3,2},{5,4},{7,6},{9,8},{11,10},{13,12},{15,14},{17,16},{19,... | collective-permute-start | bytes 1572872 | tf_op jit(solution)/shard_map/ppermute | solution.py:142
  565.5 47.2 %reduce-scatter.13.cloned.1.call-start = ((), (), s32[]{:S(2)}) async-start(), calls=%async_computation.9 | async-start | bytes 28311552 | tf_op jit(solution)/shard_map/reduce_scatter | solution.py:209
  582.3 113.8 %reduce-scatter.9.cloned.1.call-start = ((), (), s32[]{:S(2)}) async-start(), calls=%async_computation.7 | async-start | bytes 3981312 | tf_op jit(solution)/shard_map/reduce_scatter | solution.py:211
  586.1 274.3 %reduce-scatter.15.cloned.1.call-start = ((), (), s32[]{:S(2)}) async-start(), calls=%async_computation.10 | async-start | bytes 10616832 | tf_op jit(solution)/shard_map/reduce_scatter | solution.py:211
  612.7 265.3 %reduce-scatter.11.cloned.1.call-start = ((), (), s32[]{:S(2)}) async-start(), calls=%async_computation.8 | async-start | bytes 737280 | tf_op jit(solution)/shard_map/reduce_scatter | solution.py:213
  698.0 204.1 %reduce-scatter.17.cloned.1.call-start = ((), (), s32[]{:S(2)}) async-start(), calls=%async_computation.11 | async-start | bytes 1769472 | tf_op jit(solution)/shard_map/reduce_scatter | solution.py:213
  860.5 104.1 %all-gather.17.cloned.1.call-start = ((), (), s32[]{:S(2)}) async-start(), calls=%async_computation.14 | async-start | bytes 3649536 | tf_op jit(solution)/shard_map/all_gather | solution.py:215
  880.0 163.8 %all-gather.21.cloned.1.call-start = ((), (), s32[]{:S(2)}) async-start(), calls=%async_computation.16 | async-start | bytes 5308416 | tf_op jit(solution)/shard_map/all_gather | solution.py:215
  902.1 157.6 %all-gather.19.cloned.1.call-start = ((), (), s32[]{:S(2)}) async-start(), calls=%async_computation.15 | async-start | bytes 4866048 | tf_op jit(solution)/shard_map/all_gather | solution.py:216
  968.2 116.9 %all-gather.23.cloned.1.call-start = ((), (), s32[]{:S(2)}) async-start(), calls=%async_computation.17 | async-start | bytes 14155776 | tf_op jit(solution)/shard_map/all_gather | solution.py:216
  (89 other events, 776.6 us)
Sparse Core Ops, SparseCore 0:
  41.1 87.8 all-gather.12
  130.5 23.0 all-gather.14
  565.6 16.1 reduce-scatter.6
  583.9 28.6 reduce-scatter.12
  616.7 79.3 reduce-scatter.8
  699.5 160.8 reduce-scatter.14
  863.3 14.6 reduce-scatter.10
  880.2 21.8 reduce-scatter.16
  904.8 59.7 all-gather.16
  966.6 77.1 all-gather.20
  1045.9 13.7 all-gather.18
  1061.1 22.7 all-gather.22
